TPU v7x, 256 devices: a 4x2x16 block of a 4x16x16 slice. The times are simulated.
256 devices in a mesh: groups: 2 (over y), gx: 16 (over z), gy: 4 (over x), gz: 2 (over core).
Axes of the slice: x: 4, y: 2, z: 16, core: 2. Of those that a mesh axis runs over, the one named last changes fastest.
The devices are a block of a 4x16x16 slice.
Arguments:
- charge: float32 [512, 128, 256], P(('groups', 'gx'), 'gy', 'gz'), parts along dimension 0, may hold values from -6 to 6
Outputs:
- potential: float32 [512, 128, 256], P(('groups', 'gx'), 'gy', 'gz'), parts along dimension 0
There are 2 independent parts, one for each index of `groups`. A program takes and returns all parts, laid end to end along the dimension named above; each array names one. Nothing has to cross between parts.
All inputs are finite; a program needn't handle non-finite values.
Results may differ from a plain program's by a relative error of at most 0.0001.
Values sent between devices are 32-bit elements; how exact they have to be, the bound alone decides.
No kernel may reach another device: no remote copies, remote signals or barrier semaphores. Data moves between devices by JAX's collectives and lax.ppermute only.
A program may use at most 128 MiB of HBM per device.

v0:
```python
import functools

import jax
import jax.numpy as jnp
from jax import lax
from jax.experimental import pallas as pl
from jax.experimental.pallas import tpu as pltpu
from jax.sharding import PartitionSpec as P

LANES = 128
OMEGA = 2.0 / 3.0
SCREEN = 0.001
F32 = jnp.float32

BX, BY = 16, 32
X0, Y0, XA0, YA0 = 12, 24, 40, 80
X1, Y1, XA1, YA1 = 10, 16, 32, 48
HALO = 10


def coefficients(level):
    a = 0.25**level
    return a, OMEGA / (6.0 * a + SCREEN)


def residual_of(level, f, v, nb):
    a, _ = coefficients(level)
    apart = 6.0 * v - nb
    if level:
        apart = a * apart
    return (f - apart) - SCREEN * v


def relaxed(level, f, v, nb):
    return v + coefficients(level)[1] * residual_of(level, f, v, nb)


def twice_from_zero(level, f, nb):
    a, k = coefficients(level)
    return (2.0 * k - k * k * SCREEN) * f - (k * k * a) * (6.0 * f - nb)


def iota(shape, dim):
    return lax.broadcasted_iota(jnp.int32, shape, dim)


def parts(v):
    high = v.astype(jnp.bfloat16)
    rest = v - high.astype(F32)
    middle = rest.astype(jnp.bfloat16)
    return high, middle, (rest - middle.astype(F32)).astype(jnp.bfloat16)


def product(a, b):
    return lax.dot_general(a, b, (((1,), (0,)), ((), ())), preferred_element_type=F32)


def dot(a, b):
    b = b.astype(jnp.bfloat16)
    high, middle, low = (product(p, b) for p in parts(a))
    return high + (middle + low)


def dot_rows(a, b):
    a = a.astype(jnp.bfloat16)
    high, middle, low = (product(a, p) for p in parts(b))
    return high + (middle + low)


def over_layers(start, count, block, body):
    def step(b, carry):
        for u in range(block):
            body(start + b * block + u)
        return carry

    lax.fori_loop(0, -(-count // block), step, 0)


def beside_0(refs, i, j, rows):
    even, odd = (r[i, pl.ds(j, rows), :] for r in refs)
    along_z = odd + pltpu.roll(odd, 1, 1), even + pltpu.roll(even, LANES - 1, 1)
    out = []
    for r, z in zip(refs, along_z):
        out.append(
            (r[i - 1, pl.ds(j, rows), :] + r[i + 1, pl.ds(j, rows), :])
            + (r[i, pl.ds(j - 1, rows), :] + r[i, pl.ds(j + 1, rows), :])
            + z
        )
    return (even, odd), out


def sweep_0(dst, src, force, halo, block):
    def body(i):
        for j in range(Y0 - 8, Y0 + 40, 16):
            centre, nb = beside_0(src, i, j, 16)
            for h in range(2):
                dst[h][i, pl.ds(j, 16), :] = relaxed(0, force[h][i, pl.ds(j, 16), :], centre[h], nb[h])

    over_layers(X0 - halo, BX + 2 * halo, block, body)


def start_0(dst, force, halo, block):
    def body(i):
        for j in range(Y0 - 16, Y0 + 48, 16):
            centre, nb = beside_0(force, i, j, 16)
            for h in range(2):
                dst[h][i, pl.ds(j, 16), :] = twice_from_zero(0, centre[h], nb[h])

    over_layers(X0 - halo, BX + 2 * halo, block, body)


def restrict_0(f1, t0, v, force, halo):
    def body(q):
        for j in range(Y0 - 8, Y0 + 40, 16):
            total = None
            for i in (X0 - 2 * halo + 2 * q, X0 - 2 * halo + 2 * q + 1):
                centre, nb = beside_0(v, i, j, 16)
                for h in range(2):
                    r = residual_of(0, force[h][i, pl.ds(j, 16), :], centre[h], nb[h])
                    total = r if total is None else total + r
            t0[q, pl.ds(j - Y0 + 8, 16), :] = total

    layers = BX // 2 + 2 * halo
    over_layers(0, layers, 4, body)
    for m in range(layers):
        f1[X1 - halo + m, pl.ds(Y1 - 4, 24), :] = 0.125 * (t0[m, pl.ds(0, 24, stride=2), :] + t0[m, pl.ds(1, 24, stride=2), :])


def mean_matrix(source_of_out):
    source, out = iota((LANES, LANES), 0), source_of_out(iota((LANES, LANES), 1))
    return jnp.where((source == out) | (source == out + 1), 0.125, 0.0).astype(F32)


def pick_matrix(source_of_out):
    return jnp.where(iota((LANES, LANES), 0) == source_of_out(iota((LANES, LANES), 1)), 1.0, 0.0).astype(F32)


def beside_1(ref, i, j, rows):
    centre = ref[i, pl.ds(j, rows), :]
    nb = (
        (ref[i - 1, pl.ds(j, rows), :] + ref[i + 1, pl.ds(j, rows), :])
        + (ref[i, pl.ds(j - 1, rows), :] + ref[i, pl.ds(j + 1, rows), :])
        + (pltpu.roll(centre, 1, 1) + pltpu.roll(centre, LANES - 1, 1))
    )
    return centre, nb


def sweep_1(dst, src, force, halo, block):
    def body(i):
        centre, nb = beside_1(src, i, Y1 - 8, 32)
        dst[i, pl.ds(Y1 - 8, 32), :] = relaxed(1, force[i, pl.ds(Y1 - 8, 32), :], centre, nb)

    over_layers(X1 - halo, BX // 2 + 2 * halo, block, body)


def start_1(dst, force, halo, block):
    def body(i):
        centre, nb = beside_1(force, i, Y1 - 8, 32)
        dst[i, pl.ds(Y1 - 8, 32), :] = twice_from_zero(1, centre, nb)

    over_layers(X1 - halo, BX // 2 + 2 * halo, block, body)


def sizes_2():
    return lax.axis_size("gx") * BX // 4, lax.axis_size("gy") * BY // 4, lax.axis_size("gz") * LANES // 4


def coarse_source(out, f1, v1, r1, core):
    start_1(v1, f1, 1, 10)

    def body(i):
        centre, nb = beside_1(v1, i, Y1, 16)
        r1[i, pl.ds(Y1, 16), :] = residual_of(1, f1[i, pl.ds(Y1, 16), :], centre, nb)

    over_layers(X1, BX // 2, 8, body)
    layers = []
    for q in range(4):
        i = X1 + 2 * q
        s = (r1[i, pl.ds(Y1, 8, stride=2), :] + r1[i, pl.ds(Y1 + 1, 8, stride=2), :]) + (
            r1[i + 1, pl.ds(Y1, 8, stride=2), :] + r1[i + 1, pl.ds(Y1 + 1, 8, stride=2), :]
        )
        layers.append(jnp.where(core == 0, s[0:4], s[4:8]))
    n = sizes_2()[2]
    at = lambda o: 2 * lax.rem(o + n // 2 * core, n)
    low = mean_matrix(lambda o: jnp.where(o < n, at(o), -2))
    high = mean_matrix(lambda o: jnp.where(o >= n, at(o), -2))
    packed = dot(jnp.concatenate(layers[0:2], axis=0), low) + dot(jnp.concatenate(layers[2:4], axis=0), high)
    for s in range(out.shape[0]):
        out[s] = packed


def beside_whole(v):
    n = v.shape[0]
    up = jnp.concatenate([v[n - 1 :], v[: n - 1]], axis=0)
    down = jnp.concatenate([v[1:], v[:1]], axis=0)
    y = pltpu.roll(v, 1, 1) + pltpu.roll(v, v.shape[1] - 1, 1)
    return (up + down) + y + (pltpu.roll(v, 1, 2) + pltpu.roll(v, LANES - 1, 2))


def from_zero(level, f):
    return twice_from_zero(level, f, beside_whole(f))


def residual_whole(level, f, v):
    return residual_of(level, f, v, beside_whole(v))


def smooth_whole(level, f, v):
    for _ in range(2):
        v = relaxed(level, f, v, beside_whole(v))
    return v


def down_z(level):
    n = sizes_2()[2] >> (level - 1)
    return mean_matrix(lambda o: 2 * lax.rem(o, n))


def up_z(level):
    n = sizes_2()[2] >> (level - 2)
    return pick_matrix(lambda o: lax.div(lax.rem(o, n), 2))


def pair_layers(v):
    v = v.reshape(v.shape[0] // 2, 2, *v.shape[1:])
    return v[:, 0] + v[:, 1]


def twice(v):
    return jnp.concatenate([v[:, None], v[:, None]], axis=1).reshape(2 * v.shape[0], *v.shape[1:])


def flat(v):
    return v.reshape(-1, LANES)


def row_sums(size, y_size):
    out, source = iota((size, size), 0), iota((size, size), 1)
    first = (out // 8) * 8 + 2 * lax.rem(lax.rem(out, 8), y_size)
    return jnp.where((source == first) | (source == first + 1), 1.0, 0.0).astype(F32)


def row_picks(size, y_size):
    out, source = iota((size, size), 0), iota((size, size), 1)
    first = (out // 8) * 8 + lax.div(lax.rem(lax.rem(out, 8), y_size), 2)
    return jnp.where(source == first, 1.0, 0.0).astype(F32)


def solve_3(f3, t3):
    x4, y4 = f3.shape[0] // 2, f3.shape[1] // 2
    v3 = from_zero(3, f3)
    t3[...] = pair_layers(residual_whole(3, f3, v3))
    s = t3[:, pl.ds(0, y4, stride=2), :] + t3[:, pl.ds(1, y4, stride=2), :]
    f4 = dot(flat(s), down_z(3)).reshape(x4, y4, LANES)
    v4 = from_zero(4, f4)
    s = flat(pair_layers(residual_whole(4, f4, v4)))
    f5 = dot_rows(row_sums(s.shape[0], y4 // 2), dot(s, down_z(4))).reshape(x4 // 2, 8, LANES)
    v5 = from_zero(5, f5)
    s = flat(pair_layers(residual_whole(5, f5, v5)))
    f6 = dot_rows(row_sums(s.shape[0], y4 // 4), dot(s, down_z(5))).reshape(x4 // 4, 8, LANES)
    v6 = flat(from_zero(6, f6))
    e5 = dot_rows(row_picks(v6.shape[0], y4 // 2), dot(v6, up_z(5))).reshape(x4 // 4, 8, LANES)
    v5 = flat(smooth_whole(5, f5, v5 + twice(e5)))
    e4 = dot_rows(row_picks(v5.shape[0], y4), dot(v5, up_z(4))).reshape(x4 // 2, 8, LANES)
    v4 = smooth_whole(4, f4, v4 + twice(e4))
    e3 = dot(flat(v4), up_z(3)).reshape(x4, y4, LANES)
    t3[:, pl.ds(0, y4, stride=2), :] = e3
    t3[:, pl.ds(1, y4, stride=2), :] = e3
    return smooth_whole(3, f3, v3 + twice(t3[...]))


def unpack_2(f2, mine, other, core):
    low = iota((8, LANES), 1) < 64
    top = iota((8, LANES), 0) < 4
    along_y = lax.axis_size("gy")

    def body(gx):
        for gy in range(along_y):
            t, p = mine[gx * along_y + gy], other[gx * along_y + gy]
            u, w = jnp.where(core == 0, t, p), jnp.where(core == 0, p, t)
            ur, wr = pltpu.roll(u, 64, 1), pltpu.roll(w, 64, 1)
            for xp in range(2):
                d = jnp.where(low, u, ur) if xp == 0 else jnp.where(low, ur, u)
                e = jnp.where(low, w, wr) if xp == 0 else jnp.where(low, wr, w)
                f2[gx * 4 + 2 * xp, pl.ds(gy * 8, 8), :] = jnp.where(top, d, pltpu.roll(e, 4, 0))
                f2[gx * 4 + 2 * xp + 1, pl.ds(gy * 8, 8), :] = jnp.where(top, pltpu.roll(d, 4, 0), e)

    over_layers(0, f2.shape[0] // 4, 4, body)


def beside_2(centre, before, after):
    rows = centre.shape[0]
    return (
        (before + after)
        + (pltpu.roll(centre, 1, 0) + pltpu.roll(centre, rows - 1, 0))
        + (pltpu.roll(centre, 1, 1) + pltpu.roll(centre, LANES - 1, 1))
    )


def level_2(near, f2, v2, t2, t3, s3, p2, a2, b2, gx, halo):
    n, rows = f2.shape[0], f2.shape[1]

    def around(ref, i):
        return ref[i], ref[lax.rem(i + n - 1, n)], ref[lax.rem(i + 1, n)]

    def first(i):
        centre, before, after = around(f2, i)
        v2[i] = twice_from_zero(2, centre, beside_2(centre, before, after))

    over_layers(0, n, 16, first)

    def second(q):
        pair = []
        for i in (2 * q, 2 * q + 1):
            centre, before, after = around(v2, i)
            pair.append(residual_of(2, f2[i], centre, beside_2(centre, before, after)))
        t2[q] = pair[0] + pair[1]

    over_layers(0, n // 2, 8, second)
    s = t2[:, pl.ds(0, rows // 2, stride=2), :] + t2[:, pl.ds(1, rows // 2, stride=2), :]
    f3 = dot(flat(s), down_z(2)).reshape(n // 2, rows // 2, LANES)
    s3[...] = solve_3(f3, t3)

    count = 4 + 2 * halo + 4
    start = gx * 4 - halo - 2 + n
    e = jnp.concatenate([s3[lax.rem(lax.div(start, 2) + m, n // 2)] for m in range(count // 2)], axis=0)
    e = dot(e, up_z(2)).reshape(count // 2, rows // 2, LANES)
    p2[pl.ds(0, count // 2), pl.ds(0, rows // 2, stride=2), :] = e
    p2[pl.ds(0, count // 2), pl.ds(1, rows // 2, stride=2), :] = e
    for m in range(count):
        a2[m] = v2[lax.rem(start + m, n)] + p2[m // 2]
    for m in range(1, count - 1):
        nb = beside_2(a2[m], a2[m - 1], a2[m + 1])
        b2[m] = relaxed(2, f2[lax.rem(start + m, n)], a2[m], nb)
    for m in range(2, count - 2):
        nb = beside_2(b2[m], b2[m - 1], b2[m + 1])
        near[m - 2] = relaxed(2, f2[lax.rem(start + m, n)], b2[m], nb)


def add_from_2(v1, near, y2, p1, gy, core, halo):
    layers = 4 + 2 * halo
    rows, n = sizes_2()[1:]
    for m in range(layers):
        y2[m, pl.ds(0, rows), :] = near[m]
        y2[m, pl.ds(rows, rows), :] = near[m]
    start = pl.multiple_of(lax.rem(gy * 8 + rows - 4, rows), 4)
    picked = jnp.concatenate([y2[m, pl.ds(start, 16), :] for m in range(layers)], axis=0)
    e = dot(picked, pick_matrix(lambda o: lax.rem(lax.div(o, 2) + n // 2 * core, n))).reshape(layers, 16, LANES)
    p1[pl.ds(0, layers), pl.ds(0, 16, stride=2), :] = e
    p1[pl.ds(0, layers), pl.ds(1, 16, stride=2), :] = e
    for m in range(2 * layers):
        i = X1 - 2 * halo + m
        v1[i, pl.ds(Y1 - 8, 32), :] = v1[i, pl.ds(Y1 - 8, 32), :] + p1[m // 2]


def add_from_1(w, v, v1, p0, halo, x_at, y_from, skip, rows):
    for m in range(BX // 2 + 2 * halo):
        e = v1[X1 - halo + m, pl.ds(Y1 - 8, 32), :]
        p0[m, pl.ds(0, 32, stride=2), :] = e
        p0[m, pl.ds(1, 32, stride=2), :] = e
    for x in range(-2 * halo, BX + 2 * halo):
        for h in range(2):
            w[h][X0 + x, pl.ds(Y0 - skip, rows), :] = (
                v[h][x_at + x, pl.ds(y_from, rows), :] + p0[x // 2 + halo, pl.ds(16 - skip, rows), :]
            )


def lay_out_1(dst, f1, x_low, x_high, y_low, y_high, own, width):
    count = f1.shape[0]
    for m in range(count):
        i = X1 - own + m
        dst[i, pl.ds(Y1 - 4, 24), :] = f1[m]
        dst[i, pl.ds(Y1 - own - width, width), :] = y_low[pl.ds(m * width, width), :]
        dst[i, pl.ds(Y1 + 16 + own, width), :] = y_high[pl.ds(m * width, width), :]
    for m in range(width):
        dst[X1 - own - width + m, pl.ds(Y1 - 4, 24), :] = x_low[m]
        dst[X1 + 8 + own + m, pl.ds(Y1 - 4, 24), :] = x_high[m]


def put_out_1(out, up_x, down_x, up_y, down_y, f1, own, width):
    for m in range(out.shape[0]):
        i = X1 - own + m
        out[m] = f1[i, pl.ds(Y1 - 4, 24), :]
        up_y[pl.ds(m * width, width), :] = f1[i, pl.ds(Y1 + 16 - own - width, width), :]
        down_y[pl.ds(m * width, width), :] = f1[i, pl.ds(Y1 + own, width), :]
    for m in range(width):
        up_x[m] = f1[X1 + 8 - own - width + m, pl.ds(Y1 - 4, 24), :]
        down_x[m] = f1[X1 + own + m, pl.ds(Y1 - 4, 24), :]


def split_kernel(charge, mine, up, down):
    matrix = pick_matrix(lambda o: jnp.where(o < 64, 2 * o, 2 * o - 127))
    split = dot(flat(charge[...]), matrix).reshape(BX, BY, LANES)
    mine[...] = split
    up[...] = split[BX - HALO :]
    down[...] = split[:HALO]


def edges_kernel(mine, x_low, x_high, up, down):
    at = 0
    for ref in (x_low, mine, x_high):
        for i in range(ref.shape[0]):
            down[pl.ds(at * HALO, HALO), :] = ref[i, pl.ds(0, HALO), :]
            up[pl.ds(at * HALO, HALO), :] = ref[i, pl.ds(BY - HALO, HALO), :]
            at += 1


def lay_out_0(even, odd, ours, others):
    def both(p, q):
        low = iota(p.shape, p.ndim - 1) < 64
        return (
            jnp.where(low, p, pltpu.roll(q, 64, p.ndim - 1)),
            jnp.where(low, pltpu.roll(p, 64, p.ndim - 1), q),
        )

    at = X0 - HALO
    for k in (1, 0, 2):
        for m in range(ours[k].shape[0]):
            e, o = both(ours[k][m], others[k][m])
            even[at, pl.ds(Y0, BY), :] = e
            odd[at, pl.ds(Y0, BY), :] = o
            at += 1
    for k, row in ((3, Y0 - HALO), (4, Y0 + BY)):
        e, o = both(ours[k][...], others[k][...])
        for m in range(BX + 2 * HALO):
            even[X0 - HALO + m, pl.ds(row, HALO), :] = e[m * HALO : (m + 1) * HALO]
            odd[X0 - HALO + m, pl.ds(row, HALO), :] = o[m * HALO : (m + 1) * HALO]


def first_kernel(where, *refs):
    ours, others, refs = refs[0:5], refs[5:10], refs[10:]
    (f_e, f_o, v_e, v_o, send), f1_outs, (f1, v1, r1, t0) = refs[:5], refs[5:10], refs[10:]
    force, v = (f_e, f_o), (v_e, v_o)
    lay_out_0(f_e, f_o, ours, others)
    start_0(v, force, 9, 7)
    restrict_0(f1, t0, v, force, 4)
    coarse_source(send, f1, v1, r1, where()[2])
    put_out_1(*f1_outs, f1, 4, 4)


def middle_kernel(where, *refs):
    f_e, f_o, v_e, v_o, f1_in, x_low, x_high, y_low, y_high, mine, other = refs[:11]
    (n_e, n_o, send), f1_outs = refs[11:14], refs[14:19]
    a_e, a_o, b_e, b_o, f1, v1, r1, p1, y2, p0, t0, f2, v2, t2, t3, s3, p2, a2, b2, near = refs[19:]
    gx, gy, core = where()
    force, v, a0, b0 = (f_e, f_o), (v_e, v_o), (a_e, a_o), (b_e, b_o)
    unpack_2(f2, mine, other, core)
    level_2(near, f2, v2, t2, t3, s3, p2, a2, b2, gx, 4)
    lay_out_1(f1, f1_in, x_low, x_high, y_low, y_high, 4, 4)
    start_1(v1, f1, 7, 12)
    add_from_2(v1, near, y2, p1, gy, core, 4)
    sweep_1(r1, v1, f1, 6, 12)
    sweep_1(v1, r1, f1, 5, 9)
    add_from_1(a0, v, v1, p0, 5, X0, Y0 - 16, 16, 64)
    sweep_0(b0, a0, force, 8, 8)
    sweep_0(a0, b0, force, 7, 8)
    sweep_0(b0, a0, force, 6, 7)
    sweep_0(a0, b0, force, 5, 7)
    restrict_0(f1, t0, a0, force, 2)
    coarse_source(send, f1, v1, r1, core)
    put_out_1(*f1_outs, f1, 2, 2)
    for src, dst in ((a_e, n_e), (a_o, n_o)):
        dst[...] = src[pl.ds(X0 - 2, 20), pl.ds(Y0 - 8, 48), :]


def last_kernel(where, *refs):
    f_e, f_o, n_e, n_o, f1_in, x_low, x_high, y_low, y_high, mine, other, out = refs[:12]
    a_e, a_o, b_e, b_o, f1, v1, r1, p1, y2, p0, _, f2, v2, t2, t3, s3, p2, a2, b2, near = refs[12:]
    gx, gy, core = where()
    force, v, a0, b0 = (f_e, f_o), (n_e, n_o), (a_e, a_o), (b_e, b_o)
    unpack_2(f2, mine, other, core)
    level_2(near, f2, v2, t2, t3, s3, p2, a2, b2, gx, 2)
    lay_out_1(f1, f1_in, x_low, x_high, y_low, y_high, 2, 2)
    start_1(v1, f1, 3, 14)
    add_from_2(v1, near, y2, p1, gy, core, 2)
    sweep_1(r1, v1, f1, 2, 12)
    sweep_1(v1, r1, f1, 1, 10)
    add_from_1(a0, v, v1, p0, 1, 2, 0, 8, 48)
    sweep_0(b0, a0, force, 1, 6)
    low = iota((BY, LANES), 1) < 64

    def body(i):
        centre, nb = beside_0(b0, i, Y0, BY)
        even, odd = (relaxed(0, force[h][i, pl.ds(Y0, BY), :], centre[h], nb[h]) for h in range(2))
        p0[i - X0, pl.ds(0, BY), :] = jnp.where(low, even, pltpu.roll(odd, 64, 1))

    over_layers(X0, BX, 8, body)
    matrix = pick_matrix(lambda o: lax.div(o, 2) + 64 * lax.rem(o, 2))
    out[...] = dot(flat(p0[pl.ds(0, BX), pl.ds(0, BY), :]), matrix).reshape(BX, BY, LANES)


def vm(*shape):
    return pltpu.VMEM(shape, F32)


def kept(*shape):
    return jax.ShapeDtypeStruct(shape, F32)


def scratch_for_cycle():
    x2, y2, _ = sizes_2()
    return (
        [vm(XA0, YA0, LANES)] * 4
        + [vm(XA1, YA1, LANES)] * 3
        + [vm(12, y2, LANES), vm(12, 2 * y2, LANES), vm(20, 64, LANES), vm(16, 48, LANES)]
        + [vm(x2, y2, LANES)] * 2
        + [vm(x2 // 2, y2, LANES), vm(x2 // 4, y2 // 2, LANES), vm(x2 // 2, y2 // 2, LANES), vm(8, y2, LANES)]
        + [vm(16, y2, LANES)] * 2
        + [vm(12, y2, LANES)]
    )


def run(kernel, outs, scratch, flops, *args):
    return pl.pallas_call(
        kernel,
        out_shape=outs,
        scratch_shapes=scratch,
        compiler_params=pltpu.CompilerParams(vmem_limit_bytes=40 * 2**20),
        cost_estimate=pl.CostEstimate(flops=flops, bytes_accessed=2**20, transcendentals=0),
    )(*args)


def where_am_i():
    return lax.axis_index("gx"), lax.axis_index("gy"), lax.axis_index("gz")


def sources_out(layers, width):
    y = kept(layers * width, LANES)
    return [kept(peers(), 8, LANES), kept(layers, 24, LANES)] + [kept(width, 24, LANES)] * 2 + [y] * 2


def peers():
    return lax.axis_size("gx") * lax.axis_size("gy")


def split(charge):
    return run(split_kernel, [kept(BX, BY, LANES)] + [kept(HALO, BY, LANES)] * 2, [], 10**6, charge)


def edges(*args):
    return run(edges_kernel, [kept((BX + 2 * HALO) * HALO, LANES)] * 2, [], 10**6, *args)


def first(*args):
    outs = [kept(XA0, YA0, LANES)] * 4 + sources_out(16, 4)
    scratch = [vm(XA1, YA1, LANES)] * 3 + [vm(16, 48, LANES)]
    return run(functools.partial(first_kernel, where_am_i), outs, scratch, 10**7, *args)


def middle(*args):
    outs = [kept(20, 48, LANES)] * 2 + sources_out(12, 2)
    return run(functools.partial(middle_kernel, where_am_i), outs, scratch_for_cycle(), 4 * 10**7, *args)


def last(*args):
    outs = kept(BX, BY, LANES)
    return run(functools.partial(last_kernel, where_am_i), outs, scratch_for_cycle(), 2 * 10**7, *args)


def from_(value, axis, step):
    size = lax.axis_size(axis)
    return lax.ppermute(value, axis, [(i, (i + step) % size) for i in range(size)])


def exchange(send, f1, up_x, down_x, up_y, down_y):
    x_low, x_high = from_(up_x, "gx", 1), from_(down_x, "gx", -1)
    y_low, y_high = from_(up_y, "gy", 1), from_(down_y, "gy", -1)
    mine = lax.all_to_all(send, ("gx", "gy"), 0, 0, tiled=True)
    return f1, x_low, x_high, y_low, y_high, mine, from_(mine, "gz", 1)


def local(charge):
    mine, up, down = split(charge)
    x_low, x_high = from_(up, "gx", 1), from_(down, "gx", -1)
    up, down = edges(mine, x_low, x_high)
    y_low, y_high = from_(up, "gy", 1), from_(down, "gy", -1)
    ours = (mine, x_low, x_high, y_low, y_high)
    others = [from_(v, "gz", 1) for v in ours]
    f_e, f_o, v_e, v_o, *rest = first(*ours, *others)
    n_e, n_o, *rest = middle(f_e, f_o, v_e, v_o, *exchange(*rest))
    return last(f_e, f_o, n_e, n_o, *exchange(*rest))


def solution(mesh):
    return jax.shard_map(
        local,
        mesh=mesh,
        in_specs=(P(("groups", "gx"), "gy", "gz"),),
        out_specs=P(("groups", "gx"), "gy", "gz"),
        check_vma=False,
    )
```

profile of v0, /device:TPU:33, one launch (start us, length us, event | category | flops | bytes accessed | tf_op | source)
XLA Modules:
  0.0 136.1 jit_solution(13621892481352483959)
XLA Ops:
  0.0 0.0 copy-start
  0.0 0.9 copy-done
  1.0 0.3 shard_map.17
  1.2 3.4 %collective-permute-start = (f32[10,32,128]{2,1,0:T(8,128)S(1)}, f32[10,32,128]{2,1,0:T(8,128)S(1)}, u32[]{:S(2)}, u32[]{:S(2)}) collective-permute-start(f32[10,32,128]{2,1,0:T(8,128)S(1)} %get-tuple-element.29), channel_id=1, source_target_pairs={{0,8},{8,16},{16,24},{24,32},{32,40},{40,48},{48,56},{56,64},{64,7... | collective-permute-start | bytes 491528 | tf_op jit(solution)/shard_map/ppermute | solution.py:562
  4.6 19.7 %collective-permute-start.1 = (f32[10,32,128]{2,1,0:T(8,128)S(1)}, f32[10,32,128]{2,1,0:T(8,128)S(1)}, u32[]{:S(2)}, u32[]{:S(2)}) collective-permute-start(f32[10,32,128]{2,1,0:T(8,128)S(1)} %get-tuple-element.30), channel_id=1, source_target_pairs={{0,120},{8,0},{16,8},{24,16},{32,24},{40,32},{48,40},{56,48},{64,5... | collective-permute-start | bytes 491528 | tf_op jit(solution)/shard_map/ppermute | solution.py:562
  24.4 3.8 %collective-permute-done.x_low.refs_1_ = f32[10,32,128]{2,1,0:T(8,128)S(1)} collective-permute-done((f32[10,32,128]{2,1,0:T(8,128)S(1)}, f32[10,32,128]{2,1,0:T(8,128)S(1)}, u32[]{:S(2)}, u32[]{:S(2)}) %collective-permute-start) | collective-permute-done | bytes 163872 | tf_op jit(solution)/shard_map/ppermute | solution.py:562
  28.2 0.0 collective-permute-done.1.x_high.refs_2_
  28.3 1.5 %collective-permute-start.2 = (f32[360,128]{1,0:T(8,128)S(1)}, f32[360,128]{1,0:T(8,128)S(1)}, u32[]{:S(2)}, u32[]{:S(2)}) collective-permute-start(f32[360,128]{1,0:T(8,128)S(1)} %get-tuple-element.31), channel_id=1, source_target_pairs={{0,2},{2,4},{4,6},{6,0},{1,3},{3,5},{5,7},{7,1},{8,10},{10,12},{12... | collective-permute-start | bytes 552968 | tf_op jit(solution)/shard_map/ppermute | solution.py:562
  29.7 1.7 %collective-permute-start.3 = (f32[360,128]{1,0:T(8,128)S(1)}, f32[360,128]{1,0:T(8,128)S(1)}, u32[]{:S(2)}, u32[]{:S(2)}) collective-permute-start(f32[360,128]{1,0:T(8,128)S(1)} %get-tuple-element.32), channel_id=1, source_target_pairs={{0,6},{2,0},{4,2},{6,4},{1,7},{3,1},{5,3},{7,5},{8,14},{10,8},{12,... | collective-permute-start | bytes 552968 | tf_op jit(solution)/shard_map/ppermute | solution.py:562
  31.4 1.5 %collective-permute-start.4 = (f32[16,32,128]{2,1,0:T(8,128)S(1)}, f32[16,32,128]{2,1,0:T(8,128)S(1)}, u32[]{:S(2)}, u32[]{:S(2)}) collective-permute-start(f32[16,32,128]{2,1,0:T(8,128)S(1)} %get-tuple-element.28.mine.refs_0_), channel_id=1, source_target_pairs={{0,1},{1,0},{2,3},{3,2},{4,5},{5,4},{6,7},{7,6},{8,9},{9,8},{10,11... | collective-permute-start | bytes 786440 | tf_op jit(solution)/shard_map/ppermute | solution.py:562
  32.9 2.2 %collective-permute-done.2.refs_3_ = f32[360,128]{1,0:T(8,128)S(1)} collective-permute-done((f32[360,128]{1,0:T(8,128)S(1)}, f32[360,128]{1,0:T(8,128)S(1)}, u32[]{:S(2)}, u32[]{:S(2)}) %collective-permute-start.2) | collective-permute-done | bytes 184352 | tf_op jit(solution)/shard_map/ppermute | solution.py:562
  35.1 1.8 %collective-permute-start.7 = (f32[360,128]{1,0:T(8,128)S(1)}, f32[360,128]{1,0:T(8,128)S(1)}, u32[]{:S(2)}, u32[]{:S(2)}) collective-permute-start(f32[360,128]{1,0:T(8,128)S(1)} %collective-permute-done.2.refs_3_), channel_id=1, source_target_pairs={{0,1},{1,0},{2,3},{3,2},{4,5},{5,4},{6,7},{7,6},{8,9},{9,8},{10,11... | collective-permute-start | bytes 552968 | tf_op jit(solution)/shard_map/ppermute | solution.py:562
  36.9 0.0 collective-permute-done.3.refs_4_
  36.9 0.0 collective-permute-start.8
  36.9 0.5 collective-permute-start.5
  37.4 0.0 collective-permute-start.6
  37.4 0.0 collective-permute-done.4.refs_5_
  37.4 1.1 collective-permute-done.5.refs_6_
  38.5 0.2 collective-permute-done.6.refs_7_
  38.8 0.0 collective-permute-done.7.refs_8_
  38.8 0.0 collective-permute-done.8.refs_9_
  38.8 2.9 %shard_map.19 = (f32[40,80,128]{2,1,0:T(8,128)S(1)}, f32[40,80,128]{2,1,0:T(8,128)S(1)}, f32[40,80,128]{2,1,0:T(8,128)S(1)}, f32[40,80,128]{2,1,0:T(8,128)S(1)},...) custom-call(f32[16,32,128]{2,1,0:T(8,128)S(1)} %get-tuple-element.28, ...), custom_call_target="tpu_custom_call" | custom-call | flops 10000000 | bytes 1048576 | tf_op jit(solution)/shard_map/pallas_call | solution.py:514
  41.7 27.9 %all_to_all.10.refs_9_ = f32[64,8,128]{2,1,0:T(8,128)S(1)} all-to-all(f32[64,8,128]{2,1,0:T(8,128)S(1)} %get-tuple-element.42), channel_id=1, replica_groups=mesh['groups'=2,'gx'=16,'gy'=4,'gz'=2] {'gx','gy'}, dimensions={0} | all-to-all | bytes 524288 | tf_op jit(solution)/shard_map/all_to_all | solution.py:568
  69.7 3.7 %collective-permute-start.13 = (f32[64,8,128]{2,1,0:T(8,128)S(1)}, f32[64,8,128]{2,1,0:T(8,128)S(1)}, u32[]{:S(2)}, u32[]{:S(2)}) collective-permute-start(f32[64,8,128]{2,1,0:T(8,128)S(1)} %all_to_all.10.refs_9_), channel_id=1, source_target_pairs={{0,1},{1,0},{2,3},{3,2},{4,5},{5,4},{6,7},{7,6},{8,9},{9,8},{10,11... | collective-permute-start | bytes 786440 | tf_op jit(solution)/shard_map/ppermute | solution.py:562
  73.4 0.7 collective-permute-start.9
  74.1 1.9 %collective-permute-start.10 = (f32[4,24,128]{2,1,0:T(8,128)S(1)}, f32[4,24,128]{2,1,0:T(8,128)S(1)}, u32[]{:S(2)}, u32[]{:S(2)}) collective-permute-start(f32[4,24,128]{2,1,0:T(8,128)S(1)} %get-tuple-element.39), channel_id=1, source_target_pairs={{0,120},{8,0},{16,8},{24,16},{32,24},{40,32},{48,40},{56,48},{64,5... | collective-permute-start | bytes 147464 | tf_op jit(solution)/shard_map/ppermute | solution.py:562
  76.1 0.2 collective-permute-start.11
  76.3 2.4 %collective-permute-start.12 = (f32[64,128]{1,0:T(8,128)S(1)}, f32[64,128]{1,0:T(8,128)S(1)}, u32[]{:S(2)}, u32[]{:S(2)}) collective-permute-start(f32[64,128]{1,0:T(8,128)S(1)} %get-tuple-element.41), channel_id=1, source_target_pairs={{0,6},{2,0},{4,2},{6,4},{1,7},{3,1},{5,3},{7,5},{8,14},{10,8},{12,... | collective-permute-start | bytes 98312 | tf_op jit(solution)/shard_map/ppermute | solution.py:562
  78.8 1.3 collective-permute-done.11.refs_7_
  80.1 0.0 collective-permute-done.12.refs_8_
  80.1 0.0 collective-permute-done.9.refs_5_
  80.1 0.0 collective-permute-done.10.refs_6_
  80.1 0.0 collective-permute-done.13.refs_10_
  80.1 11.6 %shard_map.20 = (f32[20,48,128]{2,1,0:T(8,128)S(1)}, f32[20,48,128]{2,1,0:T(8,128)S(1)}, f32[64,8,128]{2,1,0:T(8,128)S(1)}, f32[12,24,128]{2,1,0:T(8,128)S(1)}, ...) custom-call(f32[40,80,128]{2,1,0:T(8,128)S(1)} %get-tuple-element.33.refs_, ...), custom_call_target="tpu_custom_call" | custom-call | flops 40000000 | bytes 1048576 | tf_op jit(solution)/shard_map/pallas_call | solution.py:514
  91.7 24.4 %all_to_all.11.refs_9_ = f32[64,8,128]{2,1,0:T(8,128)S(1)} all-to-all(f32[64,8,128]{2,1,0:T(8,128)S(1)} %get-tuple-element.50), channel_id=1, replica_groups=mesh['groups'=2,'gx'=16,'gy'=4,'gz'=2] {'gx','gy'}, dimensions={0} | all-to-all | bytes 524288 | tf_op jit(solution)/shard_map/all_to_all | solution.py:568
  116.1 5.4 %collective-permute-start.18 = (f32[64,8,128]{2,1,0:T(8,128)S(1)}, f32[64,8,128]{2,1,0:T(8,128)S(1)}, u32[]{:S(2)}, u32[]{:S(2)}) collective-permute-start(f32[64,8,128]{2,1,0:T(8,128)S(1)} %all_to_all.11.refs_9_), channel_id=1, source_target_pairs={{0,1},{1,0},{2,3},{3,2},{4,5},{5,4},{6,7},{7,6},{8,9},{9,8},{10,11... | collective-permute-start | bytes 786440 | tf_op jit(solution)/shard_map/ppermute | solution.py:562
  121.5 0.5 collective-permute-start.14
  121.9 2.2 %collective-permute-start.15 = (f32[2,24,128]{2,1,0:T(8,128)S(1)}, f32[2,24,128]{2,1,0:T(8,128)S(1)}, u32[]{:S(2)}, u32[]{:S(2)}) collective-permute-start(f32[2,24,128]{2,1,0:T(8,128)S(1)} %get-tuple-element.47), channel_id=1, source_target_pairs={{0,120},{8,0},{16,8},{24,16},{32,24},{40,32},{48,40},{56,48},{64,5... | collective-permute-start | bytes 73736 | tf_op jit(solution)/shard_map/ppermute | solution.py:562
  124.1 0.2 collective-permute-start.16
  124.3 2.5 %collective-permute-start.17 = (f32[24,128]{1,0:T(8,128)S(1)}, f32[24,128]{1,0:T(8,128)S(1)}, u32[]{:S(2)}, u32[]{:S(2)}) collective-permute-start(f32[24,128]{1,0:T(8,128)S(1)} %get-tuple-element.49), channel_id=1, source_target_pairs={{0,6},{2,0},{4,2},{6,4},{1,7},{3,1},{5,3},{7,5},{8,14},{10,8},{12,... | collective-permute-start | bytes 36872 | tf_op jit(solution)/shard_map/ppermute | solution.py:562
  126.8 1.1 collective-permute-done.16.refs_7_
  127.9 0.0 collective-permute-done.17.refs_8_
  127.9 0.0 collective-permute-done.14.refs_5_
  127.9 0.0 collective-permute-done.15.refs_6_
  127.9 0.0 collective-permute-done.18.refs_10_
  127.9 8.2 %shard_map.21 = f32[16,32,128]{2,1,0:T(8,128)} custom-call(f32[40,80,128]{2,1,0:T(8,128)S(1)} %get-tuple-element.33.refs_0_, f32[40,80,128]{2,1,0:T(8,128)S(1)} %get-tuple-element.34.refs_1_, f32[20,48,128]{2,1,0:T(8,128)S(1)} %get-tuple-element.43.refs_2_, f32[20,48,128]{2,1,0:T(8,128)S(1)} %get-tuple-element.44.refs_3_, ...), custom_call_target="tpu_custom_call" | custom-call | flops 20000000 | bytes 1048576 | tf_op jit(solution)/shard_map/pallas_call | solution.py:514
  (1 shorter events, 0.0 us)
Async XLA Ops:
  0.0 0.9 copy-start
  1.2 27.0 %collective-permute-start = (f32[10,32,128]{2,1,0:T(8,128)S(1)}, f32[10,32,128]{2,1,0:T(8,128)S(1)}, u32[]{:S(2)}, u32[]{:S(2)}) collective-permute-start(f32[10,32,128]{2,1,0:T(8,128)S(1)} %get-tuple-element.29), channel_id=1, source_target_pairs={{0,8},{8,16},{16,24},{24,32},{32,40},{40,48},{48,56},{56,64},{64,7... | collective-permute-start | bytes 491528 | tf_op jit(solution)/shard_map/ppermute | solution.py:562
  4.6 23.6 %collective-permute-start.1 = (f32[10,32,128]{2,1,0:T(8,128)S(1)}, f32[10,32,128]{2,1,0:T(8,128)S(1)}, u32[]{:S(2)}, u32[]{:S(2)}) collective-permute-start(f32[10,32,128]{2,1,0:T(8,128)S(1)} %get-tuple-element.30), channel_id=1, source_target_pairs={{0,120},{8,0},{16,8},{24,16},{32,24},{40,32},{48,40},{56,48},{64,5... | collective-permute-start | bytes 491528 | tf_op jit(solution)/shard_map/ppermute | solution.py:562
  28.3 6.8 %collective-permute-start.2 = (f32[360,128]{1,0:T(8,128)S(1)}, f32[360,128]{1,0:T(8,128)S(1)}, u32[]{:S(2)}, u32[]{:S(2)}) collective-permute-start(f32[360,128]{1,0:T(8,128)S(1)} %get-tuple-element.31), channel_id=1, source_target_pairs={{0,2},{2,4},{4,6},{6,0},{1,3},{3,5},{5,7},{7,1},{8,10},{10,12},{12... | collective-permute-start | bytes 552968 | tf_op jit(solution)/shard_map/ppermute | solution.py:562
  29.7 7.1 %collective-permute-start.3 = (f32[360,128]{1,0:T(8,128)S(1)}, f32[360,128]{1,0:T(8,128)S(1)}, u32[]{:S(2)}, u32[]{:S(2)}) collective-permute-start(f32[360,128]{1,0:T(8,128)S(1)} %get-tuple-element.32), channel_id=1, source_target_pairs={{0,6},{2,0},{4,2},{6,4},{1,7},{3,1},{5,3},{7,5},{8,14},{10,8},{12,... | collective-permute-start | bytes 552968 | tf_op jit(solution)/shard_map/ppermute | solution.py:562
  31.4 6.0 %collective-permute-start.4 = (f32[16,32,128]{2,1,0:T(8,128)S(1)}, f32[16,32,128]{2,1,0:T(8,128)S(1)}, u32[]{:S(2)}, u32[]{:S(2)}) collective-permute-start(f32[16,32,128]{2,1,0:T(8,128)S(1)} %get-tuple-element.28.mine.refs_0_), channel_id=1, source_target_pairs={{0,1},{1,0},{2,3},{3,2},{4,5},{5,4},{6,7},{7,6},{8,9},{9,8},{10,11... | collective-permute-start | bytes 786440 | tf_op jit(solution)/shard_map/ppermute | solution.py:562
  35.1 3.7 %collective-permute-start.7 = (f32[360,128]{1,0:T(8,128)S(1)}, f32[360,128]{1,0:T(8,128)S(1)}, u32[]{:S(2)}, u32[]{:S(2)}) collective-permute-start(f32[360,128]{1,0:T(8,128)S(1)} %collective-permute-done.2.refs_3_), channel_id=1, source_target_pairs={{0,1},{1,0},{2,3},{3,2},{4,5},{5,4},{6,7},{7,6},{8,9},{9,8},{10,11... | collective-permute-start | bytes 552968 | tf_op jit(solution)/shard_map/ppermute | solution.py:562
  36.9 1.9 %collective-permute-start.8 = (f32[360,128]{1,0:T(8,128)S(1)}, f32[360,128]{1,0:T(8,128)S(1)}, u32[]{:S(2)}, u32[]{:S(2)}) collective-permute-start(f32[360,128]{1,0:T(8,128)S(1)} %collective-permute-done.3.refs_4_), channel_id=1, source_target_pairs={{0,1},{1,0},{2,3},{3,2},{4,5},{5,4},{6,7},{7,6},{8,9},{9,8},{10,11... | collective-permute-start | bytes 552968 | tf_op jit(solution)/shard_map/ppermute | solution.py:562
  36.9 1.7 %collective-permute-start.5 = (f32[10,32,128]{2,1,0:T(8,128)S(1)}, f32[10,32,128]{2,1,0:T(8,128)S(1)}, u32[]{:S(2)}, u32[]{:S(2)}) collective-permute-start(f32[10,32,128]{2,1,0:T(8,128)S(1)} %collective-permute-done.x_low.refs_1_), channel_id=1, source_target_pairs={{0,1},{1,0},{2,3},{3,2},{4,5},{5,4},{6,7},{7,6},{8,9},{9,8},{10,11... | collective-permute-start | bytes 491528 | tf_op jit(solution)/shard_map/ppermute | solution.py:562
  37.4 1.4 %collective-permute-start.6 = (f32[10,32,128]{2,1,0:T(8,128)S(1)}, f32[10,32,128]{2,1,0:T(8,128)S(1)}, u32[]{:S(2)}, u32[]{:S(2)}) collective-permute-start(f32[10,32,128]{2,1,0:T(8,128)S(1)} %collective-permute-done.1.x_high.refs_2_), channel_id=1, source_target_pairs={{0,1},{1,0},{2,3},{3,2},{4,5},{5,4},{6,7},{7,6},{8,9},{9,8},{10,11... | collective-permute-start | bytes 491528 | tf_op jit(solution)/shard_map/ppermute | solution.py:562
  69.7 10.4 %collective-permute-start.13 = (f32[64,8,128]{2,1,0:T(8,128)S(1)}, f32[64,8,128]{2,1,0:T(8,128)S(1)}, u32[]{:S(2)}, u32[]{:S(2)}) collective-permute-start(f32[64,8,128]{2,1,0:T(8,128)S(1)} %all_to_all.10.refs_9_), channel_id=1, source_target_pairs={{0,1},{1,0},{2,3},{3,2},{4,5},{5,4},{6,7},{7,6},{8,9},{9,8},{10,11... | collective-permute-start | bytes 786440 | tf_op jit(solution)/shard_map/ppermute | solution.py:562
  73.4 6.7 %collective-permute-start.9 = (f32[4,24,128]{2,1,0:T(8,128)S(1)}, f32[4,24,128]{2,1,0:T(8,128)S(1)}, u32[]{:S(2)}, u32[]{:S(2)}) collective-permute-start(f32[4,24,128]{2,1,0:T(8,128)S(1)} %get-tuple-element.38), channel_id=1, source_target_pairs={{0,8},{8,16},{16,24},{24,32},{32,40},{40,48},{48,56},{56,64},{64,7... | collective-permute-start | bytes 147464 | tf_op jit(solution)/shard_map/ppermute | solution.py:562
  74.1 5.9 %collective-permute-start.10 = (f32[4,24,128]{2,1,0:T(8,128)S(1)}, f32[4,24,128]{2,1,0:T(8,128)S(1)}, u32[]{:S(2)}, u32[]{:S(2)}) collective-permute-start(f32[4,24,128]{2,1,0:T(8,128)S(1)} %get-tuple-element.39), channel_id=1, source_target_pairs={{0,120},{8,0},{16,8},{24,16},{32,24},{40,32},{48,40},{56,48},{64,5... | collective-permute-start | bytes 147464 | tf_op jit(solution)/shard_map/ppermute | solution.py:562
  76.1 4.0 %collective-permute-start.11 = (f32[64,128]{1,0:T(8,128)S(1)}, f32[64,128]{1,0:T(8,128)S(1)}, u32[]{:S(2)}, u32[]{:S(2)}) collective-permute-start(f32[64,128]{1,0:T(8,128)S(1)} %get-tuple-element.40), channel_id=1, source_target_pairs={{0,2},{2,4},{4,6},{6,0},{1,3},{3,5},{5,7},{7,1},{8,10},{10,12},{12... | collective-permute-start | bytes 98312 | tf_op jit(solution)/shard_map/ppermute | solution.py:562
  76.3 3.7 %collective-permute-start.12 = (f32[64,128]{1,0:T(8,128)S(1)}, f32[64,128]{1,0:T(8,128)S(1)}, u32[]{:S(2)}, u32[]{:S(2)}) collective-permute-start(f32[64,128]{1,0:T(8,128)S(1)} %get-tuple-element.41), channel_id=1, source_target_pairs={{0,6},{2,0},{4,2},{6,4},{1,7},{3,1},{5,3},{7,5},{8,14},{10,8},{12,... | collective-permute-start | bytes 98312 | tf_op jit(solution)/shard_map/ppermute | solution.py:562
  116.1 11.8 %collective-permute-start.18 = (f32[64,8,128]{2,1,0:T(8,128)S(1)}, f32[64,8,128]{2,1,0:T(8,128)S(1)}, u32[]{:S(2)}, u32[]{:S(2)}) collective-permute-start(f32[64,8,128]{2,1,0:T(8,128)S(1)} %all_to_all.11.refs_9_), channel_id=1, source_target_pairs={{0,1},{1,0},{2,3},{3,2},{4,5},{5,4},{6,7},{7,6},{8,9},{9,8},{10,11... | collective-permute-start | bytes 786440 | tf_op jit(solution)/shard_map/ppermute | solution.py:562
  121.5 6.4 %collective-permute-start.14 = (f32[2,24,128]{2,1,0:T(8,128)S(1)}, f32[2,24,128]{2,1,0:T(8,128)S(1)}, u32[]{:S(2)}, u32[]{:S(2)}) collective-permute-start(f32[2,24,128]{2,1,0:T(8,128)S(1)} %get-tuple-element.46), channel_id=1, source_target_pairs={{0,8},{8,16},{16,24},{24,32},{32,40},{40,48},{48,56},{56,64},{64,7... | collective-permute-start | bytes 73736 | tf_op jit(solution)/shard_map/ppermute | solution.py:562
  121.9 6.0 %collective-permute-start.15 = (f32[2,24,128]{2,1,0:T(8,128)S(1)}, f32[2,24,128]{2,1,0:T(8,128)S(1)}, u32[]{:S(2)}, u32[]{:S(2)}) collective-permute-start(f32[2,24,128]{2,1,0:T(8,128)S(1)} %get-tuple-element.47), channel_id=1, source_target_pairs={{0,120},{8,0},{16,8},{24,16},{32,24},{40,32},{48,40},{56,48},{64,5... | collective-permute-start | bytes 73736 | tf_op jit(solution)/shard_map/ppermute | solution.py:562
  124.1 3.8 %collective-permute-start.16 = (f32[24,128]{1,0:T(8,128)S(1)}, f32[24,128]{1,0:T(8,128)S(1)}, u32[]{:S(2)}, u32[]{:S(2)}) collective-permute-start(f32[24,128]{1,0:T(8,128)S(1)} %get-tuple-element.48), channel_id=1, source_target_pairs={{0,2},{2,4},{4,6},{6,0},{1,3},{3,5},{5,7},{7,1},{8,10},{10,12},{12... | collective-permute-start | bytes 36872 | tf_op jit(solution)/shard_map/ppermute | solution.py:562
  124.3 3.6 %collective-permute-start.17 = (f32[24,128]{1,0:T(8,128)S(1)}, f32[24,128]{1,0:T(8,128)S(1)}, u32[]{:S(2)}, u32[]{:S(2)}) collective-permute-start(f32[24,128]{1,0:T(8,128)S(1)} %get-tuple-element.49), channel_id=1, source_target_pairs={{0,6},{2,0},{4,2},{6,4},{1,7},{3,1},{5,3},{7,5},{8,14},{10,8},{12,... | collective-permute-start | bytes 36872 | tf_op jit(solution)/shard_map/ppermute | solution.py:562
where the time goes:
time: 137 us; the launch traced here: 136 us
  blocking collectives  52.4 us (38%)
  starting transfers between devices  49.9 us (36%)
  Pallas kernels  23 us (17%)
  waiting for transfers between devices  9.83 us (7%)
    all_to_all x2, blocking collectives, exchange(): mine = lax.all_to_all(send, ('gx', 'gy'), 0, 0, tiled=True)  52.4 us
    ppermute x19, starting transfers between devices, from_(): lax.ppermute(value, axis, [(i, (i + step) % size) for i in range(size)])  49.9 us
    pallas_call x5, Pallas kernels, run(): pl.pallas_call(kernel, out_shape=outs, scratch_shapes=scratch, compiler_p...  23 us
    ppermute x19, waiting for transfers between devices, from_(): lax.ppermute(value, axis, [(i, (i + step) % size) for i in range(size)])  9.83 us
  transfers between devices with their start and end apart: 19, of which 6 were waited for; matrix products, arithmetic and copies ran while one was open for 0% of the time, Pallas kernels for 0%

commit v1 on v0

--- a/solution.py
+++ b/solution.py
@@ -2,11 +2,13 @@
 
 import jax
 import jax.numpy as jnp
+import numpy as np
 from jax import lax
 from jax.experimental import pallas as pl
 from jax.experimental.pallas import tpu as pltpu
 from jax.sharding import PartitionSpec as P
 
+LEVELS = 7
 LANES = 128
 OMEGA = 2.0 / 3.0
 SCREEN = 0.001
@@ -58,12 +60,6 @@
 def dot(a, b):
     b = b.astype(jnp.bfloat16)
     high, middle, low = (product(p, b) for p in parts(a))
-    return high + (middle + low)
-
-
-def dot_rows(a, b):
-    a = a.astype(jnp.bfloat16)
-    high, middle, low = (product(a, p) for p in parts(b))
     return high + (middle + low)
 
 
@@ -163,6 +159,10 @@
 
 def sizes_2():
     return lax.axis_size("gx") * BX // 4, lax.axis_size("gy") * BY // 4, lax.axis_size("gz") * LANES // 4
+
+
+def bottom_shape():
+    return tuple(n // 8 for n in sizes_2())
 
 
 def coarse_source(out, f1, v1, r1, core):
@@ -189,26 +189,60 @@
         out[s] = packed
 
 
-def beside_whole(v):
-    n = v.shape[0]
+def across(v):
+    n, rows = v.shape[0], v.shape[1]
     up = jnp.concatenate([v[n - 1 :], v[: n - 1]], axis=0)
     down = jnp.concatenate([v[1:], v[:1]], axis=0)
-    y = pltpu.roll(v, 1, 1) + pltpu.roll(v, v.shape[1] - 1, 1)
-    return (up + down) + y + (pltpu.roll(v, 1, 2) + pltpu.roll(v, LANES - 1, 2))
-
-
-def from_zero(level, f):
-    return twice_from_zero(level, f, beside_whole(f))
-
-
-def residual_whole(level, f, v):
-    return residual_of(level, f, v, beside_whole(v))
-
-
-def smooth_whole(level, f, v):
-    for _ in range(2):
-        v = relaxed(level, f, v, beside_whole(v))
-    return v
+    return (up + down) + (pltpu.roll(v, 1, 1) + pltpu.roll(v, rows - 1, 1))
+
+
+def applied(level, v):
+    a, _ = coefficients(level)
+    z1 = pltpu.roll(v, 1, 2) + pltpu.roll(v, LANES - 1, 2)
+    z2 = pltpu.roll(v, 2, 2) + pltpu.roll(v, LANES - 2, 2)
+    one = across(v)
+    sv = one + z1
+    ssv = across(one + 2.0 * z1) + (z2 + 2.0 * v)
+    t = 6.0 * v - sv
+    tt = 6.0 * t - (6.0 * sv - ssv)
+    return t, a * t + SCREEN * v, (a * a) * tt + (2.0 * a * SCREEN) * t + (SCREEN * SCREEN) * v
+
+
+def start_whole(level, f):
+    a, k = coefficients(level)
+    t, af, aaf = applied(level, f)
+    return (2.0 * k - k * k * SCREEN) * f - (k * k * a) * t, f - 2.0 * k * af + (k * k) * aaf, af
+
+
+def smooth_whole(level, f, af, v):
+    a, k = coefficients(level)
+    t, _, aav = applied(level, v)
+    r = (f - a * t) - SCREEN * v
+    return v + 2.0 * k * r - (k * k) * (af - aav)
+
+
+def bottom_matrix(shape):
+    def beside(v):
+        return sum(np.roll(v, step, axis) for axis in (1, 2, 3) for step in (1, -1))
+
+    def residual(level, f, v):
+        return f - ((6.0 * v - beside(v)) * 0.25**level + SCREEN * v)
+
+    def cycle(level, f):
+        v = np.zeros_like(f)
+        for _ in range(2):
+            v = v + OMEGA * residual(level, f, v) / (6.0 * 0.25**level + SCREEN)
+        if level == LEVELS - 1:
+            return v
+        n, x, y, z = f.shape
+        coarse = residual(level, f, v).reshape(n, x // 2, 2, y // 2, 2, z // 2, 2).mean(axis=(2, 4, 6))
+        v = v + cycle(level + 1, coarse).repeat(2, 1).repeat(2, 2).repeat(2, 3)
+        for _ in range(2):
+            v = v + OMEGA * residual(level, f, v) / (6.0 * 0.25**level + SCREEN)
+        return v
+
+    cells = shape[0] * shape[1] * shape[2]
+    return cycle(5, np.eye(cells).reshape(cells, *shape)).reshape(cells, cells).astype(np.float32)
 
 
 def down_z(level):
@@ -234,39 +268,39 @@
     return v.reshape(-1, LANES)
 
 
-def row_sums(size, y_size):
-    out, source = iota((size, size), 0), iota((size, size), 1)
-    first = (out // 8) * 8 + 2 * lax.rem(lax.rem(out, 8), y_size)
-    return jnp.where((source == first) | (source == first + 1), 1.0, 0.0).astype(F32)
-
-
-def row_picks(size, y_size):
-    out, source = iota((size, size), 0), iota((size, size), 1)
-    first = (out // 8) * 8 + lax.div(lax.rem(lax.rem(out, 8), y_size), 2)
-    return jnp.where(source == first, 1.0, 0.0).astype(F32)
-
-
-def solve_3(f3, t3):
+def solve_bottom(s, shape, matrix):
+    x5, y5, z5 = shape
+    cells = x5 * y5 * z5
+    rows = s.shape[0]
+    cell, row = iota((rows, cells), 1), iota((rows, cells), 0)
+    mine = (cell // (y5 * z5) == row // (2 * y5)) & (lax.rem(cell // z5, y5) == lax.rem(row, 2 * y5) // 2)
+    source, out = iota((LANES, cells), 0), lax.rem(iota((LANES, cells), 1), z5)
+    means = jnp.where((source == 2 * out) | (source == 2 * out + 1), 0.125, 0.0).astype(F32)
+    f5 = jnp.sum(jnp.where(mine, dot(s, means), 0.0), axis=0, keepdims=True)
+    f_high, f_middle, f_low = parts(jnp.broadcast_to(f5, (8, cells)))
+    m_high, m_middle, m_low = parts(matrix[...])
+    v5 = product(f_high, m_high) + (
+        (product(f_high, m_middle) + product(f_middle, m_high))
+        + (product(f_high, m_low) + product(f_middle, m_middle) + product(f_low, m_high))
+    )
+    spread = jnp.where(mine, jnp.broadcast_to(v5[0:1], (rows, cells)), 0.0)
+    source, out = lax.rem(iota((cells, LANES), 0), z5), lax.rem(iota((cells, LANES), 1), 2 * z5)
+    return dot(spread, jnp.where(source == out // 2, 1.0, 0.0).astype(F32))
+
+
+def solve_3(f3, t3, matrix):
     x4, y4 = f3.shape[0] // 2, f3.shape[1] // 2
-    v3 = from_zero(3, f3)
-    t3[...] = pair_layers(residual_whole(3, f3, v3))
+    v3, r3, af3 = start_whole(3, f3)
+    t3[...] = pair_layers(r3)
     s = t3[:, pl.ds(0, y4, stride=2), :] + t3[:, pl.ds(1, y4, stride=2), :]
     f4 = dot(flat(s), down_z(3)).reshape(x4, y4, LANES)
-    v4 = from_zero(4, f4)
-    s = flat(pair_layers(residual_whole(4, f4, v4)))
-    f5 = dot_rows(row_sums(s.shape[0], y4 // 2), dot(s, down_z(4))).reshape(x4 // 2, 8, LANES)
-    v5 = from_zero(5, f5)
-    s = flat(pair_layers(residual_whole(5, f5, v5)))
-    f6 = dot_rows(row_sums(s.shape[0], y4 // 4), dot(s, down_z(5))).reshape(x4 // 4, 8, LANES)
-    v6 = flat(from_zero(6, f6))
-    e5 = dot_rows(row_picks(v6.shape[0], y4 // 2), dot(v6, up_z(5))).reshape(x4 // 4, 8, LANES)
-    v5 = flat(smooth_whole(5, f5, v5 + twice(e5)))
-    e4 = dot_rows(row_picks(v5.shape[0], y4), dot(v5, up_z(4))).reshape(x4 // 2, 8, LANES)
-    v4 = smooth_whole(4, f4, v4 + twice(e4))
+    v4, r4, af4 = start_whole(4, f4)
+    e4 = solve_bottom(flat(pair_layers(r4)), bottom_shape(), matrix).reshape(x4 // 2, y4, LANES)
+    v4 = smooth_whole(4, f4, af4, v4 + twice(e4))
     e3 = dot(flat(v4), up_z(3)).reshape(x4, y4, LANES)
     t3[:, pl.ds(0, y4, stride=2), :] = e3
     t3[:, pl.ds(1, y4, stride=2), :] = e3
-    return smooth_whole(3, f3, v3 + twice(t3[...]))
+    return smooth_whole(3, f3, af3, v3 + twice(t3[...]))
 
 
 def unpack_2(f2, mine, other, core):
@@ -297,7 +331,7 @@
     )
 
 
-def level_2(near, f2, v2, t2, t3, s3, p2, a2, b2, gx, halo):
+def level_2(near, f2, v2, t2, t3, s3, p2, a2, b2, matrix, fetch, gx, halo):
     n, rows = f2.shape[0], f2.shape[1]
 
     def around(ref, i):
@@ -319,7 +353,8 @@
     over_layers(0, n // 2, 8, second)
     s = t2[:, pl.ds(0, rows // 2, stride=2), :] + t2[:, pl.ds(1, rows // 2, stride=2), :]
     f3 = dot(flat(s), down_z(2)).reshape(n // 2, rows // 2, LANES)
-    s3[...] = solve_3(f3, t3)
+    fetch.wait()
+    s3[...] = solve_3(f3, t3, matrix)
 
     count = 4 + 2 * halo + 4
     start = gx * 4 - halo - 2 + n
@@ -365,27 +400,37 @@
             )
 
 
-def lay_out_1(dst, f1, x_low, x_high, y_low, y_high, own, width):
-    count = f1.shape[0]
-    for m in range(count):
+def lay_out_1(dst, f1, edges, core, own, width):
+    up, down = edges[0][...], edges[1][...]
+    other_up, other_down = (pltpu.roll(edge[...], 64, 1) for edge in edges[2:])
+    first = core == 0
+    x_low, y_low = jnp.where(first, up, other_up), jnp.where(first, other_up, up)
+    x_high, y_high = jnp.where(first, down, other_down), jnp.where(first, other_down, down)
+    for m in range(f1.shape[0]):
         i = X1 - own + m
         dst[i, pl.ds(Y1 - 4, 24), :] = f1[m]
-        dst[i, pl.ds(Y1 - own - width, width), :] = y_low[pl.ds(m * width, width), :]
-        dst[i, pl.ds(Y1 + 16 + own, width), :] = y_high[pl.ds(m * width, width), :]
+        dst[i, pl.ds(Y1 - own - width, width), :] = y_low[m * width : (m + 1) * width]
+        dst[i, pl.ds(Y1 + 16 + own, width), :] = y_high[m * width : (m + 1) * width]
     for m in range(width):
-        dst[X1 - own - width + m, pl.ds(Y1 - 4, 24), :] = x_low[m]
-        dst[X1 + 8 + own + m, pl.ds(Y1 - 4, 24), :] = x_high[m]
-
-
-def put_out_1(out, up_x, down_x, up_y, down_y, f1, own, width):
+        dst[X1 - own - width + m, pl.ds(Y1 - 4, 24), :] = x_low[m * 24 : (m + 1) * 24]
+        dst[X1 + 8 + own + m, pl.ds(Y1 - 4, 24), :] = x_high[m * 24 : (m + 1) * 24]
+
+
+def put_out_1(out, up, down, f1, core, own, width):
     for m in range(out.shape[0]):
-        i = X1 - own + m
-        out[m] = f1[i, pl.ds(Y1 - 4, 24), :]
-        up_y[pl.ds(m * width, width), :] = f1[i, pl.ds(Y1 + 16 - own - width, width), :]
-        down_y[pl.ds(m * width, width), :] = f1[i, pl.ds(Y1 + own, width), :]
-    for m in range(width):
-        up_x[m] = f1[X1 + 8 - own - width + m, pl.ds(Y1 - 4, 24), :]
-        down_x[m] = f1[X1 + own + m, pl.ds(Y1 - 4, 24), :]
+        out[m] = f1[X1 - own + m, pl.ds(Y1 - 4, 24), :]
+
+    @pl.when(core == 0)
+    def _():
+        for m in range(width):
+            up[pl.ds(m * 24, 24), :] = f1[X1 + 8 - own - width + m, pl.ds(Y1 - 4, 24), :]
+            down[pl.ds(m * 24, 24), :] = f1[X1 + own + m, pl.ds(Y1 - 4, 24), :]
+
+    @pl.when(core == 1)
+    def _():
+        for m in range(out.shape[0]):
+            up[pl.ds(m * width, width), :] = f1[X1 - own + m, pl.ds(Y1 + 16 - own - width, width), :]
+            down[pl.ds(m * width, width), :] = f1[X1 - own + m, pl.ds(Y1 + own, width), :]
 
 
 def split_kernel(charge, mine, up, down):
@@ -429,24 +474,27 @@
 
 def first_kernel(where, *refs):
     ours, others, refs = refs[0:5], refs[5:10], refs[10:]
-    (f_e, f_o, v_e, v_o, send), f1_outs, (f1, v1, r1, t0) = refs[:5], refs[5:10], refs[10:]
+    (f_e, f_o, v_e, v_o, send), f1_outs, (f1, v1, r1, t0) = refs[:5], refs[5:8], refs[8:]
+    core = where()[2]
     force, v = (f_e, f_o), (v_e, v_o)
     lay_out_0(f_e, f_o, ours, others)
     start_0(v, force, 9, 7)
     restrict_0(f1, t0, v, force, 4)
-    coarse_source(send, f1, v1, r1, where()[2])
-    put_out_1(*f1_outs, f1, 4, 4)
+    coarse_source(send, f1, v1, r1, core)
+    put_out_1(*f1_outs, f1, core, 4, 4)
 
 
 def middle_kernel(where, *refs):
-    f_e, f_o, v_e, v_o, f1_in, x_low, x_high, y_low, y_high, mine, other = refs[:11]
-    (n_e, n_o, send), f1_outs = refs[11:14], refs[14:19]
-    a_e, a_o, b_e, b_o, f1, v1, r1, p1, y2, p0, t0, f2, v2, t2, t3, s3, p2, a2, b2, near = refs[19:]
+    bottom, f_e, f_o, v_e, v_o, f1_in, mine, other, *edges = refs[:12]
+    (n_e, n_o, send), f1_outs = refs[12:15], refs[15:18]
+    a_e, a_o, b_e, b_o, f1, v1, r1, p1, y2, p0, t0, f2, v2, t2, t3, s3, p2, a2, b2, near, matrix, arrived = refs[18:]
+    fetch = pltpu.make_async_copy(bottom, matrix, arrived)
+    fetch.start()
     gx, gy, core = where()
     force, v, a0, b0 = (f_e, f_o), (v_e, v_o), (a_e, a_o), (b_e, b_o)
     unpack_2(f2, mine, other, core)
-    level_2(near, f2, v2, t2, t3, s3, p2, a2, b2, gx, 4)
-    lay_out_1(f1, f1_in, x_low, x_high, y_low, y_high, 4, 4)
+    level_2(near, f2, v2, t2, t3, s3, p2, a2, b2, matrix, fetch, gx, 4)
+    lay_out_1(f1, f1_in, edges, core, 4, 4)
     start_1(v1, f1, 7, 12)
     add_from_2(v1, near, y2, p1, gy, core, 4)
     sweep_1(r1, v1, f1, 6, 12)
@@ -458,19 +506,21 @@
     sweep_0(a0, b0, force, 5, 7)
     restrict_0(f1, t0, a0, force, 2)
     coarse_source(send, f1, v1, r1, core)
-    put_out_1(*f1_outs, f1, 2, 2)
+    put_out_1(*f1_outs, f1, core, 2, 2)
     for src, dst in ((a_e, n_e), (a_o, n_o)):
         dst[...] = src[pl.ds(X0 - 2, 20), pl.ds(Y0 - 8, 48), :]
 
 
 def last_kernel(where, *refs):
-    f_e, f_o, n_e, n_o, f1_in, x_low, x_high, y_low, y_high, mine, other, out = refs[:12]
-    a_e, a_o, b_e, b_o, f1, v1, r1, p1, y2, p0, _, f2, v2, t2, t3, s3, p2, a2, b2, near = refs[12:]
+    bottom, f_e, f_o, n_e, n_o, f1_in, mine, other, *edges = refs[:12]
+    out, a_e, a_o, b_e, b_o, f1, v1, r1, p1, y2, p0, _, f2, v2, t2, t3, s3, p2, a2, b2, near, matrix, arrived = refs[12:]
+    fetch = pltpu.make_async_copy(bottom, matrix, arrived)
+    fetch.start()
     gx, gy, core = where()
     force, v, a0, b0 = (f_e, f_o), (n_e, n_o), (a_e, a_o), (b_e, b_o)
     unpack_2(f2, mine, other, core)
-    level_2(near, f2, v2, t2, t3, s3, p2, a2, b2, gx, 2)
-    lay_out_1(f1, f1_in, x_low, x_high, y_low, y_high, 2, 2)
+    level_2(near, f2, v2, t2, t3, s3, p2, a2, b2, matrix, fetch, gx, 2)
+    lay_out_1(f1, f1_in, edges, core, 2, 2)
     start_1(v1, f1, 3, 14)
     add_from_2(v1, near, y2, p1, gy, core, 2)
     sweep_1(r1, v1, f1, 2, 12)
@@ -499,6 +549,7 @@
 
 def scratch_for_cycle():
     x2, y2, _ = sizes_2()
+    cells = int(np.prod(bottom_shape()))
     return (
         [vm(XA0, YA0, LANES)] * 4
         + [vm(XA1, YA1, LANES)] * 3
@@ -506,13 +557,15 @@
         + [vm(x2, y2, LANES)] * 2
         + [vm(x2 // 2, y2, LANES), vm(x2 // 4, y2 // 2, LANES), vm(x2 // 2, y2 // 2, LANES), vm(8, y2, LANES)]
         + [vm(16, y2, LANES)] * 2
-        + [vm(12, y2, LANES)]
+        + [vm(12, y2, LANES), vm(cells, cells), pltpu.SemaphoreType.DMA(())]
     )
 
 
-def run(kernel, outs, scratch, flops, *args):
+def run(kernel, outs, scratch, flops, *args, fetched=0):
+    spaces = [pltpu.HBM] * fetched + [pltpu.VMEM] * (len(args) - fetched)
     return pl.pallas_call(
         kernel,
+        in_specs=[pl.BlockSpec(memory_space=space) for space in spaces],
         out_shape=outs,
         scratch_shapes=scratch,
         compiler_params=pltpu.CompilerParams(vmem_limit_bytes=40 * 2**20),
@@ -525,8 +578,7 @@
 
 
 def sources_out(layers, width):
-    y = kept(layers * width, LANES)
-    return [kept(peers(), 8, LANES), kept(layers, 24, LANES)] + [kept(width, 24, LANES)] * 2 + [y] * 2
+    return [kept(peers(), 8, LANES), kept(layers, 24, LANES)] + [kept(width * 24, LANES)] * 2
 
 
 def peers():
@@ -549,12 +601,12 @@
 
 def middle(*args):
     outs = [kept(20, 48, LANES)] * 2 + sources_out(12, 2)
-    return run(functools.partial(middle_kernel, where_am_i), outs, scratch_for_cycle(), 4 * 10**7, *args)
+    return run(functools.partial(middle_kernel, where_am_i), outs, scratch_for_cycle(), 4 * 10**7, *args, fetched=1)
 
 
 def last(*args):
     outs = kept(BX, BY, LANES)
-    return run(functools.partial(last_kernel, where_am_i), outs, scratch_for_cycle(), 2 * 10**7, *args)
+    return run(functools.partial(last_kernel, where_am_i), outs, scratch_for_cycle(), 2 * 10**7, *args, fetched=1)
 
 
 def from_(value, axis, step):
@@ -562,11 +614,22 @@
     return lax.ppermute(value, axis, [(i, (i + step) % size) for i in range(size)])
 
 
-def exchange(send, f1, up_x, down_x, up_y, down_y):
-    x_low, x_high = from_(up_x, "gx", 1), from_(down_x, "gx", -1)
-    y_low, y_high = from_(up_y, "gy", 1), from_(down_y, "gy", -1)
+def beside_(value, step):
+    axes = ("gx", "gy", "gz")
+    sizes = [lax.axis_size(axis) for axis in axes]
+    pairs = []
+    for device in np.ndindex(*sizes):
+        to = list(device)
+        to[device[2]] = (to[device[2]] + step) % sizes[device[2]]
+        pairs.append((int(np.ravel_multi_index(device, sizes)), int(np.ravel_multi_index(to, sizes))))
+    return lax.ppermute(value, axes, pairs)
+
+
+def exchange(send, f1, up, down):
+    up, down = beside_(up, 1), beside_(down, -1)
     mine = lax.all_to_all(send, ("gx", "gy"), 0, 0, tiled=True)
-    return f1, x_low, x_high, y_low, y_high, mine, from_(mine, "gz", 1)
+    other, other_up, other_down = (from_(v, "gz", 1) for v in (mine, up, down))
+    return f1, mine, other, up, down, other_up, other_down
 
 
 def local(charge):
@@ -577,8 +640,9 @@
     ours = (mine, x_low, x_high, y_low, y_high)
     others = [from_(v, "gz", 1) for v in ours]
     f_e, f_o, v_e, v_o, *rest = first(*ours, *others)
-    n_e, n_o, *rest = middle(f_e, f_o, v_e, v_o, *exchange(*rest))
-    return last(f_e, f_o, n_e, n_o, *exchange(*rest))
+    bottom = jnp.asarray(bottom_matrix(bottom_shape()))
+    n_e, n_o, *rest = middle(bottom, f_e, f_o, v_e, v_o, *exchange(*rest))
+    return last(bottom, f_e, f_o, n_e, n_o, *exchange(*rest))
 
 
 def solution(mesh):

time: 137 us -> 135 us (0.985)
  starting transfers between devices: 49.9 us -> 45.2 us
  waiting for transfers between devices: 9.83 us -> 12.8 us
  blocking collectives: 52.4 us -> 54.3 us
  Pallas kernels: 23 us -> 21.5 us
    ppermute x19 -> x15, starting transfers between devices: 49.9 us -> 39.9 us  [from_(): lax.ppermute(value, axis, [(i, (i + step) % size) for i in range(size)])]
    ppermute x0 -> x4, starting transfers between devices: none -> 5.35 us  [beside_(): return lax.ppermute(value, axes, pairs)]
    ppermute x0 -> x4, waiting for transfers between devices: none -> 2.98 us  [beside_(): return lax.ppermute(value, axes, pairs)]
    all_to_all x2, blocking collectives: 52.4 us -> 54.3 us  [exchange(): mine = lax.all_to_all(send, ('gx', 'gy'), 0, 0, tiled=True)]
    pallas_call x5, Pallas kernels: 23 us -> 21.5 us  [run(): pl.pallas_call(kernel, in_specs=[pl.BlockSpec(memory_space=space) for spa...]
    ppermute x19 -> x15, waiting for transfers between devices: 9.83 us -> 9.86 us  [from_(): lax.ppermute(value, axis, [(i, (i + step) % size) for i in range(size)])]
  transfers between devices with their start and end apart: 19 -> 19, of which waited for: 6 -> 10; matrix products, arithmetic and copies ran while one was open for 0% -> 0% of each run, Pallas kernels for 0% -> 0%
where the time goes in v1:
time: 135 us
  blocking collectives  54.3 us (40%)
  starting transfers between devices  45.2 us (33%)
  Pallas kernels  21.5 us (16%)
  waiting for transfers between devices  12.8 us (9%)
    all_to_all x2, blocking collectives, exchange(): mine = lax.all_to_all(send, ('gx', 'gy'), 0, 0, tiled=True)  54.3 us
    ppermute x15, starting transfers between devices, from_(): lax.ppermute(value, axis, [(i, (i + step) % size) for i in range(size)])  39.9 us
    pallas_call x5, Pallas kernels, run(): pl.pallas_call(kernel, in_specs=[pl.BlockSpec(memory_space=space) for spa...  21.5 us
    ppermute x15, waiting for transfers between devices, from_(): lax.ppermute(value, axis, [(i, (i + step) % size) for i in range(size)])  9.86 us
    ppermute x4, starting transfers between devices, beside_(): return lax.ppermute(value, axes, pairs)  5.35 us
    ppermute x4, waiting for transfers between devices, beside_(): return lax.ppermute(value, axes, pairs)  2.98 us
  transfers between devices with their start and end apart: 19, of which 10 were waited for; matrix products, arithmetic and copies ran while one was open for 0% of the time, Pallas kernels for 0%

profile of v1, /device:TPU:33, one launch (start us, length us, event | category | flops | bytes accessed | tf_op | source)
XLA Modules:
  0.0 135.0 jit_solution(5277562762212903971)
XLA Ops:
  0.0 0.0 copy-start
  0.0 0.0 copy-start.1
  0.0 1.0 copy-done.1
  1.0 0.3 shard_map.28
  1.3 3.4 %collective-permute-start = (f32[10,32,128]{2,1,0:T(8,128)S(1)}, f32[10,32,128]{2,1,0:T(8,128)S(1)}, u32[]{:S(2)}, u32[]{:S(2)}) collective-permute-start(f32[10,32,128]{2,1,0:T(8,128)S(1)} %get-tuple-element.25), channel_id=1, source_target_pairs={{0,8},{8,16},{16,24},{24,32},{32,40},{40,48},{48,56},{56,64},{64,7... | collective-permute-start | bytes 491528 | tf_op jit(solution)/shard_map/ppermute | solution.py:614
  4.7 19.7 %collective-permute-start.1 = (f32[10,32,128]{2,1,0:T(8,128)S(1)}, f32[10,32,128]{2,1,0:T(8,128)S(1)}, u32[]{:S(2)}, u32[]{:S(2)}) collective-permute-start(f32[10,32,128]{2,1,0:T(8,128)S(1)} %get-tuple-element.26), channel_id=1, source_target_pairs={{0,120},{8,0},{16,8},{24,16},{32,24},{40,32},{48,40},{56,48},{64,5... | collective-permute-start | bytes 491528 | tf_op jit(solution)/shard_map/ppermute | solution.py:614
  24.4 3.8 %collective-permute-done.x_low.refs_1_ = f32[10,32,128]{2,1,0:T(8,128)S(1)} collective-permute-done((f32[10,32,128]{2,1,0:T(8,128)S(1)}, f32[10,32,128]{2,1,0:T(8,128)S(1)}, u32[]{:S(2)}, u32[]{:S(2)}) %collective-permute-start) | collective-permute-done | bytes 163872 | tf_op jit(solution)/shard_map/ppermute | solution.py:614
  28.3 0.0 collective-permute-done.1.x_high.refs_2_
  28.3 1.5 %collective-permute-start.2 = (f32[360,128]{1,0:T(8,128)S(1)}, f32[360,128]{1,0:T(8,128)S(1)}, u32[]{:S(2)}, u32[]{:S(2)}) collective-permute-start(f32[360,128]{1,0:T(8,128)S(1)} %get-tuple-element.27), channel_id=1, source_target_pairs={{0,2},{2,4},{4,6},{6,0},{1,3},{3,5},{5,7},{7,1},{8,10},{10,12},{12... | collective-permute-start | bytes 552968 | tf_op jit(solution)/shard_map/ppermute | solution.py:614
  29.8 1.7 %collective-permute-start.3 = (f32[360,128]{1,0:T(8,128)S(1)}, f32[360,128]{1,0:T(8,128)S(1)}, u32[]{:S(2)}, u32[]{:S(2)}) collective-permute-start(f32[360,128]{1,0:T(8,128)S(1)} %get-tuple-element.28), channel_id=1, source_target_pairs={{0,6},{2,0},{4,2},{6,4},{1,7},{3,1},{5,3},{7,5},{8,14},{10,8},{12,... | collective-permute-start | bytes 552968 | tf_op jit(solution)/shard_map/ppermute | solution.py:614
  31.5 1.5 %collective-permute-start.4 = (f32[16,32,128]{2,1,0:T(8,128)S(1)}, f32[16,32,128]{2,1,0:T(8,128)S(1)}, u32[]{:S(2)}, u32[]{:S(2)}) collective-permute-start(f32[16,32,128]{2,1,0:T(8,128)S(1)} %get-tuple-element.24.mine.refs_0_), channel_id=1, source_target_pairs={{0,1},{1,0},{2,3},{3,2},{4,5},{5,4},{6,7},{7,6},{8,9},{9,8},{10,11... | collective-permute-start | bytes 786440 | tf_op jit(solution)/shard_map/ppermute | solution.py:614
  32.9 2.2 %collective-permute-done.2.refs_3_ = f32[360,128]{1,0:T(8,128)S(1)} collective-permute-done((f32[360,128]{1,0:T(8,128)S(1)}, f32[360,128]{1,0:T(8,128)S(1)}, u32[]{:S(2)}, u32[]{:S(2)}) %collective-permute-start.2) | collective-permute-done | bytes 184352 | tf_op jit(solution)/shard_map/ppermute | solution.py:614
  35.1 1.8 %collective-permute-start.7 = (f32[360,128]{1,0:T(8,128)S(1)}, f32[360,128]{1,0:T(8,128)S(1)}, u32[]{:S(2)}, u32[]{:S(2)}) collective-permute-start(f32[360,128]{1,0:T(8,128)S(1)} %collective-permute-done.2.refs_3_), channel_id=1, source_target_pairs={{0,1},{1,0},{2,3},{3,2},{4,5},{5,4},{6,7},{7,6},{8,9},{9,8},{10,11... | collective-permute-start | bytes 552968 | tf_op jit(solution)/shard_map/ppermute | solution.py:614
  36.9 0.0 collective-permute-done.3.refs_4_
  36.9 0.0 collective-permute-start.8
  36.9 0.5 collective-permute-start.5
  37.4 0.0 collective-permute-start.6
  37.4 0.0 collective-permute-done.4.refs_5_
  37.4 1.1 collective-permute-done.5.refs_6_
  38.6 0.2 collective-permute-done.6.refs_7_
  38.8 0.0 collective-permute-done.7.refs_8_
  38.8 0.0 collective-permute-done.8.refs_9_
  38.8 2.9 %shard_map.30 = (f32[40,80,128]{2,1,0:T(8,128)S(1)}, f32[40,80,128]{2,1,0:T(8,128)S(1)}, f32[40,80,128]{2,1,0:T(8,128)S(1)}, f32[40,80,128]{2,1,0:T(8,128)S(1)},...) custom-call(f32[16,32,128]{2,1,0:T(8,128)S(1)} %get-tuple-element.24.min, ...), custom_call_target="tpu_custom_call" | custom-call | flops 10000000 | bytes 1048576 | tf_op jit(solution)/shard_map/pallas_call | solution.py:566
  41.8 27.9 %all_to_all.10.refs_6_ = f32[64,8,128]{2,1,0:T(8,128)S(1)} all-to-all(f32[64,8,128]{2,1,0:T(8,128)S(1)} %get-tuple-element.34), channel_id=1, replica_groups=mesh['groups'=2,'gx'=16,'gy'=4,'gz'=2] {'gx','gy'}, dimensions={0} | all-to-all | bytes 524288 | tf_op jit(solution)/shard_map/all_to_all | solution.py:630
  69.7 3.7 %collective-permute-start.9 = (f32[64,8,128]{2,1,0:T(8,128)S(1)}, f32[64,8,128]{2,1,0:T(8,128)S(1)}, u32[]{:S(2)}, u32[]{:S(2)}) collective-permute-start(f32[64,8,128]{2,1,0:T(8,128)S(1)} %all_to_all.10.refs_6_), channel_id=1, source_target_pairs={{0,1},{1,0},{2,3},{3,2},{4,5},{5,4},{6,7},{7,6},{8,9},{9,8},{10,11... | collective-permute-start | bytes 786440 | tf_op jit(solution)/shard_map/ppermute | solution.py:614
  73.5 0.2 collective-permute-start.10
  73.7 2.4 %collective-permute-start.11 = (f32[96,128]{1,0:T(8,128)S(1)}, f32[96,128]{1,0:T(8,128)S(1)}, u32[]{:S(2)}, u32[]{:S(2)}) collective-permute-start(f32[96,128]{1,0:T(8,128)S(1)} %get-tuple-element.36), channel_id=1, source_target_pairs={{0,120},{1,7},{2,122},{3,1},{4,124},{5,3},{6,126},{7,5},{8,0},{9,1... | collective-permute-start | bytes 147464 | tf_op jit(solution)/shard_map/ppermute | solution.py:625
  76.1 1.8 %collective-permute-done.10.refs_8_ = f32[96,128]{1,0:T(8,128)S(1)} collective-permute-done((f32[96,128]{1,0:T(8,128)S(1)}, f32[96,128]{1,0:T(8,128)S(1)}, u32[]{:S(2)}, u32[]{:S(2)}) %collective-permute-start.10) | collective-permute-done | bytes 49184 | tf_op jit(solution)/shard_map/ppermute | solution.py:625
  77.9 0.9 collective-permute-start.12
  78.8 0.0 collective-permute-done.11.refs_9_
  78.8 0.0 collective-permute-start.13
  78.8 0.9 collective-permute-done.12.refs_10_
  79.6 0.4 collective-permute-done.13.refs_11_
  80.0 0.0 collective-permute-done.9.refs_7_
  80.0 0.0 copy-done
  80.0 10.9 %shard_map.31 = (f32[20,48,128]{2,1,0:T(8,128)S(1)}, f32[20,48,128]{2,1,0:T(8,128)S(1)}, f32[64,8,128]{2,1,0:T(8,128)S(1)}, f32[12,24,128]{2,1,0:T(8,128)S(1)}, ...) custom-call(f32[256,256]{1,0:T(8,128)S(1)} %copy-done, f32[40,80,128]{2,1,0:T(8,128)S(1)} %get-tuple-element.29.refs_1_, ...), custom_call_target="tpu_custom_call" | custom-call | flops 40000000 | bytes 1048576 | tf_op jit(solution)/shard_map/pallas_call | solution.py:566
  90.9 26.3 %all_to_all.11.refs_6_ = f32[64,8,128]{2,1,0:T(8,128)S(1)} all-to-all(f32[64,8,128]{2,1,0:T(8,128)S(1)} %get-tuple-element.40), channel_id=1, replica_groups=mesh['groups'=2,'gx'=16,'gy'=4,'gz'=2] {'gx','gy'}, dimensions={0} | all-to-all | bytes 524288 | tf_op jit(solution)/shard_map/all_to_all | solution.py:630
  117.2 4.0 %collective-permute-start.14 = (f32[64,8,128]{2,1,0:T(8,128)S(1)}, f32[64,8,128]{2,1,0:T(8,128)S(1)}, u32[]{:S(2)}, u32[]{:S(2)}) collective-permute-start(f32[64,8,128]{2,1,0:T(8,128)S(1)} %all_to_all.11.refs_6_), channel_id=1, source_target_pairs={{0,1},{1,0},{2,3},{3,2},{4,5},{5,4},{6,7},{7,6},{8,9},{9,8},{10,11... | collective-permute-start | bytes 786440 | tf_op jit(solution)/shard_map/ppermute | solution.py:614
  121.2 0.3 collective-permute-start.15
  121.5 2.4 %collective-permute-start.16 = (f32[48,128]{1,0:T(8,128)S(1)}, f32[48,128]{1,0:T(8,128)S(1)}, u32[]{:S(2)}, u32[]{:S(2)}) collective-permute-start(f32[48,128]{1,0:T(8,128)S(1)} %get-tuple-element.42), channel_id=1, source_target_pairs={{0,120},{1,7},{2,122},{3,1},{4,124},{5,3},{6,126},{7,5},{8,0},{9,1... | collective-permute-start | bytes 73736 | tf_op jit(solution)/shard_map/ppermute | solution.py:625
  123.9 1.2 collective-permute-done.15.refs_8_
  125.1 1.2 collective-permute-start.17
  126.2 0.0 collective-permute-done.16.refs_9_
  126.2 0.0 collective-permute-start.18
  126.3 0.8 collective-permute-done.17.refs_10_
  127.1 0.3 collective-permute-done.18.refs_11_
  127.4 0.0 collective-permute-done.14.refs_7_
  127.4 7.4 %shard_map.32 = f32[16,32,128]{2,1,0:T(8,128)} custom-call(f32[256,256]{1,0:T(8,128)S(1)} %copy-done, f32[40,80,128]{2,1,0:T(8,128)S(1)} %get-tuple-element.29.refs_1_, f32[40,80,128]{2,1,0:T(8,128)S(1)} %get-tuple-element.30.refs_2_, f32[20,48,128]{2,1,0:T(8,128)S(1)} %get-tuple-element.37.refs_3_, f32[20,48,128]{2,1,0:T(8,128)S(1)} %get-tuple-element.38.refs_4_, ...), custom_call_target="tpu_custom_call" | custom-call | flops 20000000 | bytes 1048576 | tf_op jit(solution)/shard_map/pallas_call | solution.py:566
  (1 shorter events, 0.0 us)
Async XLA Ops:
  0.0 80.0 %copy-start = (f32[256,256]{1,0:T(8,128)S(1)}, f32[256,256]{1,0:T(8,128)}, u32[]{:S(2)}) copy-start(f32[256,256]{1,0:T(8,128)} %constant.2.clone.refs_0_) | copy-start | bytes 786436
  0.0 1.0 copy-start.1
  1.3 27.0 %collective-permute-start = (f32[10,32,128]{2,1,0:T(8,128)S(1)}, f32[10,32,128]{2,1,0:T(8,128)S(1)}, u32[]{:S(2)}, u32[]{:S(2)}) collective-permute-start(f32[10,32,128]{2,1,0:T(8,128)S(1)} %get-tuple-element.25), channel_id=1, source_target_pairs={{0,8},{8,16},{16,24},{24,32},{32,40},{40,48},{48,56},{56,64},{64,7... | collective-permute-start | bytes 491528 | tf_op jit(solution)/shard_map/ppermute | solution.py:614
  4.7 23.6 %collective-permute-start.1 = (f32[10,32,128]{2,1,0:T(8,128)S(1)}, f32[10,32,128]{2,1,0:T(8,128)S(1)}, u32[]{:S(2)}, u32[]{:S(2)}) collective-permute-start(f32[10,32,128]{2,1,0:T(8,128)S(1)} %get-tuple-element.26), channel_id=1, source_target_pairs={{0,120},{8,0},{16,8},{24,16},{32,24},{40,32},{48,40},{56,48},{64,5... | collective-permute-start | bytes 491528 | tf_op jit(solution)/shard_map/ppermute | solution.py:614
  28.3 6.8 %collective-permute-start.2 = (f32[360,128]{1,0:T(8,128)S(1)}, f32[360,128]{1,0:T(8,128)S(1)}, u32[]{:S(2)}, u32[]{:S(2)}) collective-permute-start(f32[360,128]{1,0:T(8,128)S(1)} %get-tuple-element.27), channel_id=1, source_target_pairs={{0,2},{2,4},{4,6},{6,0},{1,3},{3,5},{5,7},{7,1},{8,10},{10,12},{12... | collective-permute-start | bytes 552968 | tf_op jit(solution)/shard_map/ppermute | solution.py:614
  29.8 7.1 %collective-permute-start.3 = (f32[360,128]{1,0:T(8,128)S(1)}, f32[360,128]{1,0:T(8,128)S(1)}, u32[]{:S(2)}, u32[]{:S(2)}) collective-permute-start(f32[360,128]{1,0:T(8,128)S(1)} %get-tuple-element.28), channel_id=1, source_target_pairs={{0,6},{2,0},{4,2},{6,4},{1,7},{3,1},{5,3},{7,5},{8,14},{10,8},{12,... | collective-permute-start | bytes 552968 | tf_op jit(solution)/shard_map/ppermute | solution.py:614
  31.5 6.0 %collective-permute-start.4 = (f32[16,32,128]{2,1,0:T(8,128)S(1)}, f32[16,32,128]{2,1,0:T(8,128)S(1)}, u32[]{:S(2)}, u32[]{:S(2)}) collective-permute-start(f32[16,32,128]{2,1,0:T(8,128)S(1)} %get-tuple-element.24.mine.refs_0_), channel_id=1, source_target_pairs={{0,1},{1,0},{2,3},{3,2},{4,5},{5,4},{6,7},{7,6},{8,9},{9,8},{10,11... | collective-permute-start | bytes 786440 | tf_op jit(solution)/shard_map/ppermute | solution.py:614
  35.1 3.7 %collective-permute-start.7 = (f32[360,128]{1,0:T(8,128)S(1)}, f32[360,128]{1,0:T(8,128)S(1)}, u32[]{:S(2)}, u32[]{:S(2)}) collective-permute-start(f32[360,128]{1,0:T(8,128)S(1)} %collective-permute-done.2.refs_3_), channel_id=1, source_target_pairs={{0,1},{1,0},{2,3},{3,2},{4,5},{5,4},{6,7},{7,6},{8,9},{9,8},{10,11... | collective-permute-start | bytes 552968 | tf_op jit(solution)/shard_map/ppermute | solution.py:614
  36.9 1.9 %collective-permute-start.8 = (f32[360,128]{1,0:T(8,128)S(1)}, f32[360,128]{1,0:T(8,128)S(1)}, u32[]{:S(2)}, u32[]{:S(2)}) collective-permute-start(f32[360,128]{1,0:T(8,128)S(1)} %collective-permute-done.3.refs_4_), channel_id=1, source_target_pairs={{0,1},{1,0},{2,3},{3,2},{4,5},{5,4},{6,7},{7,6},{8,9},{9,8},{10,11... | collective-permute-start | bytes 552968 | tf_op jit(solution)/shard_map/ppermute | solution.py:614
  36.9 1.7 %collective-permute-start.5 = (f32[10,32,128]{2,1,0:T(8,128)S(1)}, f32[10,32,128]{2,1,0:T(8,128)S(1)}, u32[]{:S(2)}, u32[]{:S(2)}) collective-permute-start(f32[10,32,128]{2,1,0:T(8,128)S(1)} %collective-permute-done.x_low.refs_1_), channel_id=1, source_target_pairs={{0,1},{1,0},{2,3},{3,2},{4,5},{5,4},{6,7},{7,6},{8,9},{9,8},{10,11... | collective-permute-start | bytes 491528 | tf_op jit(solution)/shard_map/ppermute | solution.py:614
  37.4 1.4 %collective-permute-start.6 = (f32[10,32,128]{2,1,0:T(8,128)S(1)}, f32[10,32,128]{2,1,0:T(8,128)S(1)}, u32[]{:S(2)}, u32[]{:S(2)}) collective-permute-start(f32[10,32,128]{2,1,0:T(8,128)S(1)} %collective-permute-done.1.x_high.refs_2_), channel_id=1, source_target_pairs={{0,1},{1,0},{2,3},{3,2},{4,5},{5,4},{6,7},{7,6},{8,9},{9,8},{10,11... | collective-permute-start | bytes 491528 | tf_op jit(solution)/shard_map/ppermute | solution.py:614
  69.7 10.3 %collective-permute-start.9 = (f32[64,8,128]{2,1,0:T(8,128)S(1)}, f32[64,8,128]{2,1,0:T(8,128)S(1)}, u32[]{:S(2)}, u32[]{:S(2)}) collective-permute-start(f32[64,8,128]{2,1,0:T(8,128)S(1)} %all_to_all.10.refs_6_), channel_id=1, source_target_pairs={{0,1},{1,0},{2,3},{3,2},{4,5},{5,4},{6,7},{7,6},{8,9},{9,8},{10,11... | collective-permute-start | bytes 786440 | tf_op jit(solution)/shard_map/ppermute | solution.py:614
  73.5 4.4 %collective-permute-start.10 = (f32[96,128]{1,0:T(8,128)S(1)}, f32[96,128]{1,0:T(8,128)S(1)}, u32[]{:S(2)}, u32[]{:S(2)}) collective-permute-start(f32[96,128]{1,0:T(8,128)S(1)} %get-tuple-element.35), channel_id=1, source_target_pairs={{0,8},{1,3},{2,10},{3,5},{4,12},{5,7},{6,14},{7,1},{8,16},{9,11},{... | collective-permute-start | bytes 147464 | tf_op jit(solution)/shard_map/ppermute | solution.py:625
  73.7 5.1 %collective-permute-start.11 = (f32[96,128]{1,0:T(8,128)S(1)}, f32[96,128]{1,0:T(8,128)S(1)}, u32[]{:S(2)}, u32[]{:S(2)}) collective-permute-start(f32[96,128]{1,0:T(8,128)S(1)} %get-tuple-element.36), channel_id=1, source_target_pairs={{0,120},{1,7},{2,122},{3,1},{4,124},{5,3},{6,126},{7,5},{8,0},{9,1... | collective-permute-start | bytes 147464 | tf_op jit(solution)/shard_map/ppermute | solution.py:625
  77.9 1.7 %collective-permute-start.12 = (f32[96,128]{1,0:T(8,128)S(1)}, f32[96,128]{1,0:T(8,128)S(1)}, u32[]{:S(2)}, u32[]{:S(2)}) collective-permute-start(f32[96,128]{1,0:T(8,128)S(1)} %collective-permute-done.10.refs_8_), channel_id=1, source_target_pairs={{0,1},{1,0},{2,3},{3,2},{4,5},{5,4},{6,7},{7,6},{8,9},{9,8},{10,11... | collective-permute-start | bytes 147464 | tf_op jit(solution)/shard_map/ppermute | solution.py:614
  78.8 1.2 collective-permute-start.13
  117.2 10.3 %collective-permute-start.14 = (f32[64,8,128]{2,1,0:T(8,128)S(1)}, f32[64,8,128]{2,1,0:T(8,128)S(1)}, u32[]{:S(2)}, u32[]{:S(2)}) collective-permute-start(f32[64,8,128]{2,1,0:T(8,128)S(1)} %all_to_all.11.refs_6_), channel_id=1, source_target_pairs={{0,1},{1,0},{2,3},{3,2},{4,5},{5,4},{6,7},{7,6},{8,9},{9,8},{10,11... | collective-permute-start | bytes 786440 | tf_op jit(solution)/shard_map/ppermute | solution.py:614
  121.2 3.9 %collective-permute-start.15 = (f32[48,128]{1,0:T(8,128)S(1)}, f32[48,128]{1,0:T(8,128)S(1)}, u32[]{:S(2)}, u32[]{:S(2)}) collective-permute-start(f32[48,128]{1,0:T(8,128)S(1)} %get-tuple-element.41), channel_id=1, source_target_pairs={{0,8},{1,3},{2,10},{3,5},{4,12},{5,7},{6,14},{7,1},{8,16},{9,11},{... | collective-permute-start | bytes 73736 | tf_op jit(solution)/shard_map/ppermute | solution.py:625
  121.5 4.8 %collective-permute-start.16 = (f32[48,128]{1,0:T(8,128)S(1)}, f32[48,128]{1,0:T(8,128)S(1)}, u32[]{:S(2)}, u32[]{:S(2)}) collective-permute-start(f32[48,128]{1,0:T(8,128)S(1)} %get-tuple-element.42), channel_id=1, source_target_pairs={{0,120},{1,7},{2,122},{3,1},{4,124},{5,3},{6,126},{7,5},{8,0},{9,1... | collective-permute-start | bytes 73736 | tf_op jit(solution)/shard_map/ppermute | solution.py:625
  125.1 2.0 %collective-permute-start.17 = (f32[48,128]{1,0:T(8,128)S(1)}, f32[48,128]{1,0:T(8,128)S(1)}, u32[]{:S(2)}, u32[]{:S(2)}) collective-permute-start(f32[48,128]{1,0:T(8,128)S(1)} %collective-permute-done.15.refs_8_), channel_id=1, source_target_pairs={{0,1},{1,0},{2,3},{3,2},{4,5},{5,4},{6,7},{7,6},{8,9},{9,8},{10,11... | collective-permute-start | bytes 73736 | tf_op jit(solution)/shard_map/ppermute | solution.py:614
  126.2 1.2 collective-permute-start.18

commit v2 on v1

--- a/solution.py
+++ b/solution.py
@@ -117,7 +117,7 @@
             t0[q, pl.ds(j - Y0 + 8, 16), :] = total
 
     layers = BX // 2 + 2 * halo
-    over_layers(0, layers, 4, body)
+    over_layers(0, layers, layers // 2, body)
     for m in range(layers):
         f1[X1 - halo + m, pl.ds(Y1 - 4, 24), :] = 0.125 * (t0[m, pl.ds(0, 24, stride=2), :] + t0[m, pl.ds(1, 24, stride=2), :])
 
@@ -189,34 +189,51 @@
         out[s] = packed
 
 
-def across(v):
-    n, rows = v.shape[0], v.shape[1]
-    up = jnp.concatenate([v[n - 1 :], v[: n - 1]], axis=0)
-    down = jnp.concatenate([v[1:], v[:1]], axis=0)
+def turned(v, step, n):
+    axis = v.ndim - 1
+    moved = pltpu.roll(v, step % LANES, axis)
+    if n == LANES:
+        return moved
+    lane = lax.rem(iota(v.shape, axis), n)
+    wrapped = pltpu.roll(v, (step - n if step > 0 else step + n) % LANES, axis)
+    return jnp.where(lane < step if step > 0 else lane >= n + step, wrapped, moved)
+
+
+def along_z(v, step, n):
+    return turned(v, step, n) + turned(v, -step, n)
+
+
+def next_segment(v, n):
+    return pltpu.roll(v, n % LANES, v.ndim - 1)
+
+
+def across(v, n):
+    last, rows = v.shape[0] - 1, v.shape[1]
+    up = jnp.concatenate([next_segment(v[last:], n), v[:last]], axis=0)
+    down = jnp.concatenate([v[1:], next_segment(v[:1], -n)], axis=0)
     return (up + down) + (pltpu.roll(v, 1, 1) + pltpu.roll(v, rows - 1, 1))
 
 
-def applied(level, v):
+def applied(level, v, n):
     a, _ = coefficients(level)
-    z1 = pltpu.roll(v, 1, 2) + pltpu.roll(v, LANES - 1, 2)
-    z2 = pltpu.roll(v, 2, 2) + pltpu.roll(v, LANES - 2, 2)
-    one = across(v)
+    z1, z2 = along_z(v, 1, n), along_z(v, 2, n)
+    one = across(v, n)
     sv = one + z1
-    ssv = across(one + 2.0 * z1) + (z2 + 2.0 * v)
+    ssv = across(one + 2.0 * z1, n) + (z2 + 2.0 * v)
     t = 6.0 * v - sv
     tt = 6.0 * t - (6.0 * sv - ssv)
     return t, a * t + SCREEN * v, (a * a) * tt + (2.0 * a * SCREEN) * t + (SCREEN * SCREEN) * v
 
 
-def start_whole(level, f):
+def start_whole(level, f, n=LANES):
     a, k = coefficients(level)
-    t, af, aaf = applied(level, f)
+    t, af, aaf = applied(level, f, n)
     return (2.0 * k - k * k * SCREEN) * f - (k * k * a) * t, f - 2.0 * k * af + (k * k) * aaf, af
 
 
-def smooth_whole(level, f, af, v):
+def smooth_whole(level, f, af, v, n=LANES):
     a, k = coefficients(level)
-    t, _, aav = applied(level, v)
+    t, _, aav = applied(level, v, n)
     r = (f - a * t) - SCREEN * v
     return v + 2.0 * k * r - (k * k) * (af - aav)
 
@@ -243,11 +260,6 @@
 
     cells = shape[0] * shape[1] * shape[2]
     return cycle(5, np.eye(cells).reshape(cells, *shape)).reshape(cells, cells).astype(np.float32)
-
-
-def down_z(level):
-    n = sizes_2()[2] >> (level - 1)
-    return mean_matrix(lambda o: 2 * lax.rem(o, n))
 
 
 def up_z(level):
@@ -289,87 +301,117 @@
 
 
 def solve_3(f3, t3, matrix):
-    x4, y4 = f3.shape[0] // 2, f3.shape[1] // 2
-    v3, r3, af3 = start_whole(3, f3)
+    n, x3, y4 = sizes_2()[2] // 2, f3.shape[0], f3.shape[1] // 2
+    segments, x4 = LANES // n, x3 // 2
+    v3, r3, af3 = start_whole(3, f3, n)
     t3[...] = pair_layers(r3)
-    s = t3[:, pl.ds(0, y4, stride=2), :] + t3[:, pl.ds(1, y4, stride=2), :]
-    f4 = dot(flat(s), down_z(3)).reshape(x4, y4, LANES)
+    s = flat(t3[:, pl.ds(0, y4, stride=2), :] + t3[:, pl.ds(1, y4, stride=2), :])
+    means = [mean_matrix(lambda o: n * q + 2 * lax.rem(o, n // 2)) for q in range(segments)]
+    f4 = jnp.concatenate([dot(s, m).reshape(x4, y4, LANES) for m in means], axis=0)
     v4, r4, af4 = start_whole(4, f4)
-    e4 = solve_bottom(flat(pair_layers(r4)), bottom_shape(), matrix).reshape(x4 // 2, y4, LANES)
+    e4 = solve_bottom(flat(pair_layers(r4)), bottom_shape(), matrix).reshape(-1, y4, LANES)
     v4 = smooth_whole(4, f4, af4, v4 + twice(e4))
-    e3 = dot(flat(v4), up_z(3)).reshape(x4, y4, LANES)
+    picks = [pick_matrix(lambda o: jnp.where(o // n == q, lax.rem(o, n) // 2, -1)) for q in range(segments)]
+    e3 = sum(dot(flat(v4[x4 * q : x4 * (q + 1)]), m) for q, m in enumerate(picks)).reshape(x4, y4, LANES)
     t3[:, pl.ds(0, y4, stride=2), :] = e3
     t3[:, pl.ds(1, y4, stride=2), :] = e3
-    return smooth_whole(3, f3, af3, v3 + twice(t3[...]))
+    return smooth_whole(3, f3, af3, v3 + twice(t3[...]), n)
 
 
 def unpack_2(f2, mine, other, core):
     low = iota((8, LANES), 1) < 64
     top = iota((8, LANES), 0) < 4
     along_y = lax.axis_size("gy")
+    half = (f2.shape[0] - 2) // 4
 
     def body(gx):
         for gy in range(along_y):
-            t, p = mine[gx * along_y + gy], other[gx * along_y + gy]
-            u, w = jnp.where(core == 0, t, p), jnp.where(core == 0, p, t)
-            ur, wr = pltpu.roll(u, 64, 1), pltpu.roll(w, 64, 1)
+            tiles = []
+            for g in (gx, gx + half):
+                t, p = mine[g * along_y + gy], other[g * along_y + gy]
+                u, w = jnp.where(core == 0, t, p), jnp.where(core == 0, p, t)
+                tiles.append((u, w))
+            (u, w), (u2, w2) = tiles
             for xp in range(2):
-                d = jnp.where(low, u, ur) if xp == 0 else jnp.where(low, ur, u)
-                e = jnp.where(low, w, wr) if xp == 0 else jnp.where(low, wr, w)
-                f2[gx * 4 + 2 * xp, pl.ds(gy * 8, 8), :] = jnp.where(top, d, pltpu.roll(e, 4, 0))
-                f2[gx * 4 + 2 * xp + 1, pl.ds(gy * 8, 8), :] = jnp.where(top, pltpu.roll(d, 4, 0), e)
-
-    over_layers(0, f2.shape[0] // 4, 4, body)
-
-
-def beside_2(centre, before, after):
+                if xp == 0:
+                    d, e = jnp.where(low, u, pltpu.roll(u2, 64, 1)), jnp.where(low, w, pltpu.roll(w2, 64, 1))
+                else:
+                    d, e = jnp.where(low, pltpu.roll(u, 64, 1), u2), jnp.where(low, pltpu.roll(w, 64, 1), w2)
+                f2[1 + gx * 4 + 2 * xp, pl.ds(gy * 8, 8), :] = jnp.where(top, d, pltpu.roll(e, 4, 0))
+                f2[2 + gx * 4 + 2 * xp, pl.ds(gy * 8, 8), :] = jnp.where(top, pltpu.roll(d, 4, 0), e)
+
+    over_layers(0, half, 4, body)
+
+
+def close_2(v):
+    last = v.shape[0] - 2
+    v[0] = next_segment(v[last], 64)
+    v[last + 1] = next_segment(v[1], -64)
+
+
+def beside_2(centre, before, after, n):
     rows = centre.shape[0]
     return (
-        (before + after)
-        + (pltpu.roll(centre, 1, 0) + pltpu.roll(centre, rows - 1, 0))
-        + (pltpu.roll(centre, 1, 1) + pltpu.roll(centre, LANES - 1, 1))
+        (before + after) + (pltpu.roll(centre, 1, 0) + pltpu.roll(centre, rows - 1, 0)) + along_z(centre, 1, n)
     )
 
 
-def level_2(near, f2, v2, t2, t3, s3, p2, a2, b2, matrix, fetch, gx, halo):
-    n, rows = f2.shape[0], f2.shape[1]
-
-    def around(ref, i):
-        return ref[i], ref[lax.rem(i + n - 1, n)], ref[lax.rem(i + 1, n)]
+def level_2(near, f2, v2, t2, t3, s3, p2, a2, b2, bottom, gx, halo):
+    n, rows, length = f2.shape[0] - 2, f2.shape[1], sizes_2()[2]
+    close_2(f2)
 
     def first(i):
-        centre, before, after = around(f2, i)
-        v2[i] = twice_from_zero(2, centre, beside_2(centre, before, after))
-
-    over_layers(0, n, 16, first)
+        v2[i] = twice_from_zero(2, f2[i], beside_2(f2[i], f2[i - 1], f2[i + 1], length))
+
+    over_layers(1, n, 16, first)
+    close_2(v2)
 
     def second(q):
         pair = []
-        for i in (2 * q, 2 * q + 1):
-            centre, before, after = around(v2, i)
-            pair.append(residual_of(2, f2[i], centre, beside_2(centre, before, after)))
+        for i in (2 * q + 1, 2 * q + 2):
+            pair.append(residual_of(2, f2[i], v2[i], beside_2(v2[i], v2[i - 1], v2[i + 1], length)))
         t2[q] = pair[0] + pair[1]
 
     over_layers(0, n // 2, 8, second)
     s = t2[:, pl.ds(0, rows // 2, stride=2), :] + t2[:, pl.ds(1, rows // 2, stride=2), :]
-    f3 = dot(flat(s), down_z(2)).reshape(n // 2, rows // 2, LANES)
-    fetch.wait()
-    s3[...] = solve_3(f3, t3, matrix)
+    x3 = n // 4
+
+    def means(part):
+        def source(o):
+            q = o // (length // 2)
+            return jnp.where(lax.rem(q, 2) == part, q // 2 * length + 2 * lax.rem(o, length // 2), -2)
+
+        return mean_matrix(source)
+
+    f3 = dot(flat(s[:x3]), means(0)) + dot(flat(s[x3:]), means(1))
+    s3[...] = solve_3(f3.reshape(x3, rows // 2, LANES), t3, bottom)
 
     count = 4 + 2 * halo + 4
-    start = gx * 4 - halo - 2 + n
-    e = jnp.concatenate([s3[lax.rem(lax.div(start, 2) + m, n // 2)] for m in range(count // 2)], axis=0)
-    e = dot(e, up_z(2)).reshape(count // 2, rows // 2, LANES)
+    start = gx * 4 - halo - 2 + 2 * n
+    lines = []
+    for m in range(count // 2):
+        at = lax.rem(lax.div(start, 2) + m, n)
+        line = s3[lax.rem(at, x3)]
+        lines.append(pltpu.roll(line, lax.rem(LANES - length // 2 * lax.div(at, x3), LANES), 1))
+    e = dot(jnp.concatenate(lines, axis=0), up_z(2)).reshape(count // 2, rows // 2, LANES)
     p2[pl.ds(0, count // 2), pl.ds(0, rows // 2, stride=2), :] = e
     p2[pl.ds(0, count // 2), pl.ds(1, rows // 2, stride=2), :] = e
+    low = iota((rows, LANES), 1) < 64
     for m in range(count):
-        a2[m] = v2[lax.rem(start + m, n)] + p2[m // 2]
+        at = lax.rem(start + m, 2 * n)
+        i, lower = 1 + lax.rem(at, n), at < n
+        whole = []
+        for ref in (v2, f2):
+            turned_half = pltpu.roll(ref[i], 64, 1)
+            whole.append(jnp.where(low, jnp.where(lower, ref[i], turned_half), jnp.where(lower, turned_half, ref[i])))
+        a2[m] = whole[0] + p2[m // 2]
+        t2[m] = whole[1]
     for m in range(1, count - 1):
-        nb = beside_2(a2[m], a2[m - 1], a2[m + 1])
-        b2[m] = relaxed(2, f2[lax.rem(start + m, n)], a2[m], nb)
+        nb = beside_2(a2[m], a2[m - 1], a2[m + 1], LANES)
+        b2[m] = relaxed(2, t2[m], a2[m], nb)
     for m in range(2, count - 2):
-        nb = beside_2(b2[m], b2[m - 1], b2[m + 1])
-        near[m - 2] = relaxed(2, f2[lax.rem(start + m, n)], b2[m], nb)
+        nb = beside_2(b2[m], b2[m - 1], b2[m + 1], LANES)
+        near[m - 2] = relaxed(2, t2[m], b2[m], nb)
 
 
 def add_from_2(v1, near, y2, p1, gy, core, halo):
@@ -478,7 +520,7 @@
     core = where()[2]
     force, v = (f_e, f_o), (v_e, v_o)
     lay_out_0(f_e, f_o, ours, others)
-    start_0(v, force, 9, 7)
+    start_0(v, force, 9, 17)
     restrict_0(f1, t0, v, force, 4)
     coarse_source(send, f1, v1, r1, core)
     put_out_1(*f1_outs, f1, core, 4, 4)
@@ -487,23 +529,21 @@
 def middle_kernel(where, *refs):
     bottom, f_e, f_o, v_e, v_o, f1_in, mine, other, *edges = refs[:12]
     (n_e, n_o, send), f1_outs = refs[12:15], refs[15:18]
-    a_e, a_o, b_e, b_o, f1, v1, r1, p1, y2, p0, t0, f2, v2, t2, t3, s3, p2, a2, b2, near, matrix, arrived = refs[18:]
-    fetch = pltpu.make_async_copy(bottom, matrix, arrived)
-    fetch.start()
+    a_e, a_o, b_e, b_o, f1, v1, r1, p1, y2, p0, t0, f2, v2, t2, t3, s3, p2, a2, b2, near = refs[18:]
     gx, gy, core = where()
     force, v, a0, b0 = (f_e, f_o), (v_e, v_o), (a_e, a_o), (b_e, b_o)
     unpack_2(f2, mine, other, core)
-    level_2(near, f2, v2, t2, t3, s3, p2, a2, b2, matrix, fetch, gx, 4)
+    level_2(near, f2, v2, t2, t3, s3, p2, a2, b2, bottom, gx, 4)
     lay_out_1(f1, f1_in, edges, core, 4, 4)
     start_1(v1, f1, 7, 12)
     add_from_2(v1, near, y2, p1, gy, core, 4)
     sweep_1(r1, v1, f1, 6, 12)
     sweep_1(v1, r1, f1, 5, 9)
     add_from_1(a0, v, v1, p0, 5, X0, Y0 - 16, 16, 64)
-    sweep_0(b0, a0, force, 8, 8)
-    sweep_0(a0, b0, force, 7, 8)
-    sweep_0(b0, a0, force, 6, 7)
-    sweep_0(a0, b0, force, 5, 7)
+    sweep_0(b0, a0, force, 8, 16)
+    sweep_0(a0, b0, force, 7, 15)
+    sweep_0(b0, a0, force, 6, 14)
+    sweep_0(a0, b0, force, 5, 13)
     restrict_0(f1, t0, a0, force, 2)
     coarse_source(send, f1, v1, r1, core)
     put_out_1(*f1_outs, f1, core, 2, 2)
@@ -513,30 +553,32 @@
 
 def last_kernel(where, *refs):
     bottom, f_e, f_o, n_e, n_o, f1_in, mine, other, *edges = refs[:12]
-    out, a_e, a_o, b_e, b_o, f1, v1, r1, p1, y2, p0, _, f2, v2, t2, t3, s3, p2, a2, b2, near, matrix, arrived = refs[12:]
-    fetch = pltpu.make_async_copy(bottom, matrix, arrived)
-    fetch.start()
+    out, a_e, a_o, b_e, b_o, f1, v1, r1, p1, y2, p0, _, f2, v2, t2, t3, s3, p2, a2, b2, near, held, left = refs[12:]
     gx, gy, core = where()
     force, v, a0, b0 = (f_e, f_o), (n_e, n_o), (a_e, a_o), (b_e, b_o)
     unpack_2(f2, mine, other, core)
-    level_2(near, f2, v2, t2, t3, s3, p2, a2, b2, matrix, fetch, gx, 2)
+    level_2(near, f2, v2, t2, t3, s3, p2, a2, b2, bottom, gx, 2)
     lay_out_1(f1, f1_in, edges, core, 2, 2)
     start_1(v1, f1, 3, 14)
     add_from_2(v1, near, y2, p1, gy, core, 2)
     sweep_1(r1, v1, f1, 2, 12)
     sweep_1(v1, r1, f1, 1, 10)
     add_from_1(a0, v, v1, p0, 1, 2, 0, 8, 48)
-    sweep_0(b0, a0, force, 1, 6)
+    sweep_0(b0, a0, force, 1, 9)
     low = iota((BY, LANES), 1) < 64
-
-    def body(i):
-        centre, nb = beside_0(b0, i, Y0, BY)
-        even, odd = (relaxed(0, force[h][i, pl.ds(Y0, BY), :], centre[h], nb[h]) for h in range(2))
-        p0[i - X0, pl.ds(0, BY), :] = jnp.where(low, even, pltpu.roll(odd, 64, 1))
-
-    over_layers(X0, BX, 8, body)
     matrix = pick_matrix(lambda o: lax.div(o, 2) + 64 * lax.rem(o, 2))
-    out[...] = dot(flat(p0[pl.ds(0, BX), pl.ds(0, BY), :]), matrix).reshape(BX, BY, LANES)
+    pieces = [pl.ds(4 * k, 4) for k in range(BX // 4)]
+    stores = [pltpu.make_async_copy(held.at[p], out.at[p], left.at[k]) for k, p in enumerate(pieces)]
+    for k, store in enumerate(stores):
+        lines = []
+        for i in range(X0 + 4 * k, X0 + 4 * k + 4):
+            centre, nb = beside_0(b0, i, Y0, BY)
+            even, odd = (relaxed(0, force[h][i, pl.ds(Y0, BY), :], centre[h], nb[h]) for h in range(2))
+            lines.append(jnp.where(low, even, pltpu.roll(odd, 64, 1)))
+        held[pieces[k]] = dot(jnp.concatenate(lines, axis=0), matrix).reshape(4, BY, LANES)
+        store.start()
+    for store in stores:
+        store.wait()
 
 
 def vm(*shape):
@@ -549,24 +591,23 @@
 
 def scratch_for_cycle():
     x2, y2, _ = sizes_2()
-    cells = int(np.prod(bottom_shape()))
     return (
         [vm(XA0, YA0, LANES)] * 4
         + [vm(XA1, YA1, LANES)] * 3
         + [vm(12, y2, LANES), vm(12, 2 * y2, LANES), vm(20, 64, LANES), vm(16, 48, LANES)]
-        + [vm(x2, y2, LANES)] * 2
-        + [vm(x2 // 2, y2, LANES), vm(x2 // 4, y2 // 2, LANES), vm(x2 // 2, y2 // 2, LANES), vm(8, y2, LANES)]
+        + [vm(x2 // 2 + 2, y2, LANES)] * 2
+        + [vm(16, y2, LANES), vm(x2 // 16, y2 // 2, LANES), vm(x2 // 8, y2 // 2, LANES), vm(8, y2, LANES)]
         + [vm(16, y2, LANES)] * 2
-        + [vm(12, y2, LANES), vm(cells, cells), pltpu.SemaphoreType.DMA(())]
+        + [vm(12, y2, LANES)]
     )
 
 
-def run(kernel, outs, scratch, flops, *args, fetched=0):
-    spaces = [pltpu.HBM] * fetched + [pltpu.VMEM] * (len(args) - fetched)
+def run(kernel, outs, scratch, flops, *args, out_space=pltpu.VMEM):
+    spec = pl.BlockSpec(memory_space=out_space)
     return pl.pallas_call(
         kernel,
-        in_specs=[pl.BlockSpec(memory_space=space) for space in spaces],
         out_shape=outs,
+        out_specs=[spec] * len(outs) if isinstance(outs, list) else spec,
         scratch_shapes=scratch,
         compiler_params=pltpu.CompilerParams(vmem_limit_bytes=40 * 2**20),
         cost_estimate=pl.CostEstimate(flops=flops, bytes_accessed=2**20, transcendentals=0),
@@ -601,12 +642,13 @@
 
 def middle(*args):
     outs = [kept(20, 48, LANES)] * 2 + sources_out(12, 2)
-    return run(functools.partial(middle_kernel, where_am_i), outs, scratch_for_cycle(), 4 * 10**7, *args, fetched=1)
+    return run(functools.partial(middle_kernel, where_am_i), outs, scratch_for_cycle(), 4 * 10**7, *args)
 
 
 def last(*args):
     outs = kept(BX, BY, LANES)
-    return run(functools.partial(last_kernel, where_am_i), outs, scratch_for_cycle(), 2 * 10**7, *args, fetched=1)
+    scratch = scratch_for_cycle() + [vm(BX, BY, LANES), pltpu.SemaphoreType.DMA((BX // 4,))]
+    return run(functools.partial(last_kernel, where_am_i), outs, scratch, 2 * 10**7, *args, out_space=pltpu.HBM)
 
 
 def from_(value, axis, step):

time: 135 us -> 133 us (0.985)
  Pallas kernels: 21.5 us -> 19.2 us
    pallas_call x5, Pallas kernels: 21.5 us -> 19.2 us  [run(): pl.pallas_call(kernel, out_shape=outs, out_specs=[spec] * len(outs) if is...]
where the time goes in v2:
time: 133 us
  blocking collectives  54.2 us (41%)
  starting transfers between devices  45.3 us (34%)
  Pallas kernels  19.2 us (14%)
  waiting for transfers between devices  12.8 us (10%)
    all_to_all x2, blocking collectives, exchange(): mine = lax.all_to_all(send, ('gx', 'gy'), 0, 0, tiled=True)  54.2 us
    ppermute x15, starting transfers between devices, from_(): lax.ppermute(value, axis, [(i, (i + step) % size) for i in range(size)])  39.9 us
    pallas_call x5, Pallas kernels, run(): pl.pallas_call(kernel, out_shape=outs, out_specs=[spec] * len(outs) if is...  19.2 us
    ppermute x15, waiting for transfers between devices, from_(): lax.ppermute(value, axis, [(i, (i + step) % size) for i in range(size)])  9.86 us
    ppermute x4, starting transfers between devices, beside_(): return lax.ppermute(value, axes, pairs)  5.35 us
    ppermute x4, waiting for transfers between devices, beside_(): return lax.ppermute(value, axes, pairs)  2.98 us
  transfers between devices with their start and end apart: 19, of which 10 were waited for; matrix products, arithmetic and copies ran while one was open for 0% of the time, Pallas kernels for 0%

profile of v2, /device:TPU:33, one launch (start us, length us, event | category | flops | bytes accessed | tf_op | source)
XLA Modules:
  0.0 132.7 jit_solution(13454182751673692539)
XLA Ops:
  0.0 0.0 copy-start
  0.0 0.0 copy-start.1
  0.0 1.0 copy-done.1
  1.0 0.3 shard_map.28
  1.3 3.4 %collective-permute-start = (f32[10,32,128]{2,1,0:T(8,128)S(1)}, f32[10,32,128]{2,1,0:T(8,128)S(1)}, u32[]{:S(2)}, u32[]{:S(2)}) collective-permute-start(f32[10,32,128]{2,1,0:T(8,128)S(1)} %get-tuple-element.25), channel_id=1, source_target_pairs={{0,8},{8,16},{16,24},{24,32},{32,40},{40,48},{48,56},{56,64},{64,7... | collective-permute-start | bytes 491528 | tf_op jit(solution)/shard_map/ppermute | solution.py:656
  4.7 19.7 %collective-permute-start.1 = (f32[10,32,128]{2,1,0:T(8,128)S(1)}, f32[10,32,128]{2,1,0:T(8,128)S(1)}, u32[]{:S(2)}, u32[]{:S(2)}) collective-permute-start(f32[10,32,128]{2,1,0:T(8,128)S(1)} %get-tuple-element.26), channel_id=1, source_target_pairs={{0,120},{8,0},{16,8},{24,16},{32,24},{40,32},{48,40},{56,48},{64,5... | collective-permute-start | bytes 491528 | tf_op jit(solution)/shard_map/ppermute | solution.py:656
  24.4 3.8 %collective-permute-done.x_low.refs_1_ = f32[10,32,128]{2,1,0:T(8,128)S(1)} collective-permute-done((f32[10,32,128]{2,1,0:T(8,128)S(1)}, f32[10,32,128]{2,1,0:T(8,128)S(1)}, u32[]{:S(2)}, u32[]{:S(2)}) %collective-permute-start) | collective-permute-done | bytes 163872 | tf_op jit(solution)/shard_map/ppermute | solution.py:656
  28.3 0.0 collective-permute-done.1.x_high.refs_2_
  28.3 1.5 %collective-permute-start.2 = (f32[360,128]{1,0:T(8,128)S(1)}, f32[360,128]{1,0:T(8,128)S(1)}, u32[]{:S(2)}, u32[]{:S(2)}) collective-permute-start(f32[360,128]{1,0:T(8,128)S(1)} %get-tuple-element.27), channel_id=1, source_target_pairs={{0,2},{2,4},{4,6},{6,0},{1,3},{3,5},{5,7},{7,1},{8,10},{10,12},{12... | collective-permute-start | bytes 552968 | tf_op jit(solution)/shard_map/ppermute | solution.py:656
  29.8 1.7 %collective-permute-start.3 = (f32[360,128]{1,0:T(8,128)S(1)}, f32[360,128]{1,0:T(8,128)S(1)}, u32[]{:S(2)}, u32[]{:S(2)}) collective-permute-start(f32[360,128]{1,0:T(8,128)S(1)} %get-tuple-element.28), channel_id=1, source_target_pairs={{0,6},{2,0},{4,2},{6,4},{1,7},{3,1},{5,3},{7,5},{8,14},{10,8},{12,... | collective-permute-start | bytes 552968 | tf_op jit(solution)/shard_map/ppermute | solution.py:656
  31.5 1.5 %collective-permute-start.4 = (f32[16,32,128]{2,1,0:T(8,128)S(1)}, f32[16,32,128]{2,1,0:T(8,128)S(1)}, u32[]{:S(2)}, u32[]{:S(2)}) collective-permute-start(f32[16,32,128]{2,1,0:T(8,128)S(1)} %get-tuple-element.24.mine.refs_0_), channel_id=1, source_target_pairs={{0,1},{1,0},{2,3},{3,2},{4,5},{5,4},{6,7},{7,6},{8,9},{9,8},{10,11... | collective-permute-start | bytes 786440 | tf_op jit(solution)/shard_map/ppermute | solution.py:656
  32.9 2.2 %collective-permute-done.2.refs_3_ = f32[360,128]{1,0:T(8,128)S(1)} collective-permute-done((f32[360,128]{1,0:T(8,128)S(1)}, f32[360,128]{1,0:T(8,128)S(1)}, u32[]{:S(2)}, u32[]{:S(2)}) %collective-permute-start.2) | collective-permute-done | bytes 184352 | tf_op jit(solution)/shard_map/ppermute | solution.py:656
  35.1 1.8 %collective-permute-start.7 = (f32[360,128]{1,0:T(8,128)S(1)}, f32[360,128]{1,0:T(8,128)S(1)}, u32[]{:S(2)}, u32[]{:S(2)}) collective-permute-start(f32[360,128]{1,0:T(8,128)S(1)} %collective-permute-done.2.refs_3_), channel_id=1, source_target_pairs={{0,1},{1,0},{2,3},{3,2},{4,5},{5,4},{6,7},{7,6},{8,9},{9,8},{10,11... | collective-permute-start | bytes 552968 | tf_op jit(solution)/shard_map/ppermute | solution.py:656
  36.9 0.0 collective-permute-done.3.refs_4_
  36.9 0.0 collective-permute-start.8
  36.9 0.5 collective-permute-start.5
  37.4 0.0 collective-permute-start.6
  37.4 0.0 collective-permute-done.4.refs_5_
  37.4 1.1 collective-permute-done.5.refs_6_
  38.6 0.2 collective-permute-done.6.refs_7_
  38.8 0.0 collective-permute-done.7.refs_8_
  38.8 0.0 collective-permute-done.8.refs_9_
  38.8 2.6 %shard_map.30 = (f32[40,80,128]{2,1,0:T(8,128)S(1)}, f32[40,80,128]{2,1,0:T(8,128)S(1)}, f32[40,80,128]{2,1,0:T(8,128)S(1)}, f32[40,80,128]{2,1,0:T(8,128)S(1)},...) custom-call(f32[16,32,128]{2,1,0:T(8,128)S(1)} %get-tuple-element.24.min, ...), custom_call_target="tpu_custom_call" | custom-call | flops 10000000 | bytes 1048576 | tf_op jit(solution)/shard_map/pallas_call | solution.py:607
  41.5 27.9 %all_to_all.10.refs_6_ = f32[64,8,128]{2,1,0:T(8,128)S(1)} all-to-all(f32[64,8,128]{2,1,0:T(8,128)S(1)} %get-tuple-element.34), channel_id=1, replica_groups=mesh['groups'=2,'gx'=16,'gy'=4,'gz'=2] {'gx','gy'}, dimensions={0} | all-to-all | bytes 524288 | tf_op jit(solution)/shard_map/all_to_all | solution.py:672
  69.4 3.7 %collective-permute-start.9 = (f32[64,8,128]{2,1,0:T(8,128)S(1)}, f32[64,8,128]{2,1,0:T(8,128)S(1)}, u32[]{:S(2)}, u32[]{:S(2)}) collective-permute-start(f32[64,8,128]{2,1,0:T(8,128)S(1)} %all_to_all.10.refs_6_), channel_id=1, source_target_pairs={{0,1},{1,0},{2,3},{3,2},{4,5},{5,4},{6,7},{7,6},{8,9},{9,8},{10,11... | collective-permute-start | bytes 786440 | tf_op jit(solution)/shard_map/ppermute | solution.py:656
  73.1 0.2 collective-permute-start.10
  73.4 2.4 %collective-permute-start.11 = (f32[96,128]{1,0:T(8,128)S(1)}, f32[96,128]{1,0:T(8,128)S(1)}, u32[]{:S(2)}, u32[]{:S(2)}) collective-permute-start(f32[96,128]{1,0:T(8,128)S(1)} %get-tuple-element.36), channel_id=1, source_target_pairs={{0,120},{1,7},{2,122},{3,1},{4,124},{5,3},{6,126},{7,5},{8,0},{9,1... | collective-permute-start | bytes 147464 | tf_op jit(solution)/shard_map/ppermute | solution.py:667
  75.8 1.8 %collective-permute-done.10.refs_8_ = f32[96,128]{1,0:T(8,128)S(1)} collective-permute-done((f32[96,128]{1,0:T(8,128)S(1)}, f32[96,128]{1,0:T(8,128)S(1)}, u32[]{:S(2)}, u32[]{:S(2)}) %collective-permute-start.10) | collective-permute-done | bytes 49184 | tf_op jit(solution)/shard_map/ppermute | solution.py:667
  77.6 0.9 collective-permute-start.12
  78.4 0.0 collective-permute-done.11.refs_9_
  78.4 0.0 collective-permute-start.13
  78.4 0.9 collective-permute-done.12.refs_10_
  79.3 0.4 collective-permute-done.13.refs_11_
  79.7 0.0 collective-permute-done.9.refs_7_
  79.7 0.0 copy-done
  79.7 9.7 %shard_map.31 = (f32[20,48,128]{2,1,0:T(8,128)S(1)}, f32[20,48,128]{2,1,0:T(8,128)S(1)}, f32[64,8,128]{2,1,0:T(8,128)S(1)}, f32[12,24,128]{2,1,0:T(8,128)S(1)}, ...) custom-call(f32[256,256]{1,0:T(8,128)S(1)} %copy-done, f32[40,80,128]{2,1,0:T(8,128)S(1)} %get-tuple-element.29.refs_1_, ...), custom_call_target="tpu_custom_call" | custom-call | flops 40000000 | bytes 1048576 | tf_op jit(solution)/shard_map/pallas_call | solution.py:607
  89.3 26.2 %all_to_all.11.refs_6_ = f32[64,8,128]{2,1,0:T(8,128)S(1)} all-to-all(f32[64,8,128]{2,1,0:T(8,128)S(1)} %get-tuple-element.40), channel_id=1, replica_groups=mesh['groups'=2,'gx'=16,'gy'=4,'gz'=2] {'gx','gy'}, dimensions={0} | all-to-all | bytes 524288 | tf_op jit(solution)/shard_map/all_to_all | solution.py:672
  115.6 4.1 %collective-permute-start.14 = (f32[64,8,128]{2,1,0:T(8,128)S(1)}, f32[64,8,128]{2,1,0:T(8,128)S(1)}, u32[]{:S(2)}, u32[]{:S(2)}) collective-permute-start(f32[64,8,128]{2,1,0:T(8,128)S(1)} %all_to_all.11.refs_6_), channel_id=1, source_target_pairs={{0,1},{1,0},{2,3},{3,2},{4,5},{5,4},{6,7},{7,6},{8,9},{9,8},{10,11... | collective-permute-start | bytes 786440 | tf_op jit(solution)/shard_map/ppermute | solution.py:656
  119.7 0.2 collective-permute-start.15
  119.9 2.4 %collective-permute-start.16 = (f32[48,128]{1,0:T(8,128)S(1)}, f32[48,128]{1,0:T(8,128)S(1)}, u32[]{:S(2)}, u32[]{:S(2)}) collective-permute-start(f32[48,128]{1,0:T(8,128)S(1)} %get-tuple-element.42), channel_id=1, source_target_pairs={{0,120},{1,7},{2,122},{3,1},{4,124},{5,3},{6,126},{7,5},{8,0},{9,1... | collective-permute-start | bytes 73736 | tf_op jit(solution)/shard_map/ppermute | solution.py:667
  122.4 1.2 collective-permute-done.15.refs_8_
  123.6 1.2 collective-permute-start.17
  124.7 0.0 collective-permute-done.16.refs_9_
  124.7 0.0 collective-permute-start.18
  124.7 0.8 collective-permute-done.17.refs_10_
  125.6 0.3 collective-permute-done.18.refs_11_
  125.9 0.0 collective-permute-done.14.refs_7_
  125.9 6.6 %shard_map.32 = f32[16,32,128]{2,1,0:T(8,128)} custom-call(f32[256,256]{1,0:T(8,128)S(1)} %copy-done, f32[40,80,128]{2,1,0:T(8,128)S(1)} %get-tuple-element.29.refs_1_, f32[40,80,128]{2,1,0:T(8,128)S(1)} %get-tuple-element.30.refs_2_, f32[20,48,128]{2,1,0:T(8,128)S(1)} %get-tuple-element.37.refs_3_, f32[20,48,128]{2,1,0:T(8,128)S(1)} %get-tuple-element.38.refs_4_, ...), custom_call_target="tpu_custom_call" | custom-call | flops 20000000 | bytes 1048576 | tf_op jit(solution)/shard_map/pallas_call | solution.py:607
  (1 shorter events, 0.0 us)
Async XLA Ops:
  0.0 79.7 %copy-start = (f32[256,256]{1,0:T(8,128)S(1)}, f32[256,256]{1,0:T(8,128)}, u32[]{:S(2)}) copy-start(f32[256,256]{1,0:T(8,128)} %constant.2.clone.refs_0_) | copy-start | bytes 786436
  0.0 1.0 copy-start.1
  1.3 27.0 %collective-permute-start = (f32[10,32,128]{2,1,0:T(8,128)S(1)}, f32[10,32,128]{2,1,0:T(8,128)S(1)}, u32[]{:S(2)}, u32[]{:S(2)}) collective-permute-start(f32[10,32,128]{2,1,0:T(8,128)S(1)} %get-tuple-element.25), channel_id=1, source_target_pairs={{0,8},{8,16},{16,24},{24,32},{32,40},{40,48},{48,56},{56,64},{64,7... | collective-permute-start | bytes 491528 | tf_op jit(solution)/shard_map/ppermute | solution.py:656
  4.7 23.6 %collective-permute-start.1 = (f32[10,32,128]{2,1,0:T(8,128)S(1)}, f32[10,32,128]{2,1,0:T(8,128)S(1)}, u32[]{:S(2)}, u32[]{:S(2)}) collective-permute-start(f32[10,32,128]{2,1,0:T(8,128)S(1)} %get-tuple-element.26), channel_id=1, source_target_pairs={{0,120},{8,0},{16,8},{24,16},{32,24},{40,32},{48,40},{56,48},{64,5... | collective-permute-start | bytes 491528 | tf_op jit(solution)/shard_map/ppermute | solution.py:656
  28.3 6.8 %collective-permute-start.2 = (f32[360,128]{1,0:T(8,128)S(1)}, f32[360,128]{1,0:T(8,128)S(1)}, u32[]{:S(2)}, u32[]{:S(2)}) collective-permute-start(f32[360,128]{1,0:T(8,128)S(1)} %get-tuple-element.27), channel_id=1, source_target_pairs={{0,2},{2,4},{4,6},{6,0},{1,3},{3,5},{5,7},{7,1},{8,10},{10,12},{12... | collective-permute-start | bytes 552968 | tf_op jit(solution)/shard_map/ppermute | solution.py:656
  29.8 7.1 %collective-permute-start.3 = (f32[360,128]{1,0:T(8,128)S(1)}, f32[360,128]{1,0:T(8,128)S(1)}, u32[]{:S(2)}, u32[]{:S(2)}) collective-permute-start(f32[360,128]{1,0:T(8,128)S(1)} %get-tuple-element.28), channel_id=1, source_target_pairs={{0,6},{2,0},{4,2},{6,4},{1,7},{3,1},{5,3},{7,5},{8,14},{10,8},{12,... | collective-permute-start | bytes 552968 | tf_op jit(solution)/shard_map/ppermute | solution.py:656
  31.5 6.0 %collective-permute-start.4 = (f32[16,32,128]{2,1,0:T(8,128)S(1)}, f32[16,32,128]{2,1,0:T(8,128)S(1)}, u32[]{:S(2)}, u32[]{:S(2)}) collective-permute-start(f32[16,32,128]{2,1,0:T(8,128)S(1)} %get-tuple-element.24.mine.refs_0_), channel_id=1, source_target_pairs={{0,1},{1,0},{2,3},{3,2},{4,5},{5,4},{6,7},{7,6},{8,9},{9,8},{10,11... | collective-permute-start | bytes 786440 | tf_op jit(solution)/shard_map/ppermute | solution.py:656
  35.1 3.7 %collective-permute-start.7 = (f32[360,128]{1,0:T(8,128)S(1)}, f32[360,128]{1,0:T(8,128)S(1)}, u32[]{:S(2)}, u32[]{:S(2)}) collective-permute-start(f32[360,128]{1,0:T(8,128)S(1)} %collective-permute-done.2.refs_3_), channel_id=1, source_target_pairs={{0,1},{1,0},{2,3},{3,2},{4,5},{5,4},{6,7},{7,6},{8,9},{9,8},{10,11... | collective-permute-start | bytes 552968 | tf_op jit(solution)/shard_map/ppermute | solution.py:656
  36.9 1.9 %collective-permute-start.8 = (f32[360,128]{1,0:T(8,128)S(1)}, f32[360,128]{1,0:T(8,128)S(1)}, u32[]{:S(2)}, u32[]{:S(2)}) collective-permute-start(f32[360,128]{1,0:T(8,128)S(1)} %collective-permute-done.3.refs_4_), channel_id=1, source_target_pairs={{0,1},{1,0},{2,3},{3,2},{4,5},{5,4},{6,7},{7,6},{8,9},{9,8},{10,11... | collective-permute-start | bytes 552968 | tf_op jit(solution)/shard_map/ppermute | solution.py:656
  36.9 1.7 %collective-permute-start.5 = (f32[10,32,128]{2,1,0:T(8,128)S(1)}, f32[10,32,128]{2,1,0:T(8,128)S(1)}, u32[]{:S(2)}, u32[]{:S(2)}) collective-permute-start(f32[10,32,128]{2,1,0:T(8,128)S(1)} %collective-permute-done.x_low.refs_1_), channel_id=1, source_target_pairs={{0,1},{1,0},{2,3},{3,2},{4,5},{5,4},{6,7},{7,6},{8,9},{9,8},{10,11... | collective-permute-start | bytes 491528 | tf_op jit(solution)/shard_map/ppermute | solution.py:656
  37.4 1.4 %collective-permute-start.6 = (f32[10,32,128]{2,1,0:T(8,128)S(1)}, f32[10,32,128]{2,1,0:T(8,128)S(1)}, u32[]{:S(2)}, u32[]{:S(2)}) collective-permute-start(f32[10,32,128]{2,1,0:T(8,128)S(1)} %collective-permute-done.1.x_high.refs_2_), channel_id=1, source_target_pairs={{0,1},{1,0},{2,3},{3,2},{4,5},{5,4},{6,7},{7,6},{8,9},{9,8},{10,11... | collective-permute-start | bytes 491528 | tf_op jit(solution)/shard_map/ppermute | solution.py:656
  69.4 10.3 %collective-permute-start.9 = (f32[64,8,128]{2,1,0:T(8,128)S(1)}, f32[64,8,128]{2,1,0:T(8,128)S(1)}, u32[]{:S(2)}, u32[]{:S(2)}) collective-permute-start(f32[64,8,128]{2,1,0:T(8,128)S(1)} %all_to_all.10.refs_6_), channel_id=1, source_target_pairs={{0,1},{1,0},{2,3},{3,2},{4,5},{5,4},{6,7},{7,6},{8,9},{9,8},{10,11... | collective-permute-start | bytes 786440 | tf_op jit(solution)/shard_map/ppermute | solution.py:656
  73.1 4.4 %collective-permute-start.10 = (f32[96,128]{1,0:T(8,128)S(1)}, f32[96,128]{1,0:T(8,128)S(1)}, u32[]{:S(2)}, u32[]{:S(2)}) collective-permute-start(f32[96,128]{1,0:T(8,128)S(1)} %get-tuple-element.35), channel_id=1, source_target_pairs={{0,8},{1,3},{2,10},{3,5},{4,12},{5,7},{6,14},{7,1},{8,16},{9,11},{... | collective-permute-start | bytes 147464 | tf_op jit(solution)/shard_map/ppermute | solution.py:667
  73.4 5.1 %collective-permute-start.11 = (f32[96,128]{1,0:T(8,128)S(1)}, f32[96,128]{1,0:T(8,128)S(1)}, u32[]{:S(2)}, u32[]{:S(2)}) collective-permute-start(f32[96,128]{1,0:T(8,128)S(1)} %get-tuple-element.36), channel_id=1, source_target_pairs={{0,120},{1,7},{2,122},{3,1},{4,124},{5,3},{6,126},{7,5},{8,0},{9,1... | collective-permute-start | bytes 147464 | tf_op jit(solution)/shard_map/ppermute | solution.py:667
  77.6 1.7 %collective-permute-start.12 = (f32[96,128]{1,0:T(8,128)S(1)}, f32[96,128]{1,0:T(8,128)S(1)}, u32[]{:S(2)}, u32[]{:S(2)}) collective-permute-start(f32[96,128]{1,0:T(8,128)S(1)} %collective-permute-done.10.refs_8_), channel_id=1, source_target_pairs={{0,1},{1,0},{2,3},{3,2},{4,5},{5,4},{6,7},{7,6},{8,9},{9,8},{10,11... | collective-permute-start | bytes 147464 | tf_op jit(solution)/shard_map/ppermute | solution.py:656
  78.4 1.2 collective-permute-start.13
  115.6 10.4 %collective-permute-start.14 = (f32[64,8,128]{2,1,0:T(8,128)S(1)}, f32[64,8,128]{2,1,0:T(8,128)S(1)}, u32[]{:S(2)}, u32[]{:S(2)}) collective-permute-start(f32[64,8,128]{2,1,0:T(8,128)S(1)} %all_to_all.11.refs_6_), channel_id=1, source_target_pairs={{0,1},{1,0},{2,3},{3,2},{4,5},{5,4},{6,7},{7,6},{8,9},{9,8},{10,11... | collective-permute-start | bytes 786440 | tf_op jit(solution)/shard_map/ppermute | solution.py:656
  119.7 3.9 %collective-permute-start.15 = (f32[48,128]{1,0:T(8,128)S(1)}, f32[48,128]{1,0:T(8,128)S(1)}, u32[]{:S(2)}, u32[]{:S(2)}) collective-permute-start(f32[48,128]{1,0:T(8,128)S(1)} %get-tuple-element.41), channel_id=1, source_target_pairs={{0,8},{1,3},{2,10},{3,5},{4,12},{5,7},{6,14},{7,1},{8,16},{9,11},{... | collective-permute-start | bytes 73736 | tf_op jit(solution)/shard_map/ppermute | solution.py:667
  119.9 4.8 %collective-permute-start.16 = (f32[48,128]{1,0:T(8,128)S(1)}, f32[48,128]{1,0:T(8,128)S(1)}, u32[]{:S(2)}, u32[]{:S(2)}) collective-permute-start(f32[48,128]{1,0:T(8,128)S(1)} %get-tuple-element.42), channel_id=1, source_target_pairs={{0,120},{1,7},{2,122},{3,1},{4,124},{5,3},{6,126},{7,5},{8,0},{9,1... | collective-permute-start | bytes 73736 | tf_op jit(solution)/shard_map/ppermute | solution.py:667
  123.6 2.0 %collective-permute-start.17 = (f32[48,128]{1,0:T(8,128)S(1)}, f32[48,128]{1,0:T(8,128)S(1)}, u32[]{:S(2)}, u32[]{:S(2)}) collective-permute-start(f32[48,128]{1,0:T(8,128)S(1)} %collective-permute-done.15.refs_8_), channel_id=1, source_target_pairs={{0,1},{1,0},{2,3},{3,2},{4,5},{5,4},{6,7},{7,6},{8,9},{9,8},{10,11... | collective-permute-start | bytes 73736 | tf_op jit(solution)/shard_map/ppermute | solution.py:656
  124.7 1.2 collective-permute-start.18

commit v3 on v2

--- a/solution.py
+++ b/solution.py
@@ -122,9 +122,9 @@
         f1[X1 - halo + m, pl.ds(Y1 - 4, 24), :] = 0.125 * (t0[m, pl.ds(0, 24, stride=2), :] + t0[m, pl.ds(1, 24, stride=2), :])
 
 
-def mean_matrix(source_of_out):
+def mean_matrix(source_of_out, gap=1):
     source, out = iota((LANES, LANES), 0), source_of_out(iota((LANES, LANES), 1))
-    return jnp.where((source == out) | (source == out + 1), 0.125, 0.0).astype(F32)
+    return jnp.where((source == out) | (source == out + gap), 0.125, 0.0).astype(F32)
 
 
 def pick_matrix(source_of_out):
@@ -181,59 +181,56 @@
         )
         layers.append(jnp.where(core == 0, s[0:4], s[4:8]))
     n = sizes_2()[2]
-    at = lambda o: 2 * lax.rem(o + n // 2 * core, n)
-    low = mean_matrix(lambda o: jnp.where(o < n, at(o), -2))
-    high = mean_matrix(lambda o: jnp.where(o >= n, at(o), -2))
+    at = lambda o: 2 * lax.rem(o // 2 + n // 2 * core, n)
+    low = mean_matrix(lambda o: jnp.where(lax.rem(o, 2) == 0, at(o), -2))
+    high = mean_matrix(lambda o: jnp.where(lax.rem(o, 2) == 1, at(o), -2))
     packed = dot(jnp.concatenate(layers[0:2], axis=0), low) + dot(jnp.concatenate(layers[2:4], axis=0), high)
     for s in range(out.shape[0]):
         out[s] = packed
 
 
-def turned(v, step, n):
+def along_z(v, step, parts):
     axis = v.ndim - 1
-    moved = pltpu.roll(v, step % LANES, axis)
-    if n == LANES:
-        return moved
-    lane = lax.rem(iota(v.shape, axis), n)
-    wrapped = pltpu.roll(v, (step - n if step > 0 else step + n) % LANES, axis)
-    return jnp.where(lane < step if step > 0 else lane >= n + step, wrapped, moved)
-
-
-def along_z(v, step, n):
-    return turned(v, step, n) + turned(v, -step, n)
-
-
-def next_segment(v, n):
-    return pltpu.roll(v, n % LANES, v.ndim - 1)
-
-
-def across(v, n):
+    return pltpu.roll(v, step * parts, axis) + pltpu.roll(v, LANES - step * parts, axis)
+
+
+def next_part(v, parts, ahead):
+    if parts == 1:
+        return v
+    axis = v.ndim - 1
+    q = lax.rem(iota(v.shape, axis), parts)
+    if ahead:
+        return jnp.where(q == 0, pltpu.roll(v, LANES + 1 - parts, axis), pltpu.roll(v, 1, axis))
+    return jnp.where(q == parts - 1, pltpu.roll(v, parts - 1, axis), pltpu.roll(v, LANES - 1, axis))
+
+
+def across(v, parts):
     last, rows = v.shape[0] - 1, v.shape[1]
-    up = jnp.concatenate([next_segment(v[last:], n), v[:last]], axis=0)
-    down = jnp.concatenate([v[1:], next_segment(v[:1], -n)], axis=0)
+    up = jnp.concatenate([next_part(v[last:], parts, True), v[:last]], axis=0)
+    down = jnp.concatenate([v[1:], next_part(v[:1], parts, False)], axis=0)
     return (up + down) + (pltpu.roll(v, 1, 1) + pltpu.roll(v, rows - 1, 1))
 
 
-def applied(level, v, n):
+def applied(level, v, parts):
     a, _ = coefficients(level)
-    z1, z2 = along_z(v, 1, n), along_z(v, 2, n)
-    one = across(v, n)
+    z1, z2 = along_z(v, 1, parts), along_z(v, 2, parts)
+    one = across(v, parts)
     sv = one + z1
-    ssv = across(one + 2.0 * z1, n) + (z2 + 2.0 * v)
+    ssv = across(one + 2.0 * z1, parts) + (z2 + 2.0 * v)
     t = 6.0 * v - sv
     tt = 6.0 * t - (6.0 * sv - ssv)
     return t, a * t + SCREEN * v, (a * a) * tt + (2.0 * a * SCREEN) * t + (SCREEN * SCREEN) * v
 
 
-def start_whole(level, f, n=LANES):
+def start_whole(level, f, parts=1):
     a, k = coefficients(level)
-    t, af, aaf = applied(level, f, n)
+    t, af, aaf = applied(level, f, parts)
     return (2.0 * k - k * k * SCREEN) * f - (k * k * a) * t, f - 2.0 * k * af + (k * k) * aaf, af
 
 
-def smooth_whole(level, f, af, v, n=LANES):
+def smooth_whole(level, f, af, v, parts=1):
     a, k = coefficients(level)
-    t, _, aav = applied(level, v, n)
+    t, _, aav = applied(level, v, parts)
     r = (f - a * t) - SCREEN * v
     return v + 2.0 * k * r - (k * k) * (af - aav)
 
@@ -260,11 +257,6 @@
 
     cells = shape[0] * shape[1] * shape[2]
     return cycle(5, np.eye(cells).reshape(cells, *shape)).reshape(cells, cells).astype(np.float32)
-
-
-def up_z(level):
-    n = sizes_2()[2] >> (level - 2)
-    return pick_matrix(lambda o: lax.div(lax.rem(o, n), 2))
 
 
 def pair_layers(v):
@@ -301,25 +293,26 @@
 
 
 def solve_3(f3, t3, matrix):
-    n, x3, y4 = sizes_2()[2] // 2, f3.shape[0], f3.shape[1] // 2
-    segments, x4 = LANES // n, x3 // 2
-    v3, r3, af3 = start_whole(3, f3, n)
+    x4, y4 = f3.shape[0] // 2, f3.shape[1] // 2
+    parts_3 = LANES // (sizes_2()[2] // 2)
+    v3, r3, af3 = start_whole(3, f3, parts_3)
     t3[...] = pair_layers(r3)
     s = flat(t3[:, pl.ds(0, y4, stride=2), :] + t3[:, pl.ds(1, y4, stride=2), :])
-    means = [mean_matrix(lambda o: n * q + 2 * lax.rem(o, n // 2)) for q in range(segments)]
+    z4 = LANES // parts_3 // 2
+    means = [mean_matrix(lambda o: 2 * parts_3 * lax.rem(o, z4) + q, parts_3) for q in range(parts_3)]
     f4 = jnp.concatenate([dot(s, m).reshape(x4, y4, LANES) for m in means], axis=0)
     v4, r4, af4 = start_whole(4, f4)
     e4 = solve_bottom(flat(pair_layers(r4)), bottom_shape(), matrix).reshape(-1, y4, LANES)
     v4 = smooth_whole(4, f4, af4, v4 + twice(e4))
-    picks = [pick_matrix(lambda o: jnp.where(o // n == q, lax.rem(o, n) // 2, -1)) for q in range(segments)]
+    picks = [pick_matrix(lambda o: jnp.where(lax.rem(o, parts_3) == q, o // parts_3 // 2, -1)) for q in range(parts_3)]
     e3 = sum(dot(flat(v4[x4 * q : x4 * (q + 1)]), m) for q, m in enumerate(picks)).reshape(x4, y4, LANES)
     t3[:, pl.ds(0, y4, stride=2), :] = e3
     t3[:, pl.ds(1, y4, stride=2), :] = e3
-    return smooth_whole(3, f3, af3, v3 + twice(t3[...]), n)
+    return smooth_whole(3, f3, af3, v3 + twice(t3[...]), parts_3)
 
 
 def unpack_2(f2, mine, other, core):
-    low = iota((8, LANES), 1) < 64
+    even = lax.rem(iota((8, LANES), 1), 2) == 0
     top = iota((8, LANES), 0) < 4
     along_y = lax.axis_size("gy")
     half = (f2.shape[0] - 2) // 4
@@ -334,9 +327,9 @@
             (u, w), (u2, w2) = tiles
             for xp in range(2):
                 if xp == 0:
-                    d, e = jnp.where(low, u, pltpu.roll(u2, 64, 1)), jnp.where(low, w, pltpu.roll(w2, 64, 1))
+                    d, e = jnp.where(even, u, pltpu.roll(u2, 1, 1)), jnp.where(even, w, pltpu.roll(w2, 1, 1))
                 else:
-                    d, e = jnp.where(low, pltpu.roll(u, 64, 1), u2), jnp.where(low, pltpu.roll(w, 64, 1), w2)
+                    d, e = jnp.where(even, pltpu.roll(u, LANES - 1, 1), u2), jnp.where(even, pltpu.roll(w, LANES - 1, 1), w2)
                 f2[1 + gx * 4 + 2 * xp, pl.ds(gy * 8, 8), :] = jnp.where(top, d, pltpu.roll(e, 4, 0))
                 f2[2 + gx * 4 + 2 * xp, pl.ds(gy * 8, 8), :] = jnp.where(top, pltpu.roll(d, 4, 0), e)
 
@@ -345,23 +338,23 @@
 
 def close_2(v):
     last = v.shape[0] - 2
-    v[0] = next_segment(v[last], 64)
-    v[last + 1] = next_segment(v[1], -64)
-
-
-def beside_2(centre, before, after, n):
+    v[0] = next_part(v[last], 2, True)
+    v[last + 1] = next_part(v[1], 2, False)
+
+
+def beside_2(centre, before, after):
     rows = centre.shape[0]
     return (
-        (before + after) + (pltpu.roll(centre, 1, 0) + pltpu.roll(centre, rows - 1, 0)) + along_z(centre, 1, n)
+        (before + after) + (pltpu.roll(centre, 1, 0) + pltpu.roll(centre, rows - 1, 0)) + along_z(centre, 1, 2)
     )
 
 
 def level_2(near, f2, v2, t2, t3, s3, p2, a2, b2, bottom, gx, halo):
-    n, rows, length = f2.shape[0] - 2, f2.shape[1], sizes_2()[2]
+    n, rows = f2.shape[0] - 2, f2.shape[1]
     close_2(f2)
 
     def first(i):
-        v2[i] = twice_from_zero(2, f2[i], beside_2(f2[i], f2[i - 1], f2[i + 1], length))
+        v2[i] = twice_from_zero(2, f2[i], beside_2(f2[i], f2[i - 1], f2[i + 1]))
 
     over_layers(1, n, 16, first)
     close_2(v2)
@@ -369,7 +362,7 @@
     def second(q):
         pair = []
         for i in (2 * q + 1, 2 * q + 2):
-            pair.append(residual_of(2, f2[i], v2[i], beside_2(v2[i], v2[i - 1], v2[i + 1], length)))
+            pair.append(residual_of(2, f2[i], v2[i], beside_2(v2[i], v2[i - 1], v2[i + 1])))
         t2[q] = pair[0] + pair[1]
 
     over_layers(0, n // 2, 8, second)
@@ -378,10 +371,10 @@
 
     def means(part):
         def source(o):
-            q = o // (length // 2)
-            return jnp.where(lax.rem(q, 2) == part, q // 2 * length + 2 * lax.rem(o, length // 2), -2)
-
-        return mean_matrix(source)
+            q = lax.rem(o, 4)
+            return jnp.where(lax.rem(q, 2) == part, o // 4 * 4 + q // 2, -4)
+
+        return mean_matrix(source, 2)
 
     f3 = dot(flat(s[:x3]), means(0)) + dot(flat(s[x3:]), means(1))
     s3[...] = solve_3(f3.reshape(x3, rows // 2, LANES), t3, bottom)
@@ -392,25 +385,26 @@
     for m in range(count // 2):
         at = lax.rem(lax.div(start, 2) + m, n)
         line = s3[lax.rem(at, x3)]
-        lines.append(pltpu.roll(line, lax.rem(LANES - length // 2 * lax.div(at, x3), LANES), 1))
-    e = dot(jnp.concatenate(lines, axis=0), up_z(2)).reshape(count // 2, rows // 2, LANES)
+        lines.append(pltpu.roll(line, lax.rem(LANES - lax.div(at, x3), LANES), 1))
+    e = dot(jnp.concatenate(lines, axis=0), pick_matrix(lambda o: o // 4 * 4)).reshape(count // 2, rows // 2, LANES)
     p2[pl.ds(0, count // 2), pl.ds(0, rows // 2, stride=2), :] = e
     p2[pl.ds(0, count // 2), pl.ds(1, rows // 2, stride=2), :] = e
-    low = iota((rows, LANES), 1) < 64
+    even = lax.rem(iota((rows, LANES), 1), 2) == 0
     for m in range(count):
         at = lax.rem(start + m, 2 * n)
         i, lower = 1 + lax.rem(at, n), at < n
         whole = []
         for ref in (v2, f2):
-            turned_half = pltpu.roll(ref[i], 64, 1)
-            whole.append(jnp.where(low, jnp.where(lower, ref[i], turned_half), jnp.where(lower, turned_half, ref[i])))
+            line = ref[i]
+            moved = pltpu.roll(line, jnp.where(lower, 1, LANES - 1), 1)
+            whole.append(jnp.where(even == lower, line, moved))
         a2[m] = whole[0] + p2[m // 2]
         t2[m] = whole[1]
     for m in range(1, count - 1):
-        nb = beside_2(a2[m], a2[m - 1], a2[m + 1], LANES)
+        nb = beside_2(a2[m], a2[m - 1], a2[m + 1])
         b2[m] = relaxed(2, t2[m], a2[m], nb)
     for m in range(2, count - 2):
-        nb = beside_2(b2[m], b2[m - 1], b2[m + 1], LANES)
+        nb = beside_2(b2[m], b2[m - 1], b2[m + 1])
         near[m - 2] = relaxed(2, t2[m], b2[m], nb)
 
 
@@ -422,7 +416,7 @@
         y2[m, pl.ds(rows, rows), :] = near[m]
     start = pl.multiple_of(lax.rem(gy * 8 + rows - 4, rows), 4)
     picked = jnp.concatenate([y2[m, pl.ds(start, 16), :] for m in range(layers)], axis=0)
-    e = dot(picked, pick_matrix(lambda o: lax.rem(lax.div(o, 2) + n // 2 * core, n))).reshape(layers, 16, LANES)
+    e = dot(picked, pick_matrix(lambda o: 2 * lax.rem(lax.div(o, 2) + n // 2 * core, n))).reshape(layers, 16, LANES)
     p1[pl.ds(0, layers), pl.ds(0, 16, stride=2), :] = e
     p1[pl.ds(0, layers), pl.ds(1, 16, stride=2), :] = e
     for m in range(2 * layers):

time: 133 us -> 132 us (level)
  no operation moved by 1% of the time
where the time goes in v3:
time: 132 us
  blocking collectives  54.2 us (41%)
  starting transfers between devices  45.3 us (34%)
  Pallas kernels  18 us (14%)
  waiting for transfers between devices  12.8 us (10%)
    all_to_all x2, blocking collectives, exchange(): mine = lax.all_to_all(send, ('gx', 'gy'), 0, 0, tiled=True)  54.2 us
    ppermute x15, starting transfers between devices, from_(): lax.ppermute(value, axis, [(i, (i + step) % size) for i in range(size)])  39.9 us
    pallas_call x5, Pallas kernels, run(): pl.pallas_call(kernel, out_shape=outs, out_specs=[spec] * len(outs) if is...  18 us
    ppermute x15, waiting for transfers between devices, from_(): lax.ppermute(value, axis, [(i, (i + step) % size) for i in range(size)])  9.86 us
    ppermute x4, starting transfers between devices, beside_(): return lax.ppermute(value, axes, pairs)  5.35 us
    ppermute x4, waiting for transfers between devices, beside_(): return lax.ppermute(value, axes, pairs)  2.98 us
  transfers between devices with their start and end apart: 19, of which 10 were waited for; matrix products, arithmetic and copies ran while one was open for 0% of the time, Pallas kernels for 0%

profile of v3, /device:TPU:33, one launch (start us, length us, event | category | flops | bytes accessed | tf_op | source)
XLA Modules:
  0.0 131.5 jit_solution(14557865861036018909)
XLA Ops:
  0.0 0.0 copy-start
  0.0 0.0 copy-start.1
  0.0 1.0 copy-done.1
  1.0 0.3 shard_map.28
  1.3 3.4 %collective-permute-start = (f32[10,32,128]{2,1,0:T(8,128)S(1)}, f32[10,32,128]{2,1,0:T(8,128)S(1)}, u32[]{:S(2)}, u32[]{:S(2)}) collective-permute-start(f32[10,32,128]{2,1,0:T(8,128)S(1)} %get-tuple-element.25), channel_id=1, source_target_pairs={{0,8},{8,16},{16,24},{24,32},{32,40},{40,48},{48,56},{56,64},{64,7... | collective-permute-start | bytes 491528 | tf_op jit(solution)/shard_map/ppermute | solution.py:650
  4.7 19.7 %collective-permute-start.1 = (f32[10,32,128]{2,1,0:T(8,128)S(1)}, f32[10,32,128]{2,1,0:T(8,128)S(1)}, u32[]{:S(2)}, u32[]{:S(2)}) collective-permute-start(f32[10,32,128]{2,1,0:T(8,128)S(1)} %get-tuple-element.26), channel_id=1, source_target_pairs={{0,120},{8,0},{16,8},{24,16},{32,24},{40,32},{48,40},{56,48},{64,5... | collective-permute-start | bytes 491528 | tf_op jit(solution)/shard_map/ppermute | solution.py:650
  24.4 3.8 %collective-permute-done.x_low.refs_1_ = f32[10,32,128]{2,1,0:T(8,128)S(1)} collective-permute-done((f32[10,32,128]{2,1,0:T(8,128)S(1)}, f32[10,32,128]{2,1,0:T(8,128)S(1)}, u32[]{:S(2)}, u32[]{:S(2)}) %collective-permute-start) | collective-permute-done | bytes 163872 | tf_op jit(solution)/shard_map/ppermute | solution.py:650
  28.3 0.0 collective-permute-done.1.x_high.refs_2_
  28.3 1.5 %collective-permute-start.2 = (f32[360,128]{1,0:T(8,128)S(1)}, f32[360,128]{1,0:T(8,128)S(1)}, u32[]{:S(2)}, u32[]{:S(2)}) collective-permute-start(f32[360,128]{1,0:T(8,128)S(1)} %get-tuple-element.27), channel_id=1, source_target_pairs={{0,2},{2,4},{4,6},{6,0},{1,3},{3,5},{5,7},{7,1},{8,10},{10,12},{12... | collective-permute-start | bytes 552968 | tf_op jit(solution)/shard_map/ppermute | solution.py:650
  29.8 1.7 %collective-permute-start.3 = (f32[360,128]{1,0:T(8,128)S(1)}, f32[360,128]{1,0:T(8,128)S(1)}, u32[]{:S(2)}, u32[]{:S(2)}) collective-permute-start(f32[360,128]{1,0:T(8,128)S(1)} %get-tuple-element.28), channel_id=1, source_target_pairs={{0,6},{2,0},{4,2},{6,4},{1,7},{3,1},{5,3},{7,5},{8,14},{10,8},{12,... | collective-permute-start | bytes 552968 | tf_op jit(solution)/shard_map/ppermute | solution.py:650
  31.5 1.5 %collective-permute-start.4 = (f32[16,32,128]{2,1,0:T(8,128)S(1)}, f32[16,32,128]{2,1,0:T(8,128)S(1)}, u32[]{:S(2)}, u32[]{:S(2)}) collective-permute-start(f32[16,32,128]{2,1,0:T(8,128)S(1)} %get-tuple-element.24.mine.refs_0_), channel_id=1, source_target_pairs={{0,1},{1,0},{2,3},{3,2},{4,5},{5,4},{6,7},{7,6},{8,9},{9,8},{10,11... | collective-permute-start | bytes 786440 | tf_op jit(solution)/shard_map/ppermute | solution.py:650
  32.9 2.2 %collective-permute-done.2.refs_3_ = f32[360,128]{1,0:T(8,128)S(1)} collective-permute-done((f32[360,128]{1,0:T(8,128)S(1)}, f32[360,128]{1,0:T(8,128)S(1)}, u32[]{:S(2)}, u32[]{:S(2)}) %collective-permute-start.2) | collective-permute-done | bytes 184352 | tf_op jit(solution)/shard_map/ppermute | solution.py:650
  35.1 1.8 %collective-permute-start.7 = (f32[360,128]{1,0:T(8,128)S(1)}, f32[360,128]{1,0:T(8,128)S(1)}, u32[]{:S(2)}, u32[]{:S(2)}) collective-permute-start(f32[360,128]{1,0:T(8,128)S(1)} %collective-permute-done.2.refs_3_), channel_id=1, source_target_pairs={{0,1},{1,0},{2,3},{3,2},{4,5},{5,4},{6,7},{7,6},{8,9},{9,8},{10,11... | collective-permute-start | bytes 552968 | tf_op jit(solution)/shard_map/ppermute | solution.py:650
  36.9 0.0 collective-permute-done.3.refs_4_
  36.9 0.0 collective-permute-start.8
  36.9 0.5 collective-permute-start.5
  37.4 0.0 collective-permute-start.6
  37.4 0.0 collective-permute-done.4.refs_5_
  37.4 1.1 collective-permute-done.5.refs_6_
  38.6 0.2 collective-permute-done.6.refs_7_
  38.8 0.0 collective-permute-done.7.refs_8_
  38.8 0.0 collective-permute-done.8.refs_9_
  38.8 2.6 %shard_map.30 = (f32[40,80,128]{2,1,0:T(8,128)S(1)}, f32[40,80,128]{2,1,0:T(8,128)S(1)}, f32[40,80,128]{2,1,0:T(8,128)S(1)}, f32[40,80,128]{2,1,0:T(8,128)S(1)},...) custom-call(f32[16,32,128]{2,1,0:T(8,128)S(1)} %get-tuple-element.24.min, ...), custom_call_target="tpu_custom_call" | custom-call | flops 10000000 | bytes 1048576 | tf_op jit(solution)/shard_map/pallas_call | solution.py:601
  41.5 27.9 %all_to_all.10.refs_6_ = f32[64,8,128]{2,1,0:T(8,128)S(1)} all-to-all(f32[64,8,128]{2,1,0:T(8,128)S(1)} %get-tuple-element.34), channel_id=1, replica_groups=mesh['groups'=2,'gx'=16,'gy'=4,'gz'=2] {'gx','gy'}, dimensions={0} | all-to-all | bytes 524288 | tf_op jit(solution)/shard_map/all_to_all | solution.py:666
  69.4 3.7 %collective-permute-start.9 = (f32[64,8,128]{2,1,0:T(8,128)S(1)}, f32[64,8,128]{2,1,0:T(8,128)S(1)}, u32[]{:S(2)}, u32[]{:S(2)}) collective-permute-start(f32[64,8,128]{2,1,0:T(8,128)S(1)} %all_to_all.10.refs_6_), channel_id=1, source_target_pairs={{0,1},{1,0},{2,3},{3,2},{4,5},{5,4},{6,7},{7,6},{8,9},{9,8},{10,11... | collective-permute-start | bytes 786440 | tf_op jit(solution)/shard_map/ppermute | solution.py:650
  73.1 0.2 collective-permute-start.10
  73.4 2.4 %collective-permute-start.11 = (f32[96,128]{1,0:T(8,128)S(1)}, f32[96,128]{1,0:T(8,128)S(1)}, u32[]{:S(2)}, u32[]{:S(2)}) collective-permute-start(f32[96,128]{1,0:T(8,128)S(1)} %get-tuple-element.36), channel_id=1, source_target_pairs={{0,120},{1,7},{2,122},{3,1},{4,124},{5,3},{6,126},{7,5},{8,0},{9,1... | collective-permute-start | bytes 147464 | tf_op jit(solution)/shard_map/ppermute | solution.py:661
  75.8 1.8 %collective-permute-done.10.refs_8_ = f32[96,128]{1,0:T(8,128)S(1)} collective-permute-done((f32[96,128]{1,0:T(8,128)S(1)}, f32[96,128]{1,0:T(8,128)S(1)}, u32[]{:S(2)}, u32[]{:S(2)}) %collective-permute-start.10) | collective-permute-done | bytes 49184 | tf_op jit(solution)/shard_map/ppermute | solution.py:661
  77.6 0.9 collective-permute-start.12
  78.4 0.0 collective-permute-done.11.refs_9_
  78.4 0.0 collective-permute-start.13
  78.4 0.9 collective-permute-done.12.refs_10_
  79.3 0.4 collective-permute-done.13.refs_11_
  79.7 0.0 collective-permute-done.9.refs_7_
  79.7 0.0 copy-done
  79.7 9.1 %shard_map.31 = (f32[20,48,128]{2,1,0:T(8,128)S(1)}, f32[20,48,128]{2,1,0:T(8,128)S(1)}, f32[64,8,128]{2,1,0:T(8,128)S(1)}, f32[12,24,128]{2,1,0:T(8,128)S(1)}, ...) custom-call(f32[256,256]{1,0:T(8,128)S(1)} %copy-done, f32[40,80,128]{2,1,0:T(8,128)S(1)} %get-tuple-element.29.refs_1_, ...), custom_call_target="tpu_custom_call" | custom-call | flops 40000000 | bytes 1048576 | tf_op jit(solution)/shard_map/pallas_call | solution.py:601
  88.7 26.3 %all_to_all.11.refs_6_ = f32[64,8,128]{2,1,0:T(8,128)S(1)} all-to-all(f32[64,8,128]{2,1,0:T(8,128)S(1)} %get-tuple-element.40), channel_id=1, replica_groups=mesh['groups'=2,'gx'=16,'gy'=4,'gz'=2] {'gx','gy'}, dimensions={0} | all-to-all | bytes 524288 | tf_op jit(solution)/shard_map/all_to_all | solution.py:666
  115.0 4.1 %collective-permute-start.14 = (f32[64,8,128]{2,1,0:T(8,128)S(1)}, f32[64,8,128]{2,1,0:T(8,128)S(1)}, u32[]{:S(2)}, u32[]{:S(2)}) collective-permute-start(f32[64,8,128]{2,1,0:T(8,128)S(1)} %all_to_all.11.refs_6_), channel_id=1, source_target_pairs={{0,1},{1,0},{2,3},{3,2},{4,5},{5,4},{6,7},{7,6},{8,9},{9,8},{10,11... | collective-permute-start | bytes 786440 | tf_op jit(solution)/shard_map/ppermute | solution.py:650
  119.1 0.2 collective-permute-start.15
  119.3 2.4 %collective-permute-start.16 = (f32[48,128]{1,0:T(8,128)S(1)}, f32[48,128]{1,0:T(8,128)S(1)}, u32[]{:S(2)}, u32[]{:S(2)}) collective-permute-start(f32[48,128]{1,0:T(8,128)S(1)} %get-tuple-element.42), channel_id=1, source_target_pairs={{0,120},{1,7},{2,122},{3,1},{4,124},{5,3},{6,126},{7,5},{8,0},{9,1... | collective-permute-start | bytes 73736 | tf_op jit(solution)/shard_map/ppermute | solution.py:661
  121.8 1.2 collective-permute-done.15.refs_8_
  123.0 1.2 collective-permute-start.17
  124.1 0.0 collective-permute-done.16.refs_9_
  124.1 0.0 collective-permute-start.18
  124.1 0.8 collective-permute-done.17.refs_10_
  125.0 0.3 collective-permute-done.18.refs_11_
  125.3 0.0 collective-permute-done.14.refs_7_
  125.3 6.0 %shard_map.32 = f32[16,32,128]{2,1,0:T(8,128)} custom-call(f32[256,256]{1,0:T(8,128)S(1)} %copy-done, f32[40,80,128]{2,1,0:T(8,128)S(1)} %get-tuple-element.29.refs_1_, f32[40,80,128]{2,1,0:T(8,128)S(1)} %get-tuple-element.30.refs_2_, f32[20,48,128]{2,1,0:T(8,128)S(1)} %get-tuple-element.37.refs_3_, f32[20,48,128]{2,1,0:T(8,128)S(1)} %get-tuple-element.38.refs_4_, ...), custom_call_target="tpu_custom_call" | custom-call | flops 20000000 | bytes 1048576 | tf_op jit(solution)/shard_map/pallas_call | solution.py:601
  (1 shorter events, 0.0 us)
Async XLA Ops:
  0.0 79.7 %copy-start = (f32[256,256]{1,0:T(8,128)S(1)}, f32[256,256]{1,0:T(8,128)}, u32[]{:S(2)}) copy-start(f32[256,256]{1,0:T(8,128)} %constant.2.clone.refs_0_) | copy-start | bytes 786436
  0.0 1.0 copy-start.1
  1.3 27.0 %collective-permute-start = (f32[10,32,128]{2,1,0:T(8,128)S(1)}, f32[10,32,128]{2,1,0:T(8,128)S(1)}, u32[]{:S(2)}, u32[]{:S(2)}) collective-permute-start(f32[10,32,128]{2,1,0:T(8,128)S(1)} %get-tuple-element.25), channel_id=1, source_target_pairs={{0,8},{8,16},{16,24},{24,32},{32,40},{40,48},{48,56},{56,64},{64,7... | collective-permute-start | bytes 491528 | tf_op jit(solution)/shard_map/ppermute | solution.py:650
  4.7 23.6 %collective-permute-start.1 = (f32[10,32,128]{2,1,0:T(8,128)S(1)}, f32[10,32,128]{2,1,0:T(8,128)S(1)}, u32[]{:S(2)}, u32[]{:S(2)}) collective-permute-start(f32[10,32,128]{2,1,0:T(8,128)S(1)} %get-tuple-element.26), channel_id=1, source_target_pairs={{0,120},{8,0},{16,8},{24,16},{32,24},{40,32},{48,40},{56,48},{64,5... | collective-permute-start | bytes 491528 | tf_op jit(solution)/shard_map/ppermute | solution.py:650
  28.3 6.8 %collective-permute-start.2 = (f32[360,128]{1,0:T(8,128)S(1)}, f32[360,128]{1,0:T(8,128)S(1)}, u32[]{:S(2)}, u32[]{:S(2)}) collective-permute-start(f32[360,128]{1,0:T(8,128)S(1)} %get-tuple-element.27), channel_id=1, source_target_pairs={{0,2},{2,4},{4,6},{6,0},{1,3},{3,5},{5,7},{7,1},{8,10},{10,12},{12... | collective-permute-start | bytes 552968 | tf_op jit(solution)/shard_map/ppermute | solution.py:650
  29.8 7.1 %collective-permute-start.3 = (f32[360,128]{1,0:T(8,128)S(1)}, f32[360,128]{1,0:T(8,128)S(1)}, u32[]{:S(2)}, u32[]{:S(2)}) collective-permute-start(f32[360,128]{1,0:T(8,128)S(1)} %get-tuple-element.28), channel_id=1, source_target_pairs={{0,6},{2,0},{4,2},{6,4},{1,7},{3,1},{5,3},{7,5},{8,14},{10,8},{12,... | collective-permute-start | bytes 552968 | tf_op jit(solution)/shard_map/ppermute | solution.py:650
  31.5 6.0 %collective-permute-start.4 = (f32[16,32,128]{2,1,0:T(8,128)S(1)}, f32[16,32,128]{2,1,0:T(8,128)S(1)}, u32[]{:S(2)}, u32[]{:S(2)}) collective-permute-start(f32[16,32,128]{2,1,0:T(8,128)S(1)} %get-tuple-element.24.mine.refs_0_), channel_id=1, source_target_pairs={{0,1},{1,0},{2,3},{3,2},{4,5},{5,4},{6,7},{7,6},{8,9},{9,8},{10,11... | collective-permute-start | bytes 786440 | tf_op jit(solution)/shard_map/ppermute | solution.py:650
  35.1 3.7 %collective-permute-start.7 = (f32[360,128]{1,0:T(8,128)S(1)}, f32[360,128]{1,0:T(8,128)S(1)}, u32[]{:S(2)}, u32[]{:S(2)}) collective-permute-start(f32[360,128]{1,0:T(8,128)S(1)} %collective-permute-done.2.refs_3_), channel_id=1, source_target_pairs={{0,1},{1,0},{2,3},{3,2},{4,5},{5,4},{6,7},{7,6},{8,9},{9,8},{10,11... | collective-permute-start | bytes 552968 | tf_op jit(solution)/shard_map/ppermute | solution.py:650
  36.9 1.9 %collective-permute-start.8 = (f32[360,128]{1,0:T(8,128)S(1)}, f32[360,128]{1,0:T(8,128)S(1)}, u32[]{:S(2)}, u32[]{:S(2)}) collective-permute-start(f32[360,128]{1,0:T(8,128)S(1)} %collective-permute-done.3.refs_4_), channel_id=1, source_target_pairs={{0,1},{1,0},{2,3},{3,2},{4,5},{5,4},{6,7},{7,6},{8,9},{9,8},{10,11... | collective-permute-start | bytes 552968 | tf_op jit(solution)/shard_map/ppermute | solution.py:650
  36.9 1.7 %collective-permute-start.5 = (f32[10,32,128]{2,1,0:T(8,128)S(1)}, f32[10,32,128]{2,1,0:T(8,128)S(1)}, u32[]{:S(2)}, u32[]{:S(2)}) collective-permute-start(f32[10,32,128]{2,1,0:T(8,128)S(1)} %collective-permute-done.x_low.refs_1_), channel_id=1, source_target_pairs={{0,1},{1,0},{2,3},{3,2},{4,5},{5,4},{6,7},{7,6},{8,9},{9,8},{10,11... | collective-permute-start | bytes 491528 | tf_op jit(solution)/shard_map/ppermute | solution.py:650
  37.4 1.4 %collective-permute-start.6 = (f32[10,32,128]{2,1,0:T(8,128)S(1)}, f32[10,32,128]{2,1,0:T(8,128)S(1)}, u32[]{:S(2)}, u32[]{:S(2)}) collective-permute-start(f32[10,32,128]{2,1,0:T(8,128)S(1)} %collective-permute-done.1.x_high.refs_2_), channel_id=1, source_target_pairs={{0,1},{1,0},{2,3},{3,2},{4,5},{5,4},{6,7},{7,6},{8,9},{9,8},{10,11... | collective-permute-start | bytes 491528 | tf_op jit(solution)/shard_map/ppermute | solution.py:650
  69.4 10.3 %collective-permute-start.9 = (f32[64,8,128]{2,1,0:T(8,128)S(1)}, f32[64,8,128]{2,1,0:T(8,128)S(1)}, u32[]{:S(2)}, u32[]{:S(2)}) collective-permute-start(f32[64,8,128]{2,1,0:T(8,128)S(1)} %all_to_all.10.refs_6_), channel_id=1, source_target_pairs={{0,1},{1,0},{2,3},{3,2},{4,5},{5,4},{6,7},{7,6},{8,9},{9,8},{10,11... | collective-permute-start | bytes 786440 | tf_op jit(solution)/shard_map/ppermute | solution.py:650
  73.1 4.4 %collective-permute-start.10 = (f32[96,128]{1,0:T(8,128)S(1)}, f32[96,128]{1,0:T(8,128)S(1)}, u32[]{:S(2)}, u32[]{:S(2)}) collective-permute-start(f32[96,128]{1,0:T(8,128)S(1)} %get-tuple-element.35), channel_id=1, source_target_pairs={{0,8},{1,3},{2,10},{3,5},{4,12},{5,7},{6,14},{7,1},{8,16},{9,11},{... | collective-permute-start | bytes 147464 | tf_op jit(solution)/shard_map/ppermute | solution.py:661
  73.4 5.1 %collective-permute-start.11 = (f32[96,128]{1,0:T(8,128)S(1)}, f32[96,128]{1,0:T(8,128)S(1)}, u32[]{:S(2)}, u32[]{:S(2)}) collective-permute-start(f32[96,128]{1,0:T(8,128)S(1)} %get-tuple-element.36), channel_id=1, source_target_pairs={{0,120},{1,7},{2,122},{3,1},{4,124},{5,3},{6,126},{7,5},{8,0},{9,1... | collective-permute-start | bytes 147464 | tf_op jit(solution)/shard_map/ppermute | solution.py:661
  77.6 1.7 %collective-permute-start.12 = (f32[96,128]{1,0:T(8,128)S(1)}, f32[96,128]{1,0:T(8,128)S(1)}, u32[]{:S(2)}, u32[]{:S(2)}) collective-permute-start(f32[96,128]{1,0:T(8,128)S(1)} %collective-permute-done.10.refs_8_), channel_id=1, source_target_pairs={{0,1},{1,0},{2,3},{3,2},{4,5},{5,4},{6,7},{7,6},{8,9},{9,8},{10,11... | collective-permute-start | bytes 147464 | tf_op jit(solution)/shard_map/ppermute | solution.py:650
  78.4 1.2 collective-permute-start.13
  115.0 10.3 %collective-permute-start.14 = (f32[64,8,128]{2,1,0:T(8,128)S(1)}, f32[64,8,128]{2,1,0:T(8,128)S(1)}, u32[]{:S(2)}, u32[]{:S(2)}) collective-permute-start(f32[64,8,128]{2,1,0:T(8,128)S(1)} %all_to_all.11.refs_6_), channel_id=1, source_target_pairs={{0,1},{1,0},{2,3},{3,2},{4,5},{5,4},{6,7},{7,6},{8,9},{9,8},{10,11... | collective-permute-start | bytes 786440 | tf_op jit(solution)/shard_map/ppermute | solution.py:650
  119.1 3.9 %collective-permute-start.15 = (f32[48,128]{1,0:T(8,128)S(1)}, f32[48,128]{1,0:T(8,128)S(1)}, u32[]{:S(2)}, u32[]{:S(2)}) collective-permute-start(f32[48,128]{1,0:T(8,128)S(1)} %get-tuple-element.41), channel_id=1, source_target_pairs={{0,8},{1,3},{2,10},{3,5},{4,12},{5,7},{6,14},{7,1},{8,16},{9,11},{... | collective-permute-start | bytes 73736 | tf_op jit(solution)/shard_map/ppermute | solution.py:661
  119.3 4.8 %collective-permute-start.16 = (f32[48,128]{1,0:T(8,128)S(1)}, f32[48,128]{1,0:T(8,128)S(1)}, u32[]{:S(2)}, u32[]{:S(2)}) collective-permute-start(f32[48,128]{1,0:T(8,128)S(1)} %get-tuple-element.42), channel_id=1, source_target_pairs={{0,120},{1,7},{2,122},{3,1},{4,124},{5,3},{6,126},{7,5},{8,0},{9,1... | collective-permute-start | bytes 73736 | tf_op jit(solution)/shard_map/ppermute | solution.py:661
  123.0 2.0 %collective-permute-start.17 = (f32[48,128]{1,0:T(8,128)S(1)}, f32[48,128]{1,0:T(8,128)S(1)}, u32[]{:S(2)}, u32[]{:S(2)}) collective-permute-start(f32[48,128]{1,0:T(8,128)S(1)} %collective-permute-done.15.refs_8_), channel_id=1, source_target_pairs={{0,1},{1,0},{2,3},{3,2},{4,5},{5,4},{6,7},{7,6},{8,9},{9,8},{10,11... | collective-permute-start | bytes 73736 | tf_op jit(solution)/shard_map/ppermute | solution.py:650
  124.1 1.2 collective-permute-start.18

commit v4 on v3

--- a/solution.py
+++ b/solution.py
@@ -18,6 +18,7 @@
 X0, Y0, XA0, YA0 = 12, 24, 40, 80
 X1, Y1, XA1, YA1 = 10, 16, 32, 48
 HALO = 10
+EDGES = (((4, 4), (4, 4)), ((1, 3), (2, 2)))
 
 
 def coefficients(level):
@@ -106,20 +107,25 @@
 
 
 def restrict_0(f1, t0, v, force, halo):
+    rows = BY + 4 * halo
+
     def body(q):
-        for j in range(Y0 - 8, Y0 + 40, 16):
+        for y in range(0, rows, 16):
+            count = min(16, rows - y)
+            j = Y0 - 2 * halo + y
             total = None
             for i in (X0 - 2 * halo + 2 * q, X0 - 2 * halo + 2 * q + 1):
-                centre, nb = beside_0(v, i, j, 16)
+                centre, nb = beside_0(v, i, j, count)
                 for h in range(2):
-                    r = residual_of(0, force[h][i, pl.ds(j, 16), :], centre[h], nb[h])
+                    r = residual_of(0, force[h][i, pl.ds(j, count), :], centre[h], nb[h])
                     total = r if total is None else total + r
-            t0[q, pl.ds(j - Y0 + 8, 16), :] = total
+            t0[q, pl.ds(y, count), :] = total
 
     layers = BX // 2 + 2 * halo
     over_layers(0, layers, layers // 2, body)
     for m in range(layers):
-        f1[X1 - halo + m, pl.ds(Y1 - 4, 24), :] = 0.125 * (t0[m, pl.ds(0, 24, stride=2), :] + t0[m, pl.ds(1, 24, stride=2), :])
+        pairs = [t0[m, pl.ds(k, rows // 2, stride=2), :] for k in range(2)]
+        f1[X1 - halo + m, pl.ds(Y1 - halo, rows // 2), :] = 0.125 * (pairs[0] + pairs[1])
 
 
 def mean_matrix(source_of_out, gap=1):
@@ -436,37 +442,42 @@
             )
 
 
-def lay_out_1(dst, f1, edges, core, own, width):
+def lay_out_1(dst, f1, edges, core, own, x_edges, y_edges):
     up, down = edges[0][...], edges[1][...]
     other_up, other_down = (pltpu.roll(edge[...], 64, 1) for edge in edges[2:])
     first = core == 0
     x_low, y_low = jnp.where(first, up, other_up), jnp.where(first, other_up, up)
     x_high, y_high = jnp.where(first, down, other_down), jnp.where(first, other_down, down)
+    past, width = y_edges
     for m in range(f1.shape[0]):
         i = X1 - own + m
         dst[i, pl.ds(Y1 - 4, 24), :] = f1[m]
-        dst[i, pl.ds(Y1 - own - width, width), :] = y_low[m * width : (m + 1) * width]
-        dst[i, pl.ds(Y1 + 16 + own, width), :] = y_high[m * width : (m + 1) * width]
+        dst[i, pl.ds(Y1 - past - width, width), :] = y_low[m * width : (m + 1) * width]
+        dst[i, pl.ds(Y1 + 16 + past, width), :] = y_high[m * width : (m + 1) * width]
+    past, width = x_edges
     for m in range(width):
-        dst[X1 - own - width + m, pl.ds(Y1 - 4, 24), :] = x_low[m * 24 : (m + 1) * 24]
-        dst[X1 + 8 + own + m, pl.ds(Y1 - 4, 24), :] = x_high[m * 24 : (m + 1) * 24]
-
-
-def put_out_1(out, up, down, f1, core, own, width):
+        known = slice(m * 24 + 4 - own, m * 24 + 20 + own)
+        dst[X1 - past - width + m, pl.ds(Y1 - own, 16 + 2 * own), :] = x_low[known]
+        dst[X1 + 8 + past + m, pl.ds(Y1 - own, 16 + 2 * own), :] = x_high[known]
+
+
+def put_out_1(out, up, down, f1, core, own, x_edges, y_edges):
     for m in range(out.shape[0]):
         out[m] = f1[X1 - own + m, pl.ds(Y1 - 4, 24), :]
 
     @pl.when(core == 0)
     def _():
+        past, width = x_edges
         for m in range(width):
-            up[pl.ds(m * 24, 24), :] = f1[X1 + 8 - own - width + m, pl.ds(Y1 - 4, 24), :]
-            down[pl.ds(m * 24, 24), :] = f1[X1 + own + m, pl.ds(Y1 - 4, 24), :]
+            up[pl.ds(m * 24, 24), :] = f1[X1 + 8 - past - width + m, pl.ds(Y1 - 4, 24), :]
+            down[pl.ds(m * 24, 24), :] = f1[X1 + past + m, pl.ds(Y1 - 4, 24), :]
 
     @pl.when(core == 1)
     def _():
+        past, width = y_edges
         for m in range(out.shape[0]):
-            up[pl.ds(m * width, width), :] = f1[X1 - own + m, pl.ds(Y1 + 16 - own - width, width), :]
-            down[pl.ds(m * width, width), :] = f1[X1 - own + m, pl.ds(Y1 + own, width), :]
+            up[pl.ds(m * width, width), :] = f1[X1 - own + m, pl.ds(Y1 + 16 - past - width, width), :]
+            down[pl.ds(m * width, width), :] = f1[X1 - own + m, pl.ds(Y1 + past, width), :]
 
 
 def split_kernel(charge, mine, up, down):
@@ -517,7 +528,7 @@
     start_0(v, force, 9, 17)
     restrict_0(f1, t0, v, force, 4)
     coarse_source(send, f1, v1, r1, core)
-    put_out_1(*f1_outs, f1, core, 4, 4)
+    put_out_1(*f1_outs, f1, core, 4, *EDGES[0])
 
 
 def middle_kernel(where, *refs):
@@ -528,7 +539,7 @@
     force, v, a0, b0 = (f_e, f_o), (v_e, v_o), (a_e, a_o), (b_e, b_o)
     unpack_2(f2, mine, other, core)
     level_2(near, f2, v2, t2, t3, s3, p2, a2, b2, bottom, gx, 4)
-    lay_out_1(f1, f1_in, edges, core, 4, 4)
+    lay_out_1(f1, f1_in, edges, core, 4, *EDGES[0])
     start_1(v1, f1, 7, 12)
     add_from_2(v1, near, y2, p1, gy, core, 4)
     sweep_1(r1, v1, f1, 6, 12)
@@ -540,7 +551,7 @@
     sweep_0(a0, b0, force, 5, 13)
     restrict_0(f1, t0, a0, force, 2)
     coarse_source(send, f1, v1, r1, core)
-    put_out_1(*f1_outs, f1, core, 2, 2)
+    put_out_1(*f1_outs, f1, core, 2, *EDGES[1])
     for src, dst in ((a_e, n_e), (a_o, n_o)):
         dst[...] = src[pl.ds(X0 - 2, 20), pl.ds(Y0 - 8, 48), :]
 
@@ -552,7 +563,7 @@
     force, v, a0, b0 = (f_e, f_o), (n_e, n_o), (a_e, a_o), (b_e, b_o)
     unpack_2(f2, mine, other, core)
     level_2(near, f2, v2, t2, t3, s3, p2, a2, b2, bottom, gx, 2)
-    lay_out_1(f1, f1_in, edges, core, 2, 2)
+    lay_out_1(f1, f1_in, edges, core, 2, *EDGES[1])
     start_1(v1, f1, 3, 14)
     add_from_2(v1, near, y2, p1, gy, core, 2)
     sweep_1(r1, v1, f1, 2, 12)
@@ -629,13 +640,13 @@
 
 
 def first(*args):
-    outs = [kept(XA0, YA0, LANES)] * 4 + sources_out(16, 4)
+    outs = [kept(XA0, YA0, LANES)] * 4 + sources_out(16, EDGES[0][0][1])
     scratch = [vm(XA1, YA1, LANES)] * 3 + [vm(16, 48, LANES)]
     return run(functools.partial(first_kernel, where_am_i), outs, scratch, 10**7, *args)
 
 
 def middle(*args):
-    outs = [kept(20, 48, LANES)] * 2 + sources_out(12, 2)
+    outs = [kept(20, 48, LANES)] * 2 + sources_out(12, EDGES[1][0][1])
     return run(functools.partial(middle_kernel, where_am_i), outs, scratch_for_cycle(), 4 * 10**7, *args)
 
 

time: 132 us -> 132 us (level)
  no operation moved by 1% of the time
where the time goes in v4:
time: 132 us
  blocking collectives  54.2 us (41%)
  starting transfers between devices  45.3 us (34%)
  Pallas kernels  18.5 us (14%)
  waiting for transfers between devices  13 us (10%)
    all_to_all x2, blocking collectives, exchange(): mine = lax.all_to_all(send, ('gx', 'gy'), 0, 0, tiled=True)  54.2 us
    ppermute x15, starting transfers between devices, from_(): lax.ppermute(value, axis, [(i, (i + step) % size) for i in range(size)])  39.9 us
    pallas_call x5, Pallas kernels, run(): pl.pallas_call(kernel, out_shape=outs, out_specs=[spec] * len(outs) if is...  18.5 us
    ppermute x15, waiting for transfers between devices, from_(): lax.ppermute(value, axis, [(i, (i + step) % size) for i in range(size)])  9.88 us
    ppermute x4, starting transfers between devices, beside_(): return lax.ppermute(value, axes, pairs)  5.35 us
    ppermute x4, waiting for transfers between devices, beside_(): return lax.ppermute(value, axes, pairs)  3.12 us
  transfers between devices with their start and end apart: 19, of which 10 were waited for; matrix products, arithmetic and copies ran while one was open for 0% of the time, Pallas kernels for 0%

profile of v4, /device:TPU:33, one launch (start us, length us, event | category | flops | bytes accessed | tf_op | source)
XLA Modules:
  0.0 132.2 jit_solution(13395626660124788089)
XLA Ops:
  0.0 0.0 copy-start
  0.0 0.0 copy-start.1
  0.0 1.0 copy-done.1
  1.0 0.3 shard_map.28
  1.3 3.4 %collective-permute-start = (f32[10,32,128]{2,1,0:T(8,128)S(1)}, f32[10,32,128]{2,1,0:T(8,128)S(1)}, u32[]{:S(2)}, u32[]{:S(2)}) collective-permute-start(f32[10,32,128]{2,1,0:T(8,128)S(1)} %get-tuple-element.25), channel_id=1, source_target_pairs={{0,8},{8,16},{16,24},{24,32},{32,40},{40,48},{48,56},{56,64},{64,7... | collective-permute-start | bytes 491528 | tf_op jit(solution)/shard_map/ppermute | solution.py:661
  4.7 19.7 %collective-permute-start.1 = (f32[10,32,128]{2,1,0:T(8,128)S(1)}, f32[10,32,128]{2,1,0:T(8,128)S(1)}, u32[]{:S(2)}, u32[]{:S(2)}) collective-permute-start(f32[10,32,128]{2,1,0:T(8,128)S(1)} %get-tuple-element.26), channel_id=1, source_target_pairs={{0,120},{8,0},{16,8},{24,16},{32,24},{40,32},{48,40},{56,48},{64,5... | collective-permute-start | bytes 491528 | tf_op jit(solution)/shard_map/ppermute | solution.py:661
  24.4 3.8 %collective-permute-done.x_low.refs_1_ = f32[10,32,128]{2,1,0:T(8,128)S(1)} collective-permute-done((f32[10,32,128]{2,1,0:T(8,128)S(1)}, f32[10,32,128]{2,1,0:T(8,128)S(1)}, u32[]{:S(2)}, u32[]{:S(2)}) %collective-permute-start) | collective-permute-done | bytes 163872 | tf_op jit(solution)/shard_map/ppermute | solution.py:661
  28.3 0.0 collective-permute-done.1.x_high.refs_2_
  28.3 1.5 %collective-permute-start.2 = (f32[360,128]{1,0:T(8,128)S(1)}, f32[360,128]{1,0:T(8,128)S(1)}, u32[]{:S(2)}, u32[]{:S(2)}) collective-permute-start(f32[360,128]{1,0:T(8,128)S(1)} %get-tuple-element.27), channel_id=1, source_target_pairs={{0,2},{2,4},{4,6},{6,0},{1,3},{3,5},{5,7},{7,1},{8,10},{10,12},{12... | collective-permute-start | bytes 552968 | tf_op jit(solution)/shard_map/ppermute | solution.py:661
  29.8 1.7 %collective-permute-start.3 = (f32[360,128]{1,0:T(8,128)S(1)}, f32[360,128]{1,0:T(8,128)S(1)}, u32[]{:S(2)}, u32[]{:S(2)}) collective-permute-start(f32[360,128]{1,0:T(8,128)S(1)} %get-tuple-element.28), channel_id=1, source_target_pairs={{0,6},{2,0},{4,2},{6,4},{1,7},{3,1},{5,3},{7,5},{8,14},{10,8},{12,... | collective-permute-start | bytes 552968 | tf_op jit(solution)/shard_map/ppermute | solution.py:661
  31.5 1.5 %collective-permute-start.4 = (f32[16,32,128]{2,1,0:T(8,128)S(1)}, f32[16,32,128]{2,1,0:T(8,128)S(1)}, u32[]{:S(2)}, u32[]{:S(2)}) collective-permute-start(f32[16,32,128]{2,1,0:T(8,128)S(1)} %get-tuple-element.24.mine.refs_0_), channel_id=1, source_target_pairs={{0,1},{1,0},{2,3},{3,2},{4,5},{5,4},{6,7},{7,6},{8,9},{9,8},{10,11... | collective-permute-start | bytes 786440 | tf_op jit(solution)/shard_map/ppermute | solution.py:661
  32.9 2.2 %collective-permute-done.2.refs_3_ = f32[360,128]{1,0:T(8,128)S(1)} collective-permute-done((f32[360,128]{1,0:T(8,128)S(1)}, f32[360,128]{1,0:T(8,128)S(1)}, u32[]{:S(2)}, u32[]{:S(2)}) %collective-permute-start.2) | collective-permute-done | bytes 184352 | tf_op jit(solution)/shard_map/ppermute | solution.py:661
  35.1 1.8 %collective-permute-start.7 = (f32[360,128]{1,0:T(8,128)S(1)}, f32[360,128]{1,0:T(8,128)S(1)}, u32[]{:S(2)}, u32[]{:S(2)}) collective-permute-start(f32[360,128]{1,0:T(8,128)S(1)} %collective-permute-done.2.refs_3_), channel_id=1, source_target_pairs={{0,1},{1,0},{2,3},{3,2},{4,5},{5,4},{6,7},{7,6},{8,9},{9,8},{10,11... | collective-permute-start | bytes 552968 | tf_op jit(solution)/shard_map/ppermute | solution.py:661
  36.9 0.0 collective-permute-done.3.refs_4_
  36.9 0.0 collective-permute-start.8
  36.9 0.5 collective-permute-start.5
  37.4 0.0 collective-permute-start.6
  37.4 0.0 collective-permute-done.4.refs_5_
  37.4 1.1 collective-permute-done.5.refs_6_
  38.6 0.2 collective-permute-done.6.refs_7_
  38.8 0.0 collective-permute-done.7.refs_8_
  38.8 0.0 collective-permute-done.8.refs_9_
  38.8 2.7 %shard_map.30 = (f32[40,80,128]{2,1,0:T(8,128)S(1)}, f32[40,80,128]{2,1,0:T(8,128)S(1)}, f32[40,80,128]{2,1,0:T(8,128)S(1)}, f32[40,80,128]{2,1,0:T(8,128)S(1)},...) custom-call(f32[16,32,128]{2,1,0:T(8,128)S(1)} %get-tuple-element.24.min, ...), custom_call_target="tpu_custom_call" | custom-call | flops 10000000 | bytes 1048576 | tf_op jit(solution)/shard_map/pallas_call | solution.py:612
  41.6 27.9 %all_to_all.10.refs_6_ = f32[64,8,128]{2,1,0:T(8,128)S(1)} all-to-all(f32[64,8,128]{2,1,0:T(8,128)S(1)} %get-tuple-element.34), channel_id=1, replica_groups=mesh['groups'=2,'gx'=16,'gy'=4,'gz'=2] {'gx','gy'}, dimensions={0} | all-to-all | bytes 524288 | tf_op jit(solution)/shard_map/all_to_all | solution.py:677
  69.5 3.7 %collective-permute-start.9 = (f32[64,8,128]{2,1,0:T(8,128)S(1)}, f32[64,8,128]{2,1,0:T(8,128)S(1)}, u32[]{:S(2)}, u32[]{:S(2)}) collective-permute-start(f32[64,8,128]{2,1,0:T(8,128)S(1)} %all_to_all.10.refs_6_), channel_id=1, source_target_pairs={{0,1},{1,0},{2,3},{3,2},{4,5},{5,4},{6,7},{7,6},{8,9},{9,8},{10,11... | collective-permute-start | bytes 786440 | tf_op jit(solution)/shard_map/ppermute | solution.py:661
  73.2 0.2 collective-permute-start.10
  73.5 2.4 %collective-permute-start.11 = (f32[96,128]{1,0:T(8,128)S(1)}, f32[96,128]{1,0:T(8,128)S(1)}, u32[]{:S(2)}, u32[]{:S(2)}) collective-permute-start(f32[96,128]{1,0:T(8,128)S(1)} %get-tuple-element.36), channel_id=1, source_target_pairs={{0,120},{1,7},{2,122},{3,1},{4,124},{5,3},{6,126},{7,5},{8,0},{9,1... | collective-permute-start | bytes 147464 | tf_op jit(solution)/shard_map/ppermute | solution.py:672
  75.9 1.8 %collective-permute-done.10.refs_8_ = f32[96,128]{1,0:T(8,128)S(1)} collective-permute-done((f32[96,128]{1,0:T(8,128)S(1)}, f32[96,128]{1,0:T(8,128)S(1)}, u32[]{:S(2)}, u32[]{:S(2)}) %collective-permute-start.10) | collective-permute-done | bytes 49184 | tf_op jit(solution)/shard_map/ppermute | solution.py:672
  77.7 0.9 collective-permute-start.12
  78.5 0.0 collective-permute-done.11.refs_9_
  78.6 0.0 collective-permute-start.13
  78.6 0.9 collective-permute-done.12.refs_10_
  79.4 0.4 collective-permute-done.13.refs_11_
  79.8 0.0 collective-permute-done.9.refs_7_
  79.8 0.0 copy-done
  79.8 9.4 %shard_map.31 = (f32[20,48,128]{2,1,0:T(8,128)S(1)}, f32[20,48,128]{2,1,0:T(8,128)S(1)}, f32[64,8,128]{2,1,0:T(8,128)S(1)}, f32[12,24,128]{2,1,0:T(8,128)S(1)}, ...) custom-call(f32[256,256]{1,0:T(8,128)S(1)} %copy-done, f32[40,80,128]{2,1,0:T(8,128)S(1)} %get-tuple-element.29.refs_1_, ...), custom_call_target="tpu_custom_call" | custom-call | flops 40000000 | bytes 1048576 | tf_op jit(solution)/shard_map/pallas_call | solution.py:612
  89.2 26.3 %all_to_all.11.refs_6_ = f32[64,8,128]{2,1,0:T(8,128)S(1)} all-to-all(f32[64,8,128]{2,1,0:T(8,128)S(1)} %get-tuple-element.40), channel_id=1, replica_groups=mesh['groups'=2,'gx'=16,'gy'=4,'gz'=2] {'gx','gy'}, dimensions={0} | all-to-all | bytes 524288 | tf_op jit(solution)/shard_map/all_to_all | solution.py:677
  115.5 4.1 %collective-permute-start.14 = (f32[64,8,128]{2,1,0:T(8,128)S(1)}, f32[64,8,128]{2,1,0:T(8,128)S(1)}, u32[]{:S(2)}, u32[]{:S(2)}) collective-permute-start(f32[64,8,128]{2,1,0:T(8,128)S(1)} %all_to_all.11.refs_6_), channel_id=1, source_target_pairs={{0,1},{1,0},{2,3},{3,2},{4,5},{5,4},{6,7},{7,6},{8,9},{9,8},{10,11... | collective-permute-start | bytes 786440 | tf_op jit(solution)/shard_map/ppermute | solution.py:661
  119.6 0.2 collective-permute-start.15
  119.8 2.4 %collective-permute-start.16 = (f32[72,128]{1,0:T(8,128)S(1)}, f32[72,128]{1,0:T(8,128)S(1)}, u32[]{:S(2)}, u32[]{:S(2)}) collective-permute-start(f32[72,128]{1,0:T(8,128)S(1)} %get-tuple-element.42), channel_id=1, source_target_pairs={{0,120},{1,7},{2,122},{3,1},{4,124},{5,3},{6,126},{7,5},{8,0},{9,1... | collective-permute-start | bytes 110600 | tf_op jit(solution)/shard_map/ppermute | solution.py:672
  122.2 1.3 %collective-permute-done.15.refs_8_ = f32[72,128]{1,0:T(8,128)S(1)} collective-permute-done((f32[72,128]{1,0:T(8,128)S(1)}, f32[72,128]{1,0:T(8,128)S(1)}, u32[]{:S(2)}, u32[]{:S(2)}) %collective-permute-start.15) | collective-permute-done | bytes 36896 | tf_op jit(solution)/shard_map/ppermute | solution.py:672
  123.6 1.2 collective-permute-start.17
  124.7 0.0 collective-permute-done.16.refs_9_
  124.7 0.0 collective-permute-start.18
  124.7 0.9 collective-permute-done.17.refs_10_
  125.6 0.4 collective-permute-done.18.refs_11_
  126.0 0.0 collective-permute-done.14.refs_7_
  126.0 6.1 %shard_map.32 = f32[16,32,128]{2,1,0:T(8,128)} custom-call(f32[256,256]{1,0:T(8,128)S(1)} %copy-done, f32[40,80,128]{2,1,0:T(8,128)S(1)} %get-tuple-element.29.refs_1_, f32[40,80,128]{2,1,0:T(8,128)S(1)} %get-tuple-element.30.refs_2_, f32[20,48,128]{2,1,0:T(8,128)S(1)} %get-tuple-element.37.refs_3_, f32[20,48,128]{2,1,0:T(8,128)S(1)} %get-tuple-element.38.refs_4_, ...), custom_call_target="tpu_custom_call" | custom-call | flops 20000000 | bytes 1048576 | tf_op jit(solution)/shard_map/pallas_call | solution.py:612
  (1 shorter events, 0.0 us)
Async XLA Ops:
  0.0 79.8 %copy-start = (f32[256,256]{1,0:T(8,128)S(1)}, f32[256,256]{1,0:T(8,128)}, u32[]{:S(2)}) copy-start(f32[256,256]{1,0:T(8,128)} %constant.2.clone.refs_0_) | copy-start | bytes 786436
  0.0 1.0 copy-start.1
  1.3 27.0 %collective-permute-start = (f32[10,32,128]{2,1,0:T(8,128)S(1)}, f32[10,32,128]{2,1,0:T(8,128)S(1)}, u32[]{:S(2)}, u32[]{:S(2)}) collective-permute-start(f32[10,32,128]{2,1,0:T(8,128)S(1)} %get-tuple-element.25), channel_id=1, source_target_pairs={{0,8},{8,16},{16,24},{24,32},{32,40},{40,48},{48,56},{56,64},{64,7... | collective-permute-start | bytes 491528 | tf_op jit(solution)/shard_map/ppermute | solution.py:661
  4.7 23.6 %collective-permute-start.1 = (f32[10,32,128]{2,1,0:T(8,128)S(1)}, f32[10,32,128]{2,1,0:T(8,128)S(1)}, u32[]{:S(2)}, u32[]{:S(2)}) collective-permute-start(f32[10,32,128]{2,1,0:T(8,128)S(1)} %get-tuple-element.26), channel_id=1, source_target_pairs={{0,120},{8,0},{16,8},{24,16},{32,24},{40,32},{48,40},{56,48},{64,5... | collective-permute-start | bytes 491528 | tf_op jit(solution)/shard_map/ppermute | solution.py:661
  28.3 6.8 %collective-permute-start.2 = (f32[360,128]{1,0:T(8,128)S(1)}, f32[360,128]{1,0:T(8,128)S(1)}, u32[]{:S(2)}, u32[]{:S(2)}) collective-permute-start(f32[360,128]{1,0:T(8,128)S(1)} %get-tuple-element.27), channel_id=1, source_target_pairs={{0,2},{2,4},{4,6},{6,0},{1,3},{3,5},{5,7},{7,1},{8,10},{10,12},{12... | collective-permute-start | bytes 552968 | tf_op jit(solution)/shard_map/ppermute | solution.py:661
  29.8 7.1 %collective-permute-start.3 = (f32[360,128]{1,0:T(8,128)S(1)}, f32[360,128]{1,0:T(8,128)S(1)}, u32[]{:S(2)}, u32[]{:S(2)}) collective-permute-start(f32[360,128]{1,0:T(8,128)S(1)} %get-tuple-element.28), channel_id=1, source_target_pairs={{0,6},{2,0},{4,2},{6,4},{1,7},{3,1},{5,3},{7,5},{8,14},{10,8},{12,... | collective-permute-start | bytes 552968 | tf_op jit(solution)/shard_map/ppermute | solution.py:661
  31.5 6.0 %collective-permute-start.4 = (f32[16,32,128]{2,1,0:T(8,128)S(1)}, f32[16,32,128]{2,1,0:T(8,128)S(1)}, u32[]{:S(2)}, u32[]{:S(2)}) collective-permute-start(f32[16,32,128]{2,1,0:T(8,128)S(1)} %get-tuple-element.24.mine.refs_0_), channel_id=1, source_target_pairs={{0,1},{1,0},{2,3},{3,2},{4,5},{5,4},{6,7},{7,6},{8,9},{9,8},{10,11... | collective-permute-start | bytes 786440 | tf_op jit(solution)/shard_map/ppermute | solution.py:661
  35.1 3.7 %collective-permute-start.7 = (f32[360,128]{1,0:T(8,128)S(1)}, f32[360,128]{1,0:T(8,128)S(1)}, u32[]{:S(2)}, u32[]{:S(2)}) collective-permute-start(f32[360,128]{1,0:T(8,128)S(1)} %collective-permute-done.2.refs_3_), channel_id=1, source_target_pairs={{0,1},{1,0},{2,3},{3,2},{4,5},{5,4},{6,7},{7,6},{8,9},{9,8},{10,11... | collective-permute-start | bytes 552968 | tf_op jit(solution)/shard_map/ppermute | solution.py:661
  36.9 1.9 %collective-permute-start.8 = (f32[360,128]{1,0:T(8,128)S(1)}, f32[360,128]{1,0:T(8,128)S(1)}, u32[]{:S(2)}, u32[]{:S(2)}) collective-permute-start(f32[360,128]{1,0:T(8,128)S(1)} %collective-permute-done.3.refs_4_), channel_id=1, source_target_pairs={{0,1},{1,0},{2,3},{3,2},{4,5},{5,4},{6,7},{7,6},{8,9},{9,8},{10,11... | collective-permute-start | bytes 552968 | tf_op jit(solution)/shard_map/ppermute | solution.py:661
  36.9 1.7 %collective-permute-start.5 = (f32[10,32,128]{2,1,0:T(8,128)S(1)}, f32[10,32,128]{2,1,0:T(8,128)S(1)}, u32[]{:S(2)}, u32[]{:S(2)}) collective-permute-start(f32[10,32,128]{2,1,0:T(8,128)S(1)} %collective-permute-done.x_low.refs_1_), channel_id=1, source_target_pairs={{0,1},{1,0},{2,3},{3,2},{4,5},{5,4},{6,7},{7,6},{8,9},{9,8},{10,11... | collective-permute-start | bytes 491528 | tf_op jit(solution)/shard_map/ppermute | solution.py:661
  37.4 1.4 %collective-permute-start.6 = (f32[10,32,128]{2,1,0:T(8,128)S(1)}, f32[10,32,128]{2,1,0:T(8,128)S(1)}, u32[]{:S(2)}, u32[]{:S(2)}) collective-permute-start(f32[10,32,128]{2,1,0:T(8,128)S(1)} %collective-permute-done.1.x_high.refs_2_), channel_id=1, source_target_pairs={{0,1},{1,0},{2,3},{3,2},{4,5},{5,4},{6,7},{7,6},{8,9},{9,8},{10,11... | collective-permute-start | bytes 491528 | tf_op jit(solution)/shard_map/ppermute | solution.py:661
  69.5 10.3 %collective-permute-start.9 = (f32[64,8,128]{2,1,0:T(8,128)S(1)}, f32[64,8,128]{2,1,0:T(8,128)S(1)}, u32[]{:S(2)}, u32[]{:S(2)}) collective-permute-start(f32[64,8,128]{2,1,0:T(8,128)S(1)} %all_to_all.10.refs_6_), channel_id=1, source_target_pairs={{0,1},{1,0},{2,3},{3,2},{4,5},{5,4},{6,7},{7,6},{8,9},{9,8},{10,11... | collective-permute-start | bytes 786440 | tf_op jit(solution)/shard_map/ppermute | solution.py:661
  73.2 4.4 %collective-permute-start.10 = (f32[96,128]{1,0:T(8,128)S(1)}, f32[96,128]{1,0:T(8,128)S(1)}, u32[]{:S(2)}, u32[]{:S(2)}) collective-permute-start(f32[96,128]{1,0:T(8,128)S(1)} %get-tuple-element.35), channel_id=1, source_target_pairs={{0,8},{1,3},{2,10},{3,5},{4,12},{5,7},{6,14},{7,1},{8,16},{9,11},{... | collective-permute-start | bytes 147464 | tf_op jit(solution)/shard_map/ppermute | solution.py:672
  73.5 5.1 %collective-permute-start.11 = (f32[96,128]{1,0:T(8,128)S(1)}, f32[96,128]{1,0:T(8,128)S(1)}, u32[]{:S(2)}, u32[]{:S(2)}) collective-permute-start(f32[96,128]{1,0:T(8,128)S(1)} %get-tuple-element.36), channel_id=1, source_target_pairs={{0,120},{1,7},{2,122},{3,1},{4,124},{5,3},{6,126},{7,5},{8,0},{9,1... | collective-permute-start | bytes 147464 | tf_op jit(solution)/shard_map/ppermute | solution.py:672
  77.7 1.7 %collective-permute-start.12 = (f32[96,128]{1,0:T(8,128)S(1)}, f32[96,128]{1,0:T(8,128)S(1)}, u32[]{:S(2)}, u32[]{:S(2)}) collective-permute-start(f32[96,128]{1,0:T(8,128)S(1)} %collective-permute-done.10.refs_8_), channel_id=1, source_target_pairs={{0,1},{1,0},{2,3},{3,2},{4,5},{5,4},{6,7},{7,6},{8,9},{9,8},{10,11... | collective-permute-start | bytes 147464 | tf_op jit(solution)/shard_map/ppermute | solution.py:661
  78.6 1.2 collective-permute-start.13
  115.5 10.5 %collective-permute-start.14 = (f32[64,8,128]{2,1,0:T(8,128)S(1)}, f32[64,8,128]{2,1,0:T(8,128)S(1)}, u32[]{:S(2)}, u32[]{:S(2)}) collective-permute-start(f32[64,8,128]{2,1,0:T(8,128)S(1)} %all_to_all.11.refs_6_), channel_id=1, source_target_pairs={{0,1},{1,0},{2,3},{3,2},{4,5},{5,4},{6,7},{7,6},{8,9},{9,8},{10,11... | collective-permute-start | bytes 786440 | tf_op jit(solution)/shard_map/ppermute | solution.py:661
  119.6 4.0 %collective-permute-start.15 = (f32[72,128]{1,0:T(8,128)S(1)}, f32[72,128]{1,0:T(8,128)S(1)}, u32[]{:S(2)}, u32[]{:S(2)}) collective-permute-start(f32[72,128]{1,0:T(8,128)S(1)} %get-tuple-element.41), channel_id=1, source_target_pairs={{0,8},{1,3},{2,10},{3,5},{4,12},{5,7},{6,14},{7,1},{8,16},{9,11},{... | collective-permute-start | bytes 110600 | tf_op jit(solution)/shard_map/ppermute | solution.py:672
  119.8 4.9 %collective-permute-start.16 = (f32[72,128]{1,0:T(8,128)S(1)}, f32[72,128]{1,0:T(8,128)S(1)}, u32[]{:S(2)}, u32[]{:S(2)}) collective-permute-start(f32[72,128]{1,0:T(8,128)S(1)} %get-tuple-element.42), channel_id=1, source_target_pairs={{0,120},{1,7},{2,122},{3,1},{4,124},{5,3},{6,126},{7,5},{8,0},{9,1... | collective-permute-start | bytes 110600 | tf_op jit(solution)/shard_map/ppermute | solution.py:672
  123.6 2.0 %collective-permute-start.17 = (f32[72,128]{1,0:T(8,128)S(1)}, f32[72,128]{1,0:T(8,128)S(1)}, u32[]{:S(2)}, u32[]{:S(2)}) collective-permute-start(f32[72,128]{1,0:T(8,128)S(1)} %collective-permute-done.15.refs_8_), channel_id=1, source_target_pairs={{0,1},{1,0},{2,3},{3,2},{4,5},{5,4},{6,7},{7,6},{8,9},{9,8},{10,11... | collective-permute-start | bytes 110600 | tf_op jit(solution)/shard_map/ppermute | solution.py:661
  124.7 1.2 collective-permute-start.18

commit v5 on v4

--- a/solution.py
+++ b/solution.py
@@ -107,25 +107,20 @@
 
 
 def restrict_0(f1, t0, v, force, halo):
-    rows = BY + 4 * halo
-
     def body(q):
-        for y in range(0, rows, 16):
-            count = min(16, rows - y)
-            j = Y0 - 2 * halo + y
+        for j in range(Y0 - 8, Y0 + 40, 16):
             total = None
             for i in (X0 - 2 * halo + 2 * q, X0 - 2 * halo + 2 * q + 1):
-                centre, nb = beside_0(v, i, j, count)
+                centre, nb = beside_0(v, i, j, 16)
                 for h in range(2):
-                    r = residual_of(0, force[h][i, pl.ds(j, count), :], centre[h], nb[h])
+                    r = residual_of(0, force[h][i, pl.ds(j, 16), :], centre[h], nb[h])
                     total = r if total is None else total + r
-            t0[q, pl.ds(y, count), :] = total
+            t0[q, pl.ds(j - Y0 + 8, 16), :] = total
 
     layers = BX // 2 + 2 * halo
     over_layers(0, layers, layers // 2, body)
     for m in range(layers):
-        pairs = [t0[m, pl.ds(k, rows // 2, stride=2), :] for k in range(2)]
-        f1[X1 - halo + m, pl.ds(Y1 - halo, rows // 2), :] = 0.125 * (pairs[0] + pairs[1])
+        f1[X1 - halo + m, pl.ds(Y1 - 4, 24), :] = 0.125 * (t0[m, pl.ds(0, 24, stride=2), :] + t0[m, pl.ds(1, 24, stride=2), :])
 
 
 def mean_matrix(source_of_out, gap=1):

time: 132 us -> 132 us (level)
  no operation moved by 1% of the time
where the time goes in v5:
time: 132 us
  blocking collectives  54.2 us (41%)
  starting transfers between devices  45.3 us (34%)
  Pallas kernels  18.6 us (14%)
  waiting for transfers between devices  13 us (10%)
    all_to_all x2, blocking collectives, exchange(): mine = lax.all_to_all(send, ('gx', 'gy'), 0, 0, tiled=True)  54.2 us
    ppermute x15, starting transfers between devices, from_(): lax.ppermute(value, axis, [(i, (i + step) % size) for i in range(size)])  39.9 us
    pallas_call x5, Pallas kernels, run(): pl.pallas_call(kernel, out_shape=outs, out_specs=[spec] * len(outs) if is...  18.6 us
    ppermute x15, waiting for transfers between devices, from_(): lax.ppermute(value, axis, [(i, (i + step) % size) for i in range(size)])  9.88 us
    ppermute x4, starting transfers between devices, beside_(): return lax.ppermute(value, axes, pairs)  5.35 us
    ppermute x4, waiting for transfers between devices, beside_(): return lax.ppermute(value, axes, pairs)  3.12 us
  transfers between devices with their start and end apart: 19, of which 10 were waited for; matrix products, arithmetic and copies ran while one was open for 0% of the time, Pallas kernels for 0%

profile of v5, /device:TPU:33, one launch (start us, length us, event | category | flops | bytes accessed | tf_op | source)
XLA Modules:
  0.0 132.3 jit_solution(7844357386209880645)
XLA Ops:
  0.0 0.0 copy-start
  0.0 0.0 copy-start.1
  0.0 1.0 copy-done.1
  1.0 0.3 shard_map.28
  1.3 3.4 %collective-permute-start = (f32[10,32,128]{2,1,0:T(8,128)S(1)}, f32[10,32,128]{2,1,0:T(8,128)S(1)}, u32[]{:S(2)}, u32[]{:S(2)}) collective-permute-start(f32[10,32,128]{2,1,0:T(8,128)S(1)} %get-tuple-element.25), channel_id=1, source_target_pairs={{0,8},{8,16},{16,24},{24,32},{32,40},{40,48},{48,56},{56,64},{64,7... | collective-permute-start | bytes 491528 | tf_op jit(solution)/shard_map/ppermute | solution.py:656
  4.7 19.7 %collective-permute-start.1 = (f32[10,32,128]{2,1,0:T(8,128)S(1)}, f32[10,32,128]{2,1,0:T(8,128)S(1)}, u32[]{:S(2)}, u32[]{:S(2)}) collective-permute-start(f32[10,32,128]{2,1,0:T(8,128)S(1)} %get-tuple-element.26), channel_id=1, source_target_pairs={{0,120},{8,0},{16,8},{24,16},{32,24},{40,32},{48,40},{56,48},{64,5... | collective-permute-start | bytes 491528 | tf_op jit(solution)/shard_map/ppermute | solution.py:656
  24.4 3.8 %collective-permute-done.x_low.refs_1_ = f32[10,32,128]{2,1,0:T(8,128)S(1)} collective-permute-done((f32[10,32,128]{2,1,0:T(8,128)S(1)}, f32[10,32,128]{2,1,0:T(8,128)S(1)}, u32[]{:S(2)}, u32[]{:S(2)}) %collective-permute-start) | collective-permute-done | bytes 163872 | tf_op jit(solution)/shard_map/ppermute | solution.py:656
  28.3 0.0 collective-permute-done.1.x_high.refs_2_
  28.3 1.5 %collective-permute-start.2 = (f32[360,128]{1,0:T(8,128)S(1)}, f32[360,128]{1,0:T(8,128)S(1)}, u32[]{:S(2)}, u32[]{:S(2)}) collective-permute-start(f32[360,128]{1,0:T(8,128)S(1)} %get-tuple-element.27), channel_id=1, source_target_pairs={{0,2},{2,4},{4,6},{6,0},{1,3},{3,5},{5,7},{7,1},{8,10},{10,12},{12... | collective-permute-start | bytes 552968 | tf_op jit(solution)/shard_map/ppermute | solution.py:656
  29.8 1.7 %collective-permute-start.3 = (f32[360,128]{1,0:T(8,128)S(1)}, f32[360,128]{1,0:T(8,128)S(1)}, u32[]{:S(2)}, u32[]{:S(2)}) collective-permute-start(f32[360,128]{1,0:T(8,128)S(1)} %get-tuple-element.28), channel_id=1, source_target_pairs={{0,6},{2,0},{4,2},{6,4},{1,7},{3,1},{5,3},{7,5},{8,14},{10,8},{12,... | collective-permute-start | bytes 552968 | tf_op jit(solution)/shard_map/ppermute | solution.py:656
  31.5 1.5 %collective-permute-start.4 = (f32[16,32,128]{2,1,0:T(8,128)S(1)}, f32[16,32,128]{2,1,0:T(8,128)S(1)}, u32[]{:S(2)}, u32[]{:S(2)}) collective-permute-start(f32[16,32,128]{2,1,0:T(8,128)S(1)} %get-tuple-element.24.mine.refs_0_), channel_id=1, source_target_pairs={{0,1},{1,0},{2,3},{3,2},{4,5},{5,4},{6,7},{7,6},{8,9},{9,8},{10,11... | collective-permute-start | bytes 786440 | tf_op jit(solution)/shard_map/ppermute | solution.py:656
  32.9 2.2 %collective-permute-done.2.refs_3_ = f32[360,128]{1,0:T(8,128)S(1)} collective-permute-done((f32[360,128]{1,0:T(8,128)S(1)}, f32[360,128]{1,0:T(8,128)S(1)}, u32[]{:S(2)}, u32[]{:S(2)}) %collective-permute-start.2) | collective-permute-done | bytes 184352 | tf_op jit(solution)/shard_map/ppermute | solution.py:656
  35.1 1.8 %collective-permute-start.7 = (f32[360,128]{1,0:T(8,128)S(1)}, f32[360,128]{1,0:T(8,128)S(1)}, u32[]{:S(2)}, u32[]{:S(2)}) collective-permute-start(f32[360,128]{1,0:T(8,128)S(1)} %collective-permute-done.2.refs_3_), channel_id=1, source_target_pairs={{0,1},{1,0},{2,3},{3,2},{4,5},{5,4},{6,7},{7,6},{8,9},{9,8},{10,11... | collective-permute-start | bytes 552968 | tf_op jit(solution)/shard_map/ppermute | solution.py:656
  36.9 0.0 collective-permute-done.3.refs_4_
  36.9 0.0 collective-permute-start.8
  36.9 0.5 collective-permute-start.5
  37.4 0.0 collective-permute-start.6
  37.4 0.0 collective-permute-done.4.refs_5_
  37.4 1.1 collective-permute-done.5.refs_6_
  38.6 0.2 collective-permute-done.6.refs_7_
  38.8 0.0 collective-permute-done.7.refs_8_
  38.8 0.0 collective-permute-done.8.refs_9_
  38.8 2.7 %shard_map.30 = (f32[40,80,128]{2,1,0:T(8,128)S(1)}, f32[40,80,128]{2,1,0:T(8,128)S(1)}, f32[40,80,128]{2,1,0:T(8,128)S(1)}, f32[40,80,128]{2,1,0:T(8,128)S(1)},...) custom-call(f32[16,32,128]{2,1,0:T(8,128)S(1)} %get-tuple-element.24.min, ...), custom_call_target="tpu_custom_call" | custom-call | flops 10000000 | bytes 1048576 | tf_op jit(solution)/shard_map/pallas_call | solution.py:607
  41.6 27.9 %all_to_all.10.refs_6_ = f32[64,8,128]{2,1,0:T(8,128)S(1)} all-to-all(f32[64,8,128]{2,1,0:T(8,128)S(1)} %get-tuple-element.34), channel_id=1, replica_groups=mesh['groups'=2,'gx'=16,'gy'=4,'gz'=2] {'gx','gy'}, dimensions={0} | all-to-all | bytes 524288 | tf_op jit(solution)/shard_map/all_to_all | solution.py:672
  69.5 3.7 %collective-permute-start.9 = (f32[64,8,128]{2,1,0:T(8,128)S(1)}, f32[64,8,128]{2,1,0:T(8,128)S(1)}, u32[]{:S(2)}, u32[]{:S(2)}) collective-permute-start(f32[64,8,128]{2,1,0:T(8,128)S(1)} %all_to_all.10.refs_6_), channel_id=1, source_target_pairs={{0,1},{1,0},{2,3},{3,2},{4,5},{5,4},{6,7},{7,6},{8,9},{9,8},{10,11... | collective-permute-start | bytes 786440 | tf_op jit(solution)/shard_map/ppermute | solution.py:656
  73.2 0.2 collective-permute-start.10
  73.5 2.4 %collective-permute-start.11 = (f32[96,128]{1,0:T(8,128)S(1)}, f32[96,128]{1,0:T(8,128)S(1)}, u32[]{:S(2)}, u32[]{:S(2)}) collective-permute-start(f32[96,128]{1,0:T(8,128)S(1)} %get-tuple-element.36), channel_id=1, source_target_pairs={{0,120},{1,7},{2,122},{3,1},{4,124},{5,3},{6,126},{7,5},{8,0},{9,1... | collective-permute-start | bytes 147464 | tf_op jit(solution)/shard_map/ppermute | solution.py:667
  75.9 1.8 %collective-permute-done.10.refs_8_ = f32[96,128]{1,0:T(8,128)S(1)} collective-permute-done((f32[96,128]{1,0:T(8,128)S(1)}, f32[96,128]{1,0:T(8,128)S(1)}, u32[]{:S(2)}, u32[]{:S(2)}) %collective-permute-start.10) | collective-permute-done | bytes 49184 | tf_op jit(solution)/shard_map/ppermute | solution.py:667
  77.7 0.9 collective-permute-start.12
  78.5 0.0 collective-permute-done.11.refs_9_
  78.6 0.0 collective-permute-start.13
  78.6 0.9 collective-permute-done.12.refs_10_
  79.4 0.4 collective-permute-done.13.refs_11_
  79.8 0.0 collective-permute-done.9.refs_7_
  79.8 0.0 copy-done
  79.8 9.5 %shard_map.31 = (f32[20,48,128]{2,1,0:T(8,128)S(1)}, f32[20,48,128]{2,1,0:T(8,128)S(1)}, f32[64,8,128]{2,1,0:T(8,128)S(1)}, f32[12,24,128]{2,1,0:T(8,128)S(1)}, ...) custom-call(f32[256,256]{1,0:T(8,128)S(1)} %copy-done, f32[40,80,128]{2,1,0:T(8,128)S(1)} %get-tuple-element.29.refs_1_, ...), custom_call_target="tpu_custom_call" | custom-call | flops 40000000 | bytes 1048576 | tf_op jit(solution)/shard_map/pallas_call | solution.py:607
  89.3 26.3 %all_to_all.11.refs_6_ = f32[64,8,128]{2,1,0:T(8,128)S(1)} all-to-all(f32[64,8,128]{2,1,0:T(8,128)S(1)} %get-tuple-element.40), channel_id=1, replica_groups=mesh['groups'=2,'gx'=16,'gy'=4,'gz'=2] {'gx','gy'}, dimensions={0} | all-to-all | bytes 524288 | tf_op jit(solution)/shard_map/all_to_all | solution.py:672
  115.5 4.1 %collective-permute-start.14 = (f32[64,8,128]{2,1,0:T(8,128)S(1)}, f32[64,8,128]{2,1,0:T(8,128)S(1)}, u32[]{:S(2)}, u32[]{:S(2)}) collective-permute-start(f32[64,8,128]{2,1,0:T(8,128)S(1)} %all_to_all.11.refs_6_), channel_id=1, source_target_pairs={{0,1},{1,0},{2,3},{3,2},{4,5},{5,4},{6,7},{7,6},{8,9},{9,8},{10,11... | collective-permute-start | bytes 786440 | tf_op jit(solution)/shard_map/ppermute | solution.py:656
  119.6 0.2 collective-permute-start.15
  119.9 2.4 %collective-permute-start.16 = (f32[72,128]{1,0:T(8,128)S(1)}, f32[72,128]{1,0:T(8,128)S(1)}, u32[]{:S(2)}, u32[]{:S(2)}) collective-permute-start(f32[72,128]{1,0:T(8,128)S(1)} %get-tuple-element.42), channel_id=1, source_target_pairs={{0,120},{1,7},{2,122},{3,1},{4,124},{5,3},{6,126},{7,5},{8,0},{9,1... | collective-permute-start | bytes 110600 | tf_op jit(solution)/shard_map/ppermute | solution.py:667
  122.3 1.3 %collective-permute-done.15.refs_8_ = f32[72,128]{1,0:T(8,128)S(1)} collective-permute-done((f32[72,128]{1,0:T(8,128)S(1)}, f32[72,128]{1,0:T(8,128)S(1)}, u32[]{:S(2)}, u32[]{:S(2)}) %collective-permute-start.15) | collective-permute-done | bytes 36896 | tf_op jit(solution)/shard_map/ppermute | solution.py:667
  123.6 1.2 collective-permute-start.17
  124.8 0.0 collective-permute-done.16.refs_9_
  124.8 0.0 collective-permute-start.18
  124.8 0.9 collective-permute-done.17.refs_10_
  125.7 0.4 collective-permute-done.18.refs_11_
  126.0 0.0 collective-permute-done.14.refs_7_
  126.0 6.1 %shard_map.32 = f32[16,32,128]{2,1,0:T(8,128)} custom-call(f32[256,256]{1,0:T(8,128)S(1)} %copy-done, f32[40,80,128]{2,1,0:T(8,128)S(1)} %get-tuple-element.29.refs_1_, f32[40,80,128]{2,1,0:T(8,128)S(1)} %get-tuple-element.30.refs_2_, f32[20,48,128]{2,1,0:T(8,128)S(1)} %get-tuple-element.37.refs_3_, f32[20,48,128]{2,1,0:T(8,128)S(1)} %get-tuple-element.38.refs_4_, ...), custom_call_target="tpu_custom_call" | custom-call | flops 20000000 | bytes 1048576 | tf_op jit(solution)/shard_map/pallas_call | solution.py:607
  (1 shorter events, 0.0 us)
Async XLA Ops:
  0.0 79.8 %copy-start = (f32[256,256]{1,0:T(8,128)S(1)}, f32[256,256]{1,0:T(8,128)}, u32[]{:S(2)}) copy-start(f32[256,256]{1,0:T(8,128)} %constant.2.clone.refs_0_) | copy-start | bytes 786436
  0.0 1.0 copy-start.1
  1.3 27.0 %collective-permute-start = (f32[10,32,128]{2,1,0:T(8,128)S(1)}, f32[10,32,128]{2,1,0:T(8,128)S(1)}, u32[]{:S(2)}, u32[]{:S(2)}) collective-permute-start(f32[10,32,128]{2,1,0:T(8,128)S(1)} %get-tuple-element.25), channel_id=1, source_target_pairs={{0,8},{8,16},{16,24},{24,32},{32,40},{40,48},{48,56},{56,64},{64,7... | collective-permute-start | bytes 491528 | tf_op jit(solution)/shard_map/ppermute | solution.py:656
  4.7 23.6 %collective-permute-start.1 = (f32[10,32,128]{2,1,0:T(8,128)S(1)}, f32[10,32,128]{2,1,0:T(8,128)S(1)}, u32[]{:S(2)}, u32[]{:S(2)}) collective-permute-start(f32[10,32,128]{2,1,0:T(8,128)S(1)} %get-tuple-element.26), channel_id=1, source_target_pairs={{0,120},{8,0},{16,8},{24,16},{32,24},{40,32},{48,40},{56,48},{64,5... | collective-permute-start | bytes 491528 | tf_op jit(solution)/shard_map/ppermute | solution.py:656
  28.3 6.8 %collective-permute-start.2 = (f32[360,128]{1,0:T(8,128)S(1)}, f32[360,128]{1,0:T(8,128)S(1)}, u32[]{:S(2)}, u32[]{:S(2)}) collective-permute-start(f32[360,128]{1,0:T(8,128)S(1)} %get-tuple-element.27), channel_id=1, source_target_pairs={{0,2},{2,4},{4,6},{6,0},{1,3},{3,5},{5,7},{7,1},{8,10},{10,12},{12... | collective-permute-start | bytes 552968 | tf_op jit(solution)/shard_map/ppermute | solution.py:656
  29.8 7.1 %collective-permute-start.3 = (f32[360,128]{1,0:T(8,128)S(1)}, f32[360,128]{1,0:T(8,128)S(1)}, u32[]{:S(2)}, u32[]{:S(2)}) collective-permute-start(f32[360,128]{1,0:T(8,128)S(1)} %get-tuple-element.28), channel_id=1, source_target_pairs={{0,6},{2,0},{4,2},{6,4},{1,7},{3,1},{5,3},{7,5},{8,14},{10,8},{12,... | collective-permute-start | bytes 552968 | tf_op jit(solution)/shard_map/ppermute | solution.py:656
  31.5 6.0 %collective-permute-start.4 = (f32[16,32,128]{2,1,0:T(8,128)S(1)}, f32[16,32,128]{2,1,0:T(8,128)S(1)}, u32[]{:S(2)}, u32[]{:S(2)}) collective-permute-start(f32[16,32,128]{2,1,0:T(8,128)S(1)} %get-tuple-element.24.mine.refs_0_), channel_id=1, source_target_pairs={{0,1},{1,0},{2,3},{3,2},{4,5},{5,4},{6,7},{7,6},{8,9},{9,8},{10,11... | collective-permute-start | bytes 786440 | tf_op jit(solution)/shard_map/ppermute | solution.py:656
  35.1 3.7 %collective-permute-start.7 = (f32[360,128]{1,0:T(8,128)S(1)}, f32[360,128]{1,0:T(8,128)S(1)}, u32[]{:S(2)}, u32[]{:S(2)}) collective-permute-start(f32[360,128]{1,0:T(8,128)S(1)} %collective-permute-done.2.refs_3_), channel_id=1, source_target_pairs={{0,1},{1,0},{2,3},{3,2},{4,5},{5,4},{6,7},{7,6},{8,9},{9,8},{10,11... | collective-permute-start | bytes 552968 | tf_op jit(solution)/shard_map/ppermute | solution.py:656
  36.9 1.9 %collective-permute-start.8 = (f32[360,128]{1,0:T(8,128)S(1)}, f32[360,128]{1,0:T(8,128)S(1)}, u32[]{:S(2)}, u32[]{:S(2)}) collective-permute-start(f32[360,128]{1,0:T(8,128)S(1)} %collective-permute-done.3.refs_4_), channel_id=1, source_target_pairs={{0,1},{1,0},{2,3},{3,2},{4,5},{5,4},{6,7},{7,6},{8,9},{9,8},{10,11... | collective-permute-start | bytes 552968 | tf_op jit(solution)/shard_map/ppermute | solution.py:656
  36.9 1.7 %collective-permute-start.5 = (f32[10,32,128]{2,1,0:T(8,128)S(1)}, f32[10,32,128]{2,1,0:T(8,128)S(1)}, u32[]{:S(2)}, u32[]{:S(2)}) collective-permute-start(f32[10,32,128]{2,1,0:T(8,128)S(1)} %collective-permute-done.x_low.refs_1_), channel_id=1, source_target_pairs={{0,1},{1,0},{2,3},{3,2},{4,5},{5,4},{6,7},{7,6},{8,9},{9,8},{10,11... | collective-permute-start | bytes 491528 | tf_op jit(solution)/shard_map/ppermute | solution.py:656
  37.4 1.4 %collective-permute-start.6 = (f32[10,32,128]{2,1,0:T(8,128)S(1)}, f32[10,32,128]{2,1,0:T(8,128)S(1)}, u32[]{:S(2)}, u32[]{:S(2)}) collective-permute-start(f32[10,32,128]{2,1,0:T(8,128)S(1)} %collective-permute-done.1.x_high.refs_2_), channel_id=1, source_target_pairs={{0,1},{1,0},{2,3},{3,2},{4,5},{5,4},{6,7},{7,6},{8,9},{9,8},{10,11... | collective-permute-start | bytes 491528 | tf_op jit(solution)/shard_map/ppermute | solution.py:656
  69.5 10.3 %collective-permute-start.9 = (f32[64,8,128]{2,1,0:T(8,128)S(1)}, f32[64,8,128]{2,1,0:T(8,128)S(1)}, u32[]{:S(2)}, u32[]{:S(2)}) collective-permute-start(f32[64,8,128]{2,1,0:T(8,128)S(1)} %all_to_all.10.refs_6_), channel_id=1, source_target_pairs={{0,1},{1,0},{2,3},{3,2},{4,5},{5,4},{6,7},{7,6},{8,9},{9,8},{10,11... | collective-permute-start | bytes 786440 | tf_op jit(solution)/shard_map/ppermute | solution.py:656
  73.2 4.4 %collective-permute-start.10 = (f32[96,128]{1,0:T(8,128)S(1)}, f32[96,128]{1,0:T(8,128)S(1)}, u32[]{:S(2)}, u32[]{:S(2)}) collective-permute-start(f32[96,128]{1,0:T(8,128)S(1)} %get-tuple-element.35), channel_id=1, source_target_pairs={{0,8},{1,3},{2,10},{3,5},{4,12},{5,7},{6,14},{7,1},{8,16},{9,11},{... | collective-permute-start | bytes 147464 | tf_op jit(solution)/shard_map/ppermute | solution.py:667
  73.5 5.1 %collective-permute-start.11 = (f32[96,128]{1,0:T(8,128)S(1)}, f32[96,128]{1,0:T(8,128)S(1)}, u32[]{:S(2)}, u32[]{:S(2)}) collective-permute-start(f32[96,128]{1,0:T(8,128)S(1)} %get-tuple-element.36), channel_id=1, source_target_pairs={{0,120},{1,7},{2,122},{3,1},{4,124},{5,3},{6,126},{7,5},{8,0},{9,1... | collective-permute-start | bytes 147464 | tf_op jit(solution)/shard_map/ppermute | solution.py:667
  77.7 1.7 %collective-permute-start.12 = (f32[96,128]{1,0:T(8,128)S(1)}, f32[96,128]{1,0:T(8,128)S(1)}, u32[]{:S(2)}, u32[]{:S(2)}) collective-permute-start(f32[96,128]{1,0:T(8,128)S(1)} %collective-permute-done.10.refs_8_), channel_id=1, source_target_pairs={{0,1},{1,0},{2,3},{3,2},{4,5},{5,4},{6,7},{7,6},{8,9},{9,8},{10,11... | collective-permute-start | bytes 147464 | tf_op jit(solution)/shard_map/ppermute | solution.py:656
  78.6 1.2 collective-permute-start.13
  115.5 10.5 %collective-permute-start.14 = (f32[64,8,128]{2,1,0:T(8,128)S(1)}, f32[64,8,128]{2,1,0:T(8,128)S(1)}, u32[]{:S(2)}, u32[]{:S(2)}) collective-permute-start(f32[64,8,128]{2,1,0:T(8,128)S(1)} %all_to_all.11.refs_6_), channel_id=1, source_target_pairs={{0,1},{1,0},{2,3},{3,2},{4,5},{5,4},{6,7},{7,6},{8,9},{9,8},{10,11... | collective-permute-start | bytes 786440 | tf_op jit(solution)/shard_map/ppermute | solution.py:656
  119.6 4.0 %collective-permute-start.15 = (f32[72,128]{1,0:T(8,128)S(1)}, f32[72,128]{1,0:T(8,128)S(1)}, u32[]{:S(2)}, u32[]{:S(2)}) collective-permute-start(f32[72,128]{1,0:T(8,128)S(1)} %get-tuple-element.41), channel_id=1, source_target_pairs={{0,8},{1,3},{2,10},{3,5},{4,12},{5,7},{6,14},{7,1},{8,16},{9,11},{... | collective-permute-start | bytes 110600 | tf_op jit(solution)/shard_map/ppermute | solution.py:667
  119.9 4.9 %collective-permute-start.16 = (f32[72,128]{1,0:T(8,128)S(1)}, f32[72,128]{1,0:T(8,128)S(1)}, u32[]{:S(2)}, u32[]{:S(2)}) collective-permute-start(f32[72,128]{1,0:T(8,128)S(1)} %get-tuple-element.42), channel_id=1, source_target_pairs={{0,120},{1,7},{2,122},{3,1},{4,124},{5,3},{6,126},{7,5},{8,0},{9,1... | collective-permute-start | bytes 110600 | tf_op jit(solution)/shard_map/ppermute | solution.py:667
  123.6 2.0 %collective-permute-start.17 = (f32[72,128]{1,0:T(8,128)S(1)}, f32[72,128]{1,0:T(8,128)S(1)}, u32[]{:S(2)}, u32[]{:S(2)}) collective-permute-start(f32[72,128]{1,0:T(8,128)S(1)} %collective-permute-done.15.refs_8_), channel_id=1, source_target_pairs={{0,1},{1,0},{2,3},{3,2},{4,5},{5,4},{6,7},{7,6},{8,9},{9,8},{10,11... | collective-permute-start | bytes 110600 | tf_op jit(solution)/shard_map/ppermute | solution.py:656
  124.8 1.2 collective-permute-start.18
